TPU v7x, 32 devices: a whole 2x2x4 slice. The times are simulated.
32 devices in a mesh: dp: 8 (over z, core), mp: 4 (over y, x).
Axes of the slice: x: 2, y: 2, z: 4, core: 2. Of those that a mesh axis runs over, the one named last changes fastest.
Arguments:
- token_ids: int32 [8192], P('dp'), may hold values from 0 to 128255
- lengths: int32 [64], P('dp'), may hold values from 1 to 128
- embed_grads: bfloat16 [8192, 4096], P('dp', 'mp'), may hold values from -6 to 6
- vocab_basis: bfloat16 [128256, 32], P('mp'), may hold values from -6 to 6
- embed_basis: bfloat16 [4096, 32], P('mp'), may hold values from -0.09375 to 0.09375
- layer_inputs: bfloat16 [1, 8192, 4096], P(None, 'dp', 'mp'), may hold values from -6 to 6
- layer_grads: bfloat16 [1, 8192, 4096], P(None, 'dp', 'mp'), may hold values from -6 to 6
- input_basis: bfloat16 [1, 4096, 32], P(None, 'mp'), may hold values from -0.09375 to 0.09375
- output_basis: bfloat16 [1, 4096, 32], P(None, 'mp'), may hold values from -0.09375 to 0.09375
- queries: bfloat16 [2, 1024, 256], P(None, 'mp', 'dp'), may hold values from -0.19921875 to 0.19921875
Outputs:
- scores: float32 [64, 256], P('dp')
All inputs are finite; a program needn't handle non-finite values.
Results may differ from a plain program's by a relative error of at most 0.0003.
Values may be sent and summed in bfloat16 or wider, within the bound.
No kernel may reach another device: no remote copies, remote signals or barrier semaphores. Data moves between devices by JAX's collectives and lax.ppermute only.
A program may use at most 64 MiB of HBM per device.

v0:
```python
import functools

import jax
import jax.numpy as jnp
from jax import lax
from jax.experimental import pallas as pl
from jax.experimental.pallas import tpu as pltpu
from jax.sharding import PartitionSpec as P


ITERS = 2
LANES = 128

damping = 0.01
epsilon = 1e-06
highest = lax.Precision.HIGHEST


def solve_columns(right_side, apply_operator, column_norm, column_curve):
    solution = jnp.zeros_like(right_side)
    residual = right_side
    direction = right_side
    norm_now = column_norm(residual)
    for _ in range(ITERS):
        images = apply_operator(direction)
        step_size = norm_now / (column_curve(direction, images) + epsilon)
        solution = solution + step_size[:, None, :] * direction
        residual = residual - step_size[:, None, :] * images
        norm_next = column_norm(residual)
        direction = residual + (norm_next / (norm_now + epsilon))[:, None, :] * direction
        norm_now = norm_next
    return solution


def general_device(
    token_ids,
    lengths,
    embed_grads,
    vocab_basis,
    embed_basis,
    layer_inputs,
    layer_grads,
    input_basis,
    output_basis,
    queries,
):
    vocab_rows = vocab_basis.shape[0]
    basis_rank = embed_basis.shape[1]
    layer_count = layer_inputs.shape[0] + 1
    seq_count = lengths.shape[0]
    token_count = token_ids.shape[0]
    slot_len = token_count // seq_count
    sketch_len = basis_rank * basis_rank
    mp_index = lax.axis_index("mp")
    local_ids = token_ids - mp_index * vocab_rows
    inside = (local_ids >= 0) & (local_ids < vocab_rows)
    looked = jnp.take(vocab_basis, jnp.clip(local_ids, 0, vocab_rows - 1), axis=0)
    pieces = [
        jnp.dot(embed_grads, embed_basis, preferred_element_type=jnp.float32),
        jnp.where(inside[:, None], looked.astype(jnp.float32), 0.0),
    ]
    for layer in range(layer_count - 1):
        pieces.append(jnp.dot(layer_grads[layer], output_basis[layer], preferred_element_type=jnp.float32))
        pieces.append(jnp.dot(layer_inputs[layer], input_basis[layer], preferred_element_type=jnp.float32))
    projected = jnp.concatenate(pieces, axis=1)
    inverse_len = 1.0 / lengths.astype(jnp.float32)
    summed = lax.psum(projected, "mp")
    layout = summed.reshape(seq_count, slot_len, layer_count, 2, basis_rank)
    position = jnp.arange(slot_len, dtype=jnp.int32)
    weights = jnp.where(position[None, :] < lengths[:, None], inverse_len[:, None], 0.0)
    weighted = layout[:, :, :, 0, :] * weights[:, :, None, None]
    sketches = jnp.einsum(
        "stli,stlj->lsij", weighted, layout[:, :, :, 1, :], precision=highest
    ).reshape(layer_count, seq_count, sketch_len)
    examples = seq_count * lax.axis_size("dp")
    targets = lax.all_gather(queries, "dp", axis=2, tiled=True)
    everyone = lax.all_gather(sketches, "dp", axis=1, tiled=True)
    columns = lax.all_to_all(targets, "mp", split_axis=2, concat_axis=1, tiled=True)

    def apply_sketch(direction):
        inner_sums = jnp.einsum("lek,lkq->leq", everyone, direction, precision=highest)
        back_proj = jnp.einsum("lek,leq->lkq", everyone, inner_sums, precision=highest)
        return back_proj / examples + damping * direction

    def local_norm(residual):
        return jnp.sum(residual * residual, axis=1)

    def local_curve(direction, images):
        return jnp.sum(direction * images, axis=1)

    solution = solve_columns(columns.astype(jnp.float32), apply_sketch, local_norm, local_curve)
    partial_value = jnp.einsum("lek,lkq->eq", sketches, solution, precision=highest)
    return lax.all_gather(partial_value, "mp", axis=1, tiled=True)


def contract_last(left, right):
    return lax.dot_general(left, right, (((1,), (1,)), ((), ())), preferred_element_type=jnp.float32)


def project_kernel(
    vocab_rows,
    rank,
    slot_len,
    per_member,
    ids_any,
    table_any,
    grad0_any,
    grad1_any,
    input1_any,
    basis0_any,
    basis1_any,
    basis2_any,
    *refs,
):
    out_refs = refs[:-8]
    ids_ref, table_ref, wide_ref, weight_ref, place_ref, scalar_ref, small_sem, wide_sem = refs[-8:]
    members = len(out_refs)
    me = lax.axis_index("mp").astype(jnp.int32)
    offset = me * vocab_rows
    main = vocab_rows // LANES
    block = per_member * slot_len

    def rows_of(r):
        return pl.ds(pl.multiple_of((me ^ r) * block, block), block)

    def wide_copy(k, r):
        source = (grad0_any, grad1_any, input1_any)[k]
        return pltpu.make_async_copy(source.at[rows_of(r), :], wide_ref.at[k, rows_of(r), :], wide_sem.at[k, r])

    ids_copy = pltpu.make_async_copy(ids_any, ids_ref, small_sem.at[0])
    table_copy = pltpu.make_async_copy(table_any, table_ref, small_sem.at[1])
    basis_copies = [
        pltpu.make_async_copy(basis, weight_ref.at[k, pl.ds(k * rank, rank), :], small_sem.at[2 + k])
        for k, basis in enumerate((basis0_any, basis1_any, basis2_any))
    ]
    ids_copy.start()
    table_copy.start()
    for copy in basis_copies:
        copy.start()
    for r in range(members):
        for k in range(3):
            wide_copy(k, r).start()
    for k in range(3):
        if k:
            weight_ref[k, : k * rank, :] = jnp.zeros((k * rank, weight_ref.shape[2]), jnp.bfloat16)
        weight_ref[k, (k + 1) * rank :, :] = jnp.zeros((LANES - (k + 1) * rank, weight_ref.shape[2]), jnp.bfloat16)
    ids_copy.wait()
    local = ids_ref[...] - offset
    position = lax.broadcasted_iota(jnp.int32, local.shape, 1)
    place_ref[0] = jnp.clip(local >> 7, 0, main - 1) * LANES
    place_ref[1] = (position - local) & (LANES - 1)
    scalar_copy = pltpu.make_async_copy(place_ref, scalar_ref, small_sem.at[0])
    scalar_copy.start()
    scalar_copy.wait()
    table_copy.wait()
    for copy in basis_copies:
        copy.wait()

    lane = lax.broadcasted_iota(jnp.int32, (rank, LANES), 1)
    tail = vocab_rows - main * LANES

    def step(r, _):
        member = me ^ r
        values = []
        for k in range(3):
            wide_copy(k, r).wait()
        for s in range(per_member):
            seq = member * per_member + s
            found = jnp.zeros((rank, LANES), jnp.float32)
            for t in range(slot_len):
                start = pl.multiple_of(scalar_ref[0, seq, t], LANES)
                block = table_ref[:, pl.ds(start, LANES)].astype(jnp.float32)
                found = jnp.where(lane == t, pltpu.roll(block, scalar_ref[1, seq, t], 1), found)
            mine = ids_ref[pl.ds(seq, 1), :] - offset
            found = jnp.where((mine >= 0) & (mine < main * LANES), found, 0.0)
            if tail:
                sub = lax.broadcasted_iota(jnp.int32, (tail, LANES), 0)
                pick = jnp.where(mine - main * LANES == sub, 1.0, 0.0).astype(jnp.bfloat16)
                found += jnp.dot(table_ref[:, main * LANES :], pick, preferred_element_type=jnp.float32)
            rows = pl.ds(pl.multiple_of(seq * slot_len, slot_len), slot_len)
            total = contract_last(wide_ref[0, rows, :], weight_ref[0])
            total += contract_last(wide_ref[1, rows, :], weight_ref[1])
            total += contract_last(wide_ref[2, rows, :], weight_ref[2])
            spread = jnp.concatenate([jnp.zeros((3 * rank, LANES), jnp.float32), found], axis=0)
            values.append(total + spread.T)
        for place, out_ref in enumerate(out_refs):

            @pl.when(r == place)
            def _():
                for s in range(per_member):
                    out_ref[s * slot_len : (s + 1) * slot_len, :] = values[s]

        return 0

    lax.fori_loop(0, members, step, 0)


def sketch_kernel(rank, slot_len, per_member, len_ref, *refs):
    parts, out_ref, full_ref = refs[:-2], refs[-2], refs[-1]
    me = lax.axis_index("mp").astype(jnp.int32)
    lane = lax.broadcasted_iota(jnp.int32, (8, LANES), 1)
    for s in range(per_member):
        rows = slice(s * slot_len, (s + 1) * slot_len)
        total = parts[0][rows, :]
        for part in parts[1:]:
            total = total + part[rows, :]
        live = len_ref[me * per_member + s]
        position = lax.broadcasted_iota(jnp.int32, (slot_len, LANES), 0)
        share = 1.0 / jnp.full((slot_len, LANES), live, jnp.int32).astype(jnp.float32)
        weighted = total * jnp.where(position < live, share, 0.0)
        full_ref[s] = lax.dot_general(
            weighted, total, (((0,), (0,)), ((), ())), precision=highest, preferred_element_type=jnp.float32
        )
        for layer in range(2):
            source = 3 - layer
            unit = jnp.zeros((8, LANES), jnp.float32)
            for c in range(4):
                piece = full_ref[s, pl.ds(layer * rank + c, 8, stride=4), :]
                turned = pltpu.roll(piece, ((c - source) * rank) % LANES, 1)
                unit = jnp.where((lane >= c * rank) & (lane < (c + 1) * rank), turned, unit)
            out_ref[pl.ds((s * 2 + layer) * 8, 8), :] = unit


def swap_blocks(value, axis, width, index, count):
    size = value.shape[axis]
    place = lax.broadcasted_iota(jnp.int32, value.shape, axis)
    bit = 1
    while bit < count:
        shift = bit * width
        up = pltpu.roll(value, shift, axis)
        down = pltpu.roll(value, size - shift, axis)
        other = jnp.where((place // shift) % 2 == 1, up, down)
        value = jnp.where((index // bit) % 2 == 1, other, value)
        bit *= 2
    return value


def solve_kernel(mp, zs, per_member, examples, mine_ref, other_ref, qmine_ref, qother_ref, out_ref):
    me = lax.axis_index("mp").astype(jnp.int32)
    mydp = lax.axis_index("dp").astype(jnp.int32)
    half = mp * zs * per_member
    columns = qmine_ref.shape[1] * qmine_ref.shape[3]
    chunk = qmine_ref.shape[4]
    scores = None
    for layer in range(2):
        square = jnp.zeros((4 * half, 4 * half), jnp.float32)
        mixed = [jnp.zeros((4 * half, columns), jnp.float32) for _ in range(2)]
        norms = [jnp.zeros((columns, LANES), jnp.float32) for _ in range(2)]
        for k in range(mp):
            first = (me ^ k) * (chunk // LANES)
            wide = []
            for j in range(chunk // LANES):
                start = layer * 8 + first + j
                wide.append(
                    jnp.concatenate(
                        [ref[pl.ds(start, half, stride=16), :] for ref in (mine_ref, other_ref)], axis=0
                    )
                )
            value = jnp.concatenate(wide, axis=1)
            high = value.astype(jnp.bfloat16)
            low = (value - high.astype(jnp.float32)).astype(jnp.bfloat16)
            both = jnp.concatenate([high, low], axis=0)
            square += contract_last(both, both)
            for side, ref in enumerate((qmine_ref, qother_ref)):
                query = ref[k, :, layer].reshape(columns, chunk)
                mixed[side] += contract_last(both, query)
                wide_query = query.astype(jnp.float32)
                squared = wide_query * wide_query
                for j in range(chunk // LANES):
                    norms[side] += squared[:, j * LANES : (j + 1) * LANES]
        n = 2 * half
        gram = square[:n, :n] + square[:n, n:] + square[n:, :n] + square[n:, n:]
        u = jnp.concatenate([m[:n] + m[n:] for m in mixed], axis=1)
        ku = jnp.dot(gram, u, precision=highest, preferred_element_type=jnp.float32)
        qq = lax.dot_general(
            jnp.ones((8, LANES), jnp.float32),
            jnp.concatenate(norms, axis=0),
            (((1,), (1,)), ((), ())),
            precision=highest,
            preferred_element_type=jnp.float32,
        )[:1]
        uu = jnp.sum(u * u, axis=0, keepdims=True)
        uku = jnp.sum(u * ku, axis=0, keepdims=True)
        step0 = qq / (uu / examples + damping * qq + epsilon)
        alpha = 1.0 - damping * step0
        beta = -step0 / examples
        rr = jnp.maximum(alpha * alpha * qq + 2.0 * alpha * beta * uu + beta * beta * uku, 0.0)
        a = alpha + rr / (qq + epsilon)
        sd = a * u + beta * ku
        dd = jnp.maximum(a * a * qq + 2.0 * a * beta * uu + beta * beta * uku, 0.0)
        step1 = rr / (jnp.sum(sd * sd, axis=0, keepdims=True) / examples + damping * dd + epsilon)
        value = step0 * u + step1 * sd
        scores = value if scores is None else scores + value
    own = jnp.concatenate(
        [scores[k * zs * per_member : k * zs * per_member + per_member] for k in range(mp)], axis=0
    )
    own = swap_blocks(own, 0, per_member, me, mp)
    width = columns // zs
    own = jnp.concatenate(
        [own[:, (c * zs + z) * width : (c * zs + z + 1) * width] for z in range(zs) for c in range(2)], axis=1
    )
    out_ref[...] = swap_blocks(own, 1, width, mydp, 2 * zs)


def exchange(value, axis, count, unit=1):
    size = lax.axis_size(axis)
    return [value] + [
        lax.ppermute(value, axis, [(i, i ^ (k * unit)) for i in range(size)]) for k in range(1, count)
    ]


def fast_device(
    token_ids,
    lengths,
    embed_grads,
    vocab_basis,
    embed_basis,
    layer_inputs,
    layer_grads,
    input_basis,
    output_basis,
    queries,
):
    vocab_rows, rank = vocab_basis.shape
    seq_count = lengths.shape[0]
    token_count, features = embed_grads.shape
    slot_len = token_count // seq_count
    mp, dp = lax.axis_size("mp"), lax.axis_size("dp")
    zs = dp // 2
    per_member = seq_count // mp
    examples = seq_count * dp
    placed = lambda space, *values: [pltpu.with_memory_space_constraint(v, space) for v in values]
    whole = lambda n: [pl.BlockSpec(memory_space=pltpu.VMEM)] * n
    limit = pltpu.CompilerParams(vmem_limit_bytes=16 * 2**20)

    block = per_member * slot_len
    sent = pl.pallas_call(
        functools.partial(project_kernel, vocab_rows, rank, slot_len, per_member),
        out_shape=[pltpu.VMEM((block, LANES), jnp.float32)] * mp,
        in_specs=[pl.BlockSpec(memory_space=pl.ANY)] * 8,
        out_specs=whole(mp),
        scratch_shapes=[
            pltpu.VMEM((seq_count, slot_len), jnp.int32),
            pltpu.VMEM((rank, vocab_rows), jnp.bfloat16),
            pltpu.VMEM((3, token_count, features), jnp.bfloat16),
            pltpu.VMEM((3, LANES, features), jnp.bfloat16),
            pltpu.VMEM((2, seq_count, slot_len), jnp.int32),
            pltpu.SMEM((2, seq_count, slot_len), jnp.int32),
            pltpu.SemaphoreType.DMA((5,)),
            pltpu.SemaphoreType.DMA((3, mp)),
        ],
        compiler_params=limit,
        name="project",
    )(
        *placed(
            pltpu.HBM,
            token_ids.reshape(seq_count, slot_len),
            vocab_basis.T,
            embed_grads,
            layer_grads[0],
            layer_inputs[0],
            embed_basis.T,
            output_basis[0].T,
            input_basis[0].T,
        )
    )
    parts = [sent[0]]
    for k in range(1, mp):
        parts.append(lax.ppermute(sent[k], "mp", [(i, i ^ k) for i in range(mp)]))

    qt = queries.transpose(0, 2, 1)
    qz = jnp.stack(exchange(qt, "dp", zs, 2))
    qall = jnp.stack(exchange(qz, "mp", mp))
    qcore = exchange(qall, "dp", 2)[1]
    rows = per_member * 2 * 8
    units = pl.pallas_call(
        functools.partial(sketch_kernel, rank, slot_len, per_member),
        out_shape=pltpu.VMEM((rows, LANES), jnp.float32),
        in_specs=[pl.BlockSpec(memory_space=pltpu.SMEM)] + whole(mp),
        out_specs=whole(1)[0],
        scratch_shapes=[pltpu.VMEM((per_member, LANES, LANES), jnp.float32)],
        compiler_params=limit,
        name="sketch",
    )(lengths, *placed(pltpu.VMEM, *parts))
    along_z = jnp.concatenate(exchange(units, "dp", zs, 2))
    mine = jnp.concatenate(exchange(along_z, "mp", mp))
    other = exchange(mine, "dp", 2)[1]
    return pl.pallas_call(
        functools.partial(solve_kernel, mp, zs, per_member, examples),
        out_shape=jax.ShapeDtypeStruct((seq_count, queries.shape[2] * dp), jnp.float32),
        in_specs=whole(4),
        out_specs=whole(1)[0],
        compiler_params=limit,
        name="solve",
    )(*placed(pltpu.VMEM, mine, other, qall, qcore))


def power_of_two(n):
    return n & (n - 1) == 0


def solution(mesh):
    placed = (
        P("dp"),
        P("dp"),
        P("dp", "mp"),
        P("mp", None),
        P("mp", None),
        P(None, "dp", "mp"),
        P(None, "dp", "mp"),
        P(None, "mp", None),
        P(None, "mp", None),
        P(None, "mp", "dp"),
    )

    def per_device(*args):
        mp, dp = mesh.shape["mp"], mesh.shape["dp"]
        token_ids, lengths, layer_inputs, queries = args[0], args[1], args[5], args[9]
        seq_count, rank = lengths.shape[0], args[3].shape[1]
        fits = (
            layer_inputs.shape[0] == 1
            and token_ids.shape[0] == seq_count * LANES
            and rank * 4 == LANES
            and seq_count % 8 == 0
            and seq_count % mp == 0
            and power_of_two(mp)
            and power_of_two(dp)
            and dp % 2 == 0
            and queries.shape[1] % LANES == 0
            and queries.shape[2] % 16 == 0
            and queries.shape[2] * dp // 2 == LANES
        )
        if not fits:
            return general_device(*args)
        return fast_device(*args)

    return jax.shard_map(per_device, mesh=mesh, in_specs=placed, out_specs=P("dp", None), check_vma=False)
```

profile of v0, /device:TPU:0, one launch (start us, length us, event | category | flops | bytes accessed | tf_op | source)
XLA Modules:
  0.0 43.4 jit_solution(12215943396553826475)
XLA Ops:
  0.0 4.1 %collective-permute-start.11 = (bf16[2,32,256]{2,1,0:T(8,128)(2,1)}, bf16[2,32,256]{2,1,0:T(8,128)(2,1)S(1)}, u32[]{:S(2)}, u32[]{:S(2)}) collective-permute-start(bf16[2,32,256]{2,1,0:T(8,128)(2,1)} %bitcast.31), channel_id=1, source_target_pairs={{0,16},{4,20},{8,24},{12,28},{16,0},{20,4},{24,8},{28,12},{1,17},{... | collective-permute-start | bytes 98312 | tf_op jit(solution)/shard_map/ppermute | solution.py:308
  4.1 1.6 %collective-permute-start.10 = (bf16[2,32,256]{2,1,0:T(8,128)(2,1)}, bf16[2,32,256]{2,1,0:T(8,128)(2,1)S(1)}, u32[]{:S(2)}, u32[]{:S(2)}) collective-permute-start(bf16[2,32,256]{2,1,0:T(8,128)(2,1)} %bitcast.32), channel_id=1, source_target_pairs={{0,8},{4,12},{8,0},{12,4},{16,24},{20,28},{24,16},{28,20},{1,9},{5... | collective-permute-start | bytes 98312 | tf_op jit(solution)/shard_map/ppermute | solution.py:308
  5.6 0.0 collective-permute-start.12
  5.6 0.0 copy-start.1
  5.6 0.0 copy-start
  5.7 7.3 %project.1 = (f32[256,128]{1,0:T(8,128)S(1)}, f32[256,128]{1,0:T(8,128)S(1)}, f32[256,128]{1,0:T(8,128)S(1)}, f32[256,128]{1,0:T(8,128)S(1)}) custom-call(s32[8,128]{1,0:T(8,128)} %bitcast.38, bf16[32,32064]{1,0:T(8,128)(2,1)} %bitcast.24, bf16[1024,1024]{1,0:T(8,128)(2,1)} %grad0_any.1, bf16[1024,1024]{1,0:T(8,128)(2,1)} %bitcast.22, ...), custom_call_target="tpu_custom_call" | custom-call | tf_op jit(solution)/shard_map/project/pallas_call | solution.py:337
  12.9 1.8 %collective-permute-start = (f32[256,128]{1,0:T(8,128)S(1)}, f32[256,128]{1,0:T(8,128)S(1)}, u32[]{:S(2)}, u32[]{:S(2)}) collective-permute-start(f32[256,128]{1,0:T(8,128)S(1)} %get-tuple-element.10), channel_id=1, source_target_pairs={{0,1},{1,0},{2,3},{3,2},{4,5},{5,4},{6,7},{7,6},{8,9},{9,8},{10,11... | collective-permute-start | bytes 393224 | tf_op jit(solution)/shard_map/ppermute | solution.py:369
  14.7 1.5 %collective-permute-start.1 = (f32[256,128]{1,0:T(8,128)S(1)}, f32[256,128]{1,0:T(8,128)S(1)}, u32[]{:S(2)}, u32[]{:S(2)}) collective-permute-start(f32[256,128]{1,0:T(8,128)S(1)} %get-tuple-element.11), channel_id=1, source_target_pairs={{0,2},{1,3},{2,0},{3,1},{4,6},{5,7},{6,4},{7,5},{8,10},{9,11},{10,... | collective-permute-start | bytes 393224 | tf_op jit(solution)/shard_map/ppermute | solution.py:369
  16.3 0.0 collective-permute-done.11
  16.3 0.2 collective-permute-start.2
  16.5 0.0 collective-permute-done.10
  16.5 0.0 collective-permute-done.12
  16.5 0.0 copy-done.1
  16.5 1.8 %collective-permute-start.14 = (bf16[4,2,32,256]{3,2,1,0:T(8,128)(2,1)S(1)}, bf16[4,2,32,256]{3,2,1,0:T(8,128)(2,1)S(1)}, u32[]{:S(2)}, u32[]{:S(2)}) collective-permute-start(bf16[4,2,32,256]{3,2,1,0:T(8,128)(2,1)S(1)} %get-tuple-element.14), channel_id=1, source_target_pairs={{0,2},{1,3},{2,0},{3,1},{4,6},{5,7},{6,4},{7,5},{8,10},{9,11},{10,... | collective-permute-start | bytes 393224 | tf_op jit(solution)/shard_map/ppermute | solution.py:308
  18.4 1.5 %collective-permute-start.13 = (bf16[4,2,32,256]{3,2,1,0:T(8,128)(2,1)S(1)}, bf16[4,2,32,256]{3,2,1,0:T(8,128)(2,1)S(1)}, u32[]{:S(2)}, u32[]{:S(2)}) collective-permute-start(bf16[4,2,32,256]{3,2,1,0:T(8,128)(2,1)S(1)} %get-tuple-element.14), channel_id=1, source_target_pairs={{0,1},{1,0},{2,3},{3,2},{4,5},{5,4},{6,7},{7,6},{8,9},{9,8},{10,11... | collective-permute-start | bytes 393224 | tf_op jit(solution)/shard_map/ppermute | solution.py:308
  19.9 0.0 collective-permute-done.refs_1_
  19.9 3.1 %collective-permute-done.1.refs_2_ = f32[256,128]{1,0:T(8,128)S(1)} collective-permute-done((f32[256,128]{1,0:T(8,128)S(1)}, f32[256,128]{1,0:T(8,128)S(1)}, u32[]{:S(2)}, u32[]{:S(2)}) %collective-permute-start.1) | collective-permute-done | bytes 131104 | tf_op jit(solution)/shard_map/ppermute | solution.py:369
  22.9 0.4 collective-permute-done.2.refs_3_
  23.4 0.0 copy-done
  23.4 0.9 %sketch.1 = f32[32,128]{1,0:T(8,128)S(1)} custom-call(s32[8]{0:T(128)S(1)} %copy-done, f32[256,128]{1,0:T(8,128)S(1)} %get-tuple-element.9.refs_0_, f32[256,128]{1,0:T(8,128)S(1)} %collective-permute-done.refs_1_, f32[256,128]{1,0:T(8,128)S(1)} %collective-permute-done.1.refs_2_, f32[256,128]{1,0:T(8,128)S(1)} %collective-permute-done.2.refs_3_), custom_call_target="tpu_custom_call" | custom-call | tf_op jit(solution)/shard_map/sketch/pallas_call | solution.py:376
  24.3 3.7 %collective-permute-start.5 = (f32[32,128]{1,0:T(8,128)S(1)}, f32[32,128]{1,0:T(8,128)S(1)}, u32[]{:S(2)}, u32[]{:S(2)}) collective-permute-start(f32[32,128]{1,0:T(8,128)S(1)} %sketch.1), channel_id=1, source_target_pairs={{0,24},{4,28},{8,16},{12,20},{16,8},{20,12},{24,0},{28,4},{1,25},{... | collective-permute-start | bytes 49160 | tf_op jit(solution)/shard_map/ppermute | solution.py:308
  28.0 0.0 collective-permute-start.4
  28.0 0.8 %collective-permute-start.3 = (f32[32,128]{1,0:T(8,128)S(1)}, f32[32,128]{1,0:T(8,128)S(1)}, u32[]{:S(2)}, u32[]{:S(2)}) collective-permute-start(f32[32,128]{1,0:T(8,128)S(1)} %sketch.1), channel_id=1, source_target_pairs={{0,8},{4,12},{8,0},{12,4},{16,24},{20,28},{24,16},{28,20},{1,9},{5... | collective-permute-start | bytes 49160 | tf_op jit(solution)/shard_map/ppermute | solution.py:308
  28.8 1.1 %collective-permute-done.5 = f32[32,128]{1,0:T(8,128)S(1)} collective-permute-done((f32[32,128]{1,0:T(8,128)S(1)}, f32[32,128]{1,0:T(8,128)S(1)}, u32[]{:S(2)}, u32[]{:S(2)}) %collective-permute-start.5) | collective-permute-done | bytes 16416 | tf_op jit(solution)/shard_map/ppermute | solution.py:308
  29.9 1.1 %collective-permute-start.15 = (bf16[4,2,32,256]{3,2,1,0:T(8,128)(2,1)S(1)}, bf16[4,2,32,256]{3,2,1,0:T(8,128)(2,1)S(1)}, u32[]{:S(2)}, u32[]{:S(2)}) collective-permute-start(bf16[4,2,32,256]{3,2,1,0:T(8,128)(2,1)S(1)} %get-tuple-element.14), channel_id=1, source_target_pairs={{0,3},{1,2},{2,1},{3,0},{4,7},{5,6},{6,5},{7,4},{8,11},{9,10},{10,... | collective-permute-start | bytes 393224 | tf_op jit(solution)/shard_map/ppermute | solution.py:308
  31.0 1.6 %collective-permute-done.4 = f32[32,128]{1,0:T(8,128)S(1)} collective-permute-done((f32[32,128]{1,0:T(8,128)S(1)}, f32[32,128]{1,0:T(8,128)S(1)}, u32[]{:S(2)}, u32[]{:S(2)}) %collective-permute-start.4) | collective-permute-done | bytes 16416 | tf_op jit(solution)/shard_map/ppermute | solution.py:308
  32.6 0.0 collective-permute-done.3
  32.6 1.1 %collective-permute-start.8 = (f32[128,128]{1,0:T(8,128)S(1)}, f32[128,128]{1,0:T(8,128)S(1)}, u32[]{:S(2)}, u32[]{:S(2)}) collective-permute-start(f32[128,128]{1,0:T(8,128)S(1)} %pad_maximum_fusion.2), channel_id=1, source_target_pairs={{0,3},{1,2},{2,1},{3,0},{4,7},{5,6},{6,5},{7,4},{8,11},{9,10},{10,... | collective-permute-start | bytes 196616 | tf_op jit(solution)/shard_map/ppermute | solution.py:308
  33.8 1.5 %collective-permute-start.7 = (f32[128,128]{1,0:T(8,128)S(1)}, f32[128,128]{1,0:T(8,128)S(1)}, u32[]{:S(2)}, u32[]{:S(2)}) collective-permute-start(f32[128,128]{1,0:T(8,128)S(1)} %pad_maximum_fusion.2), channel_id=1, source_target_pairs={{0,2},{1,3},{2,0},{3,1},{4,6},{5,7},{6,4},{7,5},{8,10},{9,11},{10,... | collective-permute-start | bytes 196616 | tf_op jit(solution)/shard_map/ppermute | solution.py:308
  35.2 0.0 collective-permute-done.14
  35.2 1.0 %collective-permute-start.6 = (f32[128,128]{1,0:T(8,128)S(1)}, f32[128,128]{1,0:T(8,128)S(1)}, u32[]{:S(2)}, u32[]{:S(2)}) collective-permute-start(f32[128,128]{1,0:T(8,128)S(1)} %pad_maximum_fusion.2), channel_id=1, source_target_pairs={{0,1},{1,0},{2,3},{3,2},{4,5},{5,4},{6,7},{7,6},{8,9},{9,8},{10,11... | collective-permute-start | bytes 196616 | tf_op jit(solution)/shard_map/ppermute | solution.py:308
  36.3 0.0 collective-permute-done.13
  36.3 0.0 collective-permute-done.15
  36.3 0.1 pad_maximum_fusion.qmine_ref
  36.4 0.1 collective-permute-start.16
  36.4 3.1 %collective-permute-done.6 = f32[128,128]{1,0:T(8,128)S(1)} collective-permute-done((f32[128,128]{1,0:T(8,128)S(1)}, f32[128,128]{1,0:T(8,128)S(1)}, u32[]{:S(2)}, u32[]{:S(2)}) %collective-permute-start.6) | collective-permute-done | bytes 65568 | tf_op jit(solution)/shard_map/ppermute | solution.py:308
  39.6 0.0 collective-permute-done.7
  39.6 0.0 collective-permute-done.8
  39.6 0.1 collective-permute-start.9
  39.7 1.5 %collective-permute-done.9.other_ref = f32[512,128]{1,0:T(8,128)S(1)} collective-permute-done((f32[512,128]{1,0:T(8,128)S(1)}, f32[512,128]{1,0:T(8,128)S(1)}, u32[]{:S(2)}, u32[]{:S(2)}) %collective-permute-start.9) | collective-permute-done | bytes 262176 | tf_op jit(solution)/shard_map/ppermute | solution.py:308
  41.2 0.0 collective-permute-done.16.qother_ref
  41.2 2.1 %solve.1 = f32[8,256]{1,0:T(8,128)} custom-call(f32[512,128]{1,0:T(8,128)S(1)} %constant_dynamic-update-slice_fusion.mine_ref, f32[512,128]{1,0:T(8,128)S(1)} %collective-permute-done.9.other_ref, bf16[4,4,2,32,256]{4,3,2,1,0:T(8,128)(2,1)S(1)} %pad_maximum_fusion.qmine_ref, bf16[4,4,2,32,256]{4,3,2,1,0:T(8,128)(2,1)S(1)} %collective-permute-done.16.qother_ref), custom_call_target="tpu_custom_call" | custom-call | tf_op jit(solution)/shard_map/solve/pallas_call | solution.py:388
  (9 shorter events, 0.1 us)
Async XLA Ops:
  0.0 16.3 %collective-permute-start.11 = (bf16[2,32,256]{2,1,0:T(8,128)(2,1)}, bf16[2,32,256]{2,1,0:T(8,128)(2,1)S(1)}, u32[]{:S(2)}, u32[]{:S(2)}) collective-permute-start(bf16[2,32,256]{2,1,0:T(8,128)(2,1)} %bitcast.31), channel_id=1, source_target_pairs={{0,16},{4,20},{8,24},{12,28},{16,0},{20,4},{24,8},{28,12},{1,17},{... | collective-permute-start | bytes 98312 | tf_op jit(solution)/shard_map/ppermute | solution.py:308
  4.1 12.4 %collective-permute-start.10 = (bf16[2,32,256]{2,1,0:T(8,128)(2,1)}, bf16[2,32,256]{2,1,0:T(8,128)(2,1)S(1)}, u32[]{:S(2)}, u32[]{:S(2)}) collective-permute-start(bf16[2,32,256]{2,1,0:T(8,128)(2,1)} %bitcast.32), channel_id=1, source_target_pairs={{0,8},{4,12},{8,0},{12,4},{16,24},{20,28},{24,16},{28,20},{1,9},{5... | collective-permute-start | bytes 98312 | tf_op jit(solution)/shard_map/ppermute | solution.py:308
  5.6 10.8 %collective-permute-start.12 = (bf16[2,32,256]{2,1,0:T(8,128)(2,1)}, bf16[2,32,256]{2,1,0:T(8,128)(2,1)S(1)}, u32[]{:S(2)}, u32[]{:S(2)}) collective-permute-start(bf16[2,32,256]{2,1,0:T(8,128)(2,1)} %bitcast.33), channel_id=1, source_target_pairs={{0,24},{4,28},{8,16},{12,20},{16,8},{20,12},{24,0},{28,4},{1,25},{... | collective-permute-start | bytes 98312 | tf_op jit(solution)/shard_map/ppermute | solution.py:308
  5.6 10.8 %copy-start.1 = (bf16[2,256,32]{1,2,0:T(8,128)(2,1)S(1)}, bf16[2,256,32]{1,2,0:T(8,128)(2,1)}, u32[]{:S(2)}) copy-start(bf16[2,256,32]{1,2,0:T(8,128)(2,1)} %param.19) | copy-start | bytes 98308
  5.6 17.7 %copy-start = (s32[8]{0:T(128)S(1)}, s32[8]{0:T(128)}, u32[]{:S(2)}) copy-start(s32[8]{0:T(128)} %len_ref.1) | copy-start | bytes 100
  12.9 6.9 %collective-permute-start = (f32[256,128]{1,0:T(8,128)S(1)}, f32[256,128]{1,0:T(8,128)S(1)}, u32[]{:S(2)}, u32[]{:S(2)}) collective-permute-start(f32[256,128]{1,0:T(8,128)S(1)} %get-tuple-element.10), channel_id=1, source_target_pairs={{0,1},{1,0},{2,3},{3,2},{4,5},{5,4},{6,7},{7,6},{8,9},{9,8},{10,11... | collective-permute-start | bytes 393224 | tf_op jit(solution)/shard_map/ppermute | solution.py:369
  14.7 8.2 %collective-permute-start.1 = (f32[256,128]{1,0:T(8,128)S(1)}, f32[256,128]{1,0:T(8,128)S(1)}, u32[]{:S(2)}, u32[]{:S(2)}) collective-permute-start(f32[256,128]{1,0:T(8,128)S(1)} %get-tuple-element.11), channel_id=1, source_target_pairs={{0,2},{1,3},{2,0},{3,1},{4,6},{5,7},{6,4},{7,5},{8,10},{9,11},{10,... | collective-permute-start | bytes 393224 | tf_op jit(solution)/shard_map/ppermute | solution.py:369
  16.3 7.1 %collective-permute-start.2 = (f32[256,128]{1,0:T(8,128)S(1)}, f32[256,128]{1,0:T(8,128)S(1)}, u32[]{:S(2)}, u32[]{:S(2)}) collective-permute-start(f32[256,128]{1,0:T(8,128)S(1)} %get-tuple-element.12), channel_id=1, source_target_pairs={{0,3},{1,2},{2,1},{3,0},{4,7},{5,6},{6,5},{7,4},{8,11},{9,10},{10,... | collective-permute-start | bytes 393224 | tf_op jit(solution)/shard_map/ppermute | solution.py:369
  16.5 18.7 %collective-permute-start.14 = (bf16[4,2,32,256]{3,2,1,0:T(8,128)(2,1)S(1)}, bf16[4,2,32,256]{3,2,1,0:T(8,128)(2,1)S(1)}, u32[]{:S(2)}, u32[]{:S(2)}) collective-permute-start(bf16[4,2,32,256]{3,2,1,0:T(8,128)(2,1)S(1)} %get-tuple-element.14), channel_id=1, source_target_pairs={{0,2},{1,3},{2,0},{3,1},{4,6},{5,7},{6,4},{7,5},{8,10},{9,11},{10,... | collective-permute-start | bytes 393224 | tf_op jit(solution)/shard_map/ppermute | solution.py:308
  18.4 17.9 %collective-permute-start.13 = (bf16[4,2,32,256]{3,2,1,0:T(8,128)(2,1)S(1)}, bf16[4,2,32,256]{3,2,1,0:T(8,128)(2,1)S(1)}, u32[]{:S(2)}, u32[]{:S(2)}) collective-permute-start(bf16[4,2,32,256]{3,2,1,0:T(8,128)(2,1)S(1)} %get-tuple-element.14), channel_id=1, source_target_pairs={{0,1},{1,0},{2,3},{3,2},{4,5},{5,4},{6,7},{7,6},{8,9},{9,8},{10,11... | collective-permute-start | bytes 393224 | tf_op jit(solution)/shard_map/ppermute | solution.py:308
  24.3 5.6 %collective-permute-start.5 = (f32[32,128]{1,0:T(8,128)S(1)}, f32[32,128]{1,0:T(8,128)S(1)}, u32[]{:S(2)}, u32[]{:S(2)}) collective-permute-start(f32[32,128]{1,0:T(8,128)S(1)} %sketch.1), channel_id=1, source_target_pairs={{0,24},{4,28},{8,16},{12,20},{16,8},{20,12},{24,0},{28,4},{1,25},{... | collective-permute-start | bytes 49160 | tf_op jit(solution)/shard_map/ppermute | solution.py:308
  28.0 4.6 %collective-permute-start.4 = (f32[32,128]{1,0:T(8,128)S(1)}, f32[32,128]{1,0:T(8,128)S(1)}, u32[]{:S(2)}, u32[]{:S(2)}) collective-permute-start(f32[32,128]{1,0:T(8,128)S(1)} %sketch.1), channel_id=1, source_target_pairs={{0,16},{4,20},{8,24},{12,28},{16,0},{20,4},{24,8},{28,12},{1,17},{... | collective-permute-start | bytes 49160 | tf_op jit(solution)/shard_map/ppermute | solution.py:308
  28.0 4.6 %collective-permute-start.3 = (f32[32,128]{1,0:T(8,128)S(1)}, f32[32,128]{1,0:T(8,128)S(1)}, u32[]{:S(2)}, u32[]{:S(2)}) collective-permute-start(f32[32,128]{1,0:T(8,128)S(1)} %sketch.1), channel_id=1, source_target_pairs={{0,8},{4,12},{8,0},{12,4},{16,24},{20,28},{24,16},{28,20},{1,9},{5... | collective-permute-start | bytes 49160 | tf_op jit(solution)/shard_map/ppermute | solution.py:308
  29.9 6.3 %collective-permute-start.15 = (bf16[4,2,32,256]{3,2,1,0:T(8,128)(2,1)S(1)}, bf16[4,2,32,256]{3,2,1,0:T(8,128)(2,1)S(1)}, u32[]{:S(2)}, u32[]{:S(2)}) collective-permute-start(bf16[4,2,32,256]{3,2,1,0:T(8,128)(2,1)S(1)} %get-tuple-element.14), channel_id=1, source_target_pairs={{0,3},{1,2},{2,1},{3,0},{4,7},{5,6},{6,5},{7,4},{8,11},{9,10},{10,... | collective-permute-start | bytes 393224 | tf_op jit(solution)/shard_map/ppermute | solution.py:308
  32.6 7.0 %collective-permute-start.8 = (f32[128,128]{1,0:T(8,128)S(1)}, f32[128,128]{1,0:T(8,128)S(1)}, u32[]{:S(2)}, u32[]{:S(2)}) collective-permute-start(f32[128,128]{1,0:T(8,128)S(1)} %pad_maximum_fusion.2), channel_id=1, source_target_pairs={{0,3},{1,2},{2,1},{3,0},{4,7},{5,6},{6,5},{7,4},{8,11},{9,10},{10,... | collective-permute-start | bytes 196616 | tf_op jit(solution)/shard_map/ppermute | solution.py:308
  33.8 5.8 %collective-permute-start.7 = (f32[128,128]{1,0:T(8,128)S(1)}, f32[128,128]{1,0:T(8,128)S(1)}, u32[]{:S(2)}, u32[]{:S(2)}) collective-permute-start(f32[128,128]{1,0:T(8,128)S(1)} %pad_maximum_fusion.2), channel_id=1, source_target_pairs={{0,2},{1,3},{2,0},{3,1},{4,6},{5,7},{6,4},{7,5},{8,10},{9,11},{10,... | collective-permute-start | bytes 196616 | tf_op jit(solution)/shard_map/ppermute | solution.py:308
  35.2 4.3 %collective-permute-start.6 = (f32[128,128]{1,0:T(8,128)S(1)}, f32[128,128]{1,0:T(8,128)S(1)}, u32[]{:S(2)}, u32[]{:S(2)}) collective-permute-start(f32[128,128]{1,0:T(8,128)S(1)} %pad_maximum_fusion.2), channel_id=1, source_target_pairs={{0,1},{1,0},{2,3},{3,2},{4,5},{5,4},{6,7},{7,6},{8,9},{9,8},{10,11... | collective-permute-start | bytes 196616 | tf_op jit(solution)/shard_map/ppermute | solution.py:308
  36.4 4.9 %collective-permute-start.16 = (bf16[4,4,2,32,256]{4,3,2,1,0:T(8,128)(2,1)S(1)}, bf16[4,4,2,32,256]{4,3,2,1,0:T(8,128)(2,1)S(1)}, u32[]{:S(2)}, u32[]{:S(2)}) collective-permute-start(bf16[4,4,2,32,256]{4,3,2,1,0:T(8,128)(2,1)S(1)} %pad_maximum_fusion.qmine_ref), channel_id=1, source_target_pairs={{0,4},{4,0},{8,12},{12,8},{16,20},{20,16},{24,28},{28,24},{1,5},{5... | collective-permute-start | bytes 1572872 | tf_op jit(solution)/shard_map/ppermute | solution.py:308
  39.6 1.6 %collective-permute-start.9 = (f32[512,128]{1,0:T(8,128)S(1)}, f32[512,128]{1,0:T(8,128)S(1)}, u32[]{:S(2)}, u32[]{:S(2)}) collective-permute-start(f32[512,128]{1,0:T(8,128)S(1)} %constant_dynamic-update-slice_fusion.mine_ref), channel_id=1, source_target_pairs={{0,4},{4,0},{8,12},{12,8},{16,20},{20,16},{24,28},{28,24},{1,5},{5... | collective-permute-start | bytes 786440 | tf_op jit(solution)/shard_map/ppermute | solution.py:308
where the time goes:
time: 43.5 us; the launch traced here: 43.4 us
  starting transfers between devices  21.8 us (50%)
  waiting for transfers between devices  11 us (25%)
  Pallas kernels  10.3 us (24%)
    ppermute x14, starting transfers between devices, exchange(): lax.ppermute(value, axis, [(i, i ^ k * unit) for i in range(size)])  18.3 us
    ppermute x14, waiting for transfers between devices, exchange(): lax.ppermute(value, axis, [(i, i ^ k * unit) for i in range(size)])  7.47 us
    pallas_call x1, Pallas kernels, fast_device(): pl.pallas_call(functools.partial(project_kernel, vocab_rows, rank, slot_l...  7.26 us
    ppermute x3, starting transfers between devices, fast_device(): parts.append(lax.ppermute(sent[k], 'mp', [(i, i ^ k) for i in range(mp)]))  3.55 us
    ppermute x3, waiting for transfers between devices, fast_device(): parts.append(lax.ppermute(sent[k], 'mp', [(i, i ^ k) for i in range(mp)]))  3.51 us
    pallas_call x1, Pallas kernels, fast_device(): pl.pallas_call(functools.partial(solve_kernel, mp, zs, per_member, exampl...  2.13 us
    pallas_call x1, Pallas kernels, fast_device(): pl.pallas_call(functools.partial(sketch_kernel, rank, slot_len, per_membe...  0.95 us
  transfers between devices with their start and end apart: 17, of which 6 were waited for; matrix products, arithmetic and copies ran while one was open for 0% of the time, Pallas kernels for 19%

commit v1 on v0

--- a/solution.py
+++ b/solution.py
@@ -134,12 +134,11 @@
         for k, basis in enumerate((basis0_any, basis1_any, basis2_any))
     ]
     ids_copy.start()
-    table_copy.start()
     for copy in basis_copies:
         copy.start()
-    for r in range(members):
-        for k in range(3):
-            wide_copy(k, r).start()
+    table_copy.start()
+    for k in range(3):
+        wide_copy(k, 0).start()
     for k in range(3):
         if k:
             weight_ref[k, : k * rank, :] = jnp.zeros((k * rank, weight_ref.shape[2]), jnp.bfloat16)
@@ -152,9 +151,12 @@
     scalar_copy = pltpu.make_async_copy(place_ref, scalar_ref, small_sem.at[0])
     scalar_copy.start()
     scalar_copy.wait()
-    table_copy.wait()
     for copy in basis_copies:
         copy.wait()
+    table_copy.wait()
+    for r in range(1, members):
+        for k in range(3):
+            wide_copy(k, r).start()
 
     lane = lax.broadcasted_iota(jnp.int32, (rank, LANES), 1)
     tail = vocab_rows - main * LANES
@@ -235,31 +237,37 @@
     return value
 
 
-def solve_kernel(mp, zs, per_member, examples, mine_ref, other_ref, qmine_ref, qother_ref, out_ref):
+def split_halves(ref, layer, first, count, chunk):
+    wide = [ref[pl.ds(layer * 8 + first + j, count, stride=16), :] for j in range(chunk // LANES)]
+    value = jnp.concatenate(wide, axis=1)
+    high = value.astype(jnp.bfloat16)
+    low = (value - high.astype(jnp.float32)).astype(jnp.bfloat16)
+    return jnp.concatenate([high, low], axis=0)
+
+
+def fold_rows(value):
+    half = value.shape[0] // 2
+    return value[:half] + value[half:]
+
+
+def fold(value):
+    half = value.shape[1] // 2
+    value = fold_rows(value)
+    return value[:, :half] + value[:, half:]
+
+
+def own_kernel(mp, mine_ref, qmine_ref, qother_ref, both_ref, gram_ref, u_ref, norm_ref):
     me = lax.axis_index("mp").astype(jnp.int32)
-    mydp = lax.axis_index("dp").astype(jnp.int32)
-    half = mp * zs * per_member
+    half = gram_ref.shape[1]
     columns = qmine_ref.shape[1] * qmine_ref.shape[3]
     chunk = qmine_ref.shape[4]
-    scores = None
     for layer in range(2):
-        square = jnp.zeros((4 * half, 4 * half), jnp.float32)
-        mixed = [jnp.zeros((4 * half, columns), jnp.float32) for _ in range(2)]
+        square = jnp.zeros((2 * half, 2 * half), jnp.float32)
+        mixed = [jnp.zeros((2 * half, columns), jnp.float32) for _ in range(2)]
         norms = [jnp.zeros((columns, LANES), jnp.float32) for _ in range(2)]
         for k in range(mp):
-            first = (me ^ k) * (chunk // LANES)
-            wide = []
-            for j in range(chunk // LANES):
-                start = layer * 8 + first + j
-                wide.append(
-                    jnp.concatenate(
-                        [ref[pl.ds(start, half, stride=16), :] for ref in (mine_ref, other_ref)], axis=0
-                    )
-                )
-            value = jnp.concatenate(wide, axis=1)
-            high = value.astype(jnp.bfloat16)
-            low = (value - high.astype(jnp.float32)).astype(jnp.bfloat16)
-            both = jnp.concatenate([high, low], axis=0)
+            both = split_halves(mine_ref, layer, (me ^ k) * (chunk // LANES), half, chunk)
+            both_ref[layer, :, k * chunk : (k + 1) * chunk] = both
             square += contract_last(both, both)
             for side, ref in enumerate((qmine_ref, qother_ref)):
                 query = ref[k, :, layer].reshape(columns, chunk)
@@ -268,17 +276,47 @@
                 squared = wide_query * wide_query
                 for j in range(chunk // LANES):
                     norms[side] += squared[:, j * LANES : (j + 1) * LANES]
-        n = 2 * half
-        gram = square[:n, :n] + square[:n, n:] + square[n:, :n] + square[n:, n:]
-        u = jnp.concatenate([m[:n] + m[n:] for m in mixed], axis=1)
-        ku = jnp.dot(gram, u, precision=highest, preferred_element_type=jnp.float32)
-        qq = lax.dot_general(
+        gram_ref[layer] = fold(square)
+        for side in range(2):
+            u_ref[layer, :, side * columns : (side + 1) * columns] = fold_rows(mixed[side])
+        norm_ref[layer] = lax.dot_general(
             jnp.ones((8, LANES), jnp.float32),
             jnp.concatenate(norms, axis=0),
             (((1,), (1,)), ((), ())),
             precision=highest,
             preferred_element_type=jnp.float32,
-        )[:1]
+        )
+
+
+def solve_kernel(
+    mp, zs, per_member, examples, other_ref, both_ref, gram_ref, u_ref, norm_ref, qmine_ref, qother_ref, out_ref
+):
+    me = lax.axis_index("mp").astype(jnp.int32)
+    mydp = lax.axis_index("dp").astype(jnp.int32)
+    half = gram_ref.shape[1]
+    columns = qmine_ref.shape[1] * qmine_ref.shape[3]
+    chunk = qmine_ref.shape[4]
+    scores = None
+    for layer in range(2):
+        square = jnp.zeros((2 * half, 2 * half), jnp.float32)
+        cross = jnp.zeros((2 * half, 2 * half), jnp.float32)
+        mixed = [jnp.zeros((2 * half, columns), jnp.float32) for _ in range(2)]
+        for k in range(mp):
+            both = split_halves(other_ref, layer, (me ^ k) * (chunk // LANES), half, chunk)
+            square += contract_last(both, both)
+            cross += contract_last(both_ref[layer, :, k * chunk : (k + 1) * chunk], both)
+            for side, ref in enumerate((qmine_ref, qother_ref)):
+                mixed[side] += contract_last(both, ref[k, :, layer].reshape(columns, chunk))
+        cross = fold(cross)
+        own_u = u_ref[layer]
+        other_u = jnp.concatenate([fold_rows(m) for m in mixed], axis=1)
+        u = jnp.concatenate([own_u, other_u], axis=0)
+        dot = functools.partial(jnp.dot, precision=highest, preferred_element_type=jnp.float32)
+        ku = jnp.concatenate(
+            [dot(gram_ref[layer], own_u) + dot(cross, other_u), dot(cross.T, own_u) + dot(fold(square), other_u)],
+            axis=0,
+        )
+        qq = norm_ref[layer][:1]
         uu = jnp.sum(u * u, axis=0, keepdims=True)
         uku = jnp.sum(u * ku, axis=0, keepdims=True)
         step0 = qq / (uu / examples + damping * qq + epsilon)
@@ -368,10 +406,7 @@
     for k in range(1, mp):
         parts.append(lax.ppermute(sent[k], "mp", [(i, i ^ k) for i in range(mp)]))
 
-    qt = queries.transpose(0, 2, 1)
-    qz = jnp.stack(exchange(qt, "dp", zs, 2))
-    qall = jnp.stack(exchange(qz, "mp", mp))
-    qcore = exchange(qall, "dp", 2)[1]
+    pieces = exchange(queries.transpose(0, 2, 1), "dp", zs, 2)
     rows = per_member * 2 * 8
     units = pl.pallas_call(
         functools.partial(sketch_kernel, rank, slot_len, per_member),
@@ -383,16 +418,35 @@
         name="sketch",
     )(lengths, *placed(pltpu.VMEM, *parts))
     along_z = jnp.concatenate(exchange(units, "dp", zs, 2))
+    pieces = lax.optimization_barrier((*pieces, units))[:-1]
+    qall = jnp.stack(exchange(jnp.stack(pieces), "mp", mp))
+    qcore = exchange(qall, "dp", 2)[1]
     mine = jnp.concatenate(exchange(along_z, "mp", mp))
     other = exchange(mine, "dp", 2)[1]
+    half = mp * zs * per_member
+    columns = queries.shape[2] * dp
+    sketch_len = rank * rank
+    own_terms = pl.pallas_call(
+        functools.partial(own_kernel, mp),
+        out_shape=[
+            pltpu.VMEM((2, 2 * half, sketch_len), jnp.bfloat16),
+            pltpu.VMEM((2, half, half), jnp.float32),
+            pltpu.VMEM((2, half, columns), jnp.float32),
+            pltpu.VMEM((2, 8, columns), jnp.float32),
+        ],
+        in_specs=whole(3),
+        out_specs=whole(4),
+        compiler_params=limit,
+        name="own",
+    )(*placed(pltpu.VMEM, mine, qall, qcore))
     return pl.pallas_call(
         functools.partial(solve_kernel, mp, zs, per_member, examples),
-        out_shape=jax.ShapeDtypeStruct((seq_count, queries.shape[2] * dp), jnp.float32),
-        in_specs=whole(4),
+        out_shape=jax.ShapeDtypeStruct((seq_count, columns), jnp.float32),
+        in_specs=whole(7),
         out_specs=whole(1)[0],
         compiler_params=limit,
         name="solve",
-    )(*placed(pltpu.VMEM, mine, other, qall, qcore))
+    )(*placed(pltpu.VMEM, other, *own_terms, qall, qcore))
 
 
 def power_of_two(n):

time: 43.5 us -> 38.1 us (0.88)
  waiting for transfers between devices: 11 us -> 5.97 us
    ppermute x14, waiting for transfers between devices: 7.47 us -> 4.35 us  [exchange(): lax.ppermute(value, axis, [(i, i ^ k * unit) for i in range(size)])]
    ppermute x3, waiting for transfers between devices: 3.51 us -> 1.62 us  [fast_device(): parts.append(lax.ppermute(sent[k], 'mp', [(i, i ^ k) for i in range(mp)]))]
    ppermute x14, starting transfers between devices: 18.3 us -> 17.1 us  [exchange(): lax.ppermute(value, axis, [(i, i ^ k * unit) for i in range(size)])]
    ppermute x3, starting transfers between devices: 3.55 us -> 4.59 us  [fast_device(): parts.append(lax.ppermute(sent[k], 'mp', [(i, i ^ k) for i in range(mp)]))]
    pallas_call x1, Pallas kernels: 7.26 us -> 6.35 us  [fast_device(): pl.pallas_call(functools.partial(project_kernel, vocab_rows, rank, slot_l...]
    pallas_call x0 -> x1, Pallas kernels: none -> 0.7 us  [fast_device(): pl.pallas_call(functools.partial(own_kernel, mp), out_shape=[pltpu.VMEM((...]
  transfers between devices with their start and end apart: 17 -> 17, of which waited for: 6 -> 5; matrix products, arithmetic and copies ran while one was open for 0% -> 0% of each run, Pallas kernels for 19% -> 4%
where the time goes in v1:
time: 38.1 us; the launch traced here: 38 us
  starting transfers between devices  21.7 us (57%)
  Pallas kernels  10.1 us (27%)
  waiting for transfers between devices  5.97 us (16%)
    ppermute x14, starting transfers between devices, exchange(): lax.ppermute(value, axis, [(i, i ^ k * unit) for i in range(size)])  17.1 us
    pallas_call x1, Pallas kernels, fast_device(): pl.pallas_call(functools.partial(project_kernel, vocab_rows, rank, slot_l...  6.35 us
    ppermute x3, starting transfers between devices, fast_device(): parts.append(lax.ppermute(sent[k], 'mp', [(i, i ^ k) for i in range(mp)]))  4.59 us
    ppermute x14, waiting for transfers between devices, exchange(): lax.ppermute(value, axis, [(i, i ^ k * unit) for i in range(size)])  4.35 us
    pallas_call x1, Pallas kernels, fast_device(): pl.pallas_call(functools.partial(solve_kernel, mp, zs, per_member, exampl...  2.06 us
    ppermute x3, waiting for transfers between devices, fast_device(): parts.append(lax.ppermute(sent[k], 'mp', [(i, i ^ k) for i in range(mp)]))  1.62 us
    pallas_call x1, Pallas kernels, fast_device(): pl.pallas_call(functools.partial(sketch_kernel, rank, slot_len, per_membe...  0.95 us
  transfers between devices with their start and end apart: 17, of which 5 were waited for; matrix products, arithmetic and copies ran while one was open for 0% of the time, Pallas kernels for 4%

profile of v1, /device:TPU:0, one launch (start us, length us, event | category | flops | bytes accessed | tf_op | source)
XLA Modules:
  0.0 38.0 jit_solution(8476274819177367611)
XLA Ops:
  0.0 0.0 copy-start.1
  0.0 0.0 copy-start
  0.0 6.3 %project.1 = (f32[256,128]{1,0:T(8,128)S(1)}, f32[256,128]{1,0:T(8,128)S(1)}, f32[256,128]{1,0:T(8,128)S(1)}, f32[256,128]{1,0:T(8,128)S(1)}) custom-call(s32[8,128]{1,0:T(8,128)} %bitcast.37, bf16[32,32064]{1,0:T(8,128)(2,1)} %bitcast.23, bf16[1024,1024]{1,0:T(8,128)(2,1)} %grad0_any.1, bf16[1024,1024]{1,0:T(8,128)(2,1)} %bitcast.21, ...), custom_call_target="tpu_custom_call" | custom-call | tf_op jit(solution)/shard_map/project/pallas_call | solution.py:375
  6.4 3.0 %collective-permute-start = (f32[256,128]{1,0:T(8,128)S(1)}, f32[256,128]{1,0:T(8,128)S(1)}, u32[]{:S(2)}, u32[]{:S(2)}) collective-permute-start(f32[256,128]{1,0:T(8,128)S(1)} %get-tuple-element.18), channel_id=1, source_target_pairs={{0,1},{1,0},{2,3},{3,2},{4,5},{5,4},{6,7},{7,6},{8,9},{9,8},{10,11... | collective-permute-start | bytes 393224 | tf_op jit(solution)/shard_map/ppermute | solution.py:407
  9.4 1.5 %collective-permute-start.1 = (f32[256,128]{1,0:T(8,128)S(1)}, f32[256,128]{1,0:T(8,128)S(1)}, u32[]{:S(2)}, u32[]{:S(2)}) collective-permute-start(f32[256,128]{1,0:T(8,128)S(1)} %get-tuple-element.19), channel_id=1, source_target_pairs={{0,2},{1,3},{2,0},{3,1},{4,6},{5,7},{6,4},{7,5},{8,10},{9,11},{10,... | collective-permute-start | bytes 393224 | tf_op jit(solution)/shard_map/ppermute | solution.py:407
  10.9 0.0 collective-permute-start.2
  10.9 0.0 copy-done.1
  11.0 4.0 %collective-permute-start.12 = (bf16[2,32,256]{2,1,0:T(8,128)(2,1)S(1)}, bf16[2,32,256]{2,1,0:T(8,128)(2,1)S(1)}, u32[]{:S(2)}, u32[]{:S(2)}) collective-permute-start(bf16[2,32,256]{2,1,0:T(8,128)(2,1)S(1)} %bitcast.30), channel_id=1, source_target_pairs={{0,24},{4,28},{8,16},{12,20},{16,8},{20,12},{24,0},{28,4},{1,25},{... | collective-permute-start | bytes 98312 | tf_op jit(solution)/shard_map/ppermute | solution.py:346
  15.0 0.0 collective-permute-start.11
  15.0 0.0 collective-permute-done.refs_1_
  15.0 0.6 %collective-permute-start.10 = (bf16[2,32,256]{2,1,0:T(8,128)(2,1)S(1)}, bf16[2,32,256]{2,1,0:T(8,128)(2,1)S(1)}, u32[]{:S(2)}, u32[]{:S(2)}) collective-permute-start(bf16[2,32,256]{2,1,0:T(8,128)(2,1)S(1)} %bitcast.32), channel_id=1, source_target_pairs={{0,8},{4,12},{8,0},{12,4},{16,24},{20,28},{24,16},{28,20},{1,9},{5... | collective-permute-start | bytes 98312 | tf_op jit(solution)/shard_map/ppermute | solution.py:346
  15.6 1.6 %collective-permute-done.1.refs_2_ = f32[256,128]{1,0:T(8,128)S(1)} collective-permute-done((f32[256,128]{1,0:T(8,128)S(1)}, f32[256,128]{1,0:T(8,128)S(1)}, u32[]{:S(2)}, u32[]{:S(2)}) %collective-permute-start.1) | collective-permute-done | bytes 131104 | tf_op jit(solution)/shard_map/ppermute | solution.py:407
  17.2 0.0 collective-permute-done.2.refs_3_
  17.2 0.0 copy-done
  17.2 0.9 %sketch.1 = f32[32,128]{1,0:T(8,128)S(1)} custom-call(s32[8]{0:T(128)S(1)} %copy-done, f32[256,128]{1,0:T(8,128)S(1)} %get-tuple-element.17.refs_0_, f32[256,128]{1,0:T(8,128)S(1)} %collective-permute-done.refs_1_, f32[256,128]{1,0:T(8,128)S(1)} %collective-permute-done.1.refs_2_, f32[256,128]{1,0:T(8,128)S(1)} %collective-permute-done.2.refs_3_), custom_call_target="tpu_custom_call" | custom-call | tf_op jit(solution)/shard_map/sketch/pallas_call | solution.py:411
  18.1 3.7 %collective-permute-start.5 = (f32[32,128]{1,0:T(8,128)S(1)}, f32[32,128]{1,0:T(8,128)S(1)}, u32[]{:S(2)}, u32[]{:S(2)}) collective-permute-start(f32[32,128]{1,0:T(8,128)S(1)} %sketch.1), channel_id=1, source_target_pairs={{0,24},{4,28},{8,16},{12,20},{16,8},{20,12},{24,0},{28,4},{1,25},{... | collective-permute-start | bytes 49160 | tf_op jit(solution)/shard_map/ppermute | solution.py:346
  21.8 0.0 collective-permute-start.4
  21.8 0.0 collective-permute-done.12
  21.8 0.8 %collective-permute-start.3 = (f32[32,128]{1,0:T(8,128)S(1)}, f32[32,128]{1,0:T(8,128)S(1)}, u32[]{:S(2)}, u32[]{:S(2)}) collective-permute-start(f32[32,128]{1,0:T(8,128)S(1)} %sketch.1), channel_id=1, source_target_pairs={{0,8},{4,12},{8,0},{12,4},{16,24},{20,28},{24,16},{28,20},{1,9},{5... | collective-permute-start | bytes 49160 | tf_op jit(solution)/shard_map/ppermute | solution.py:346
  22.6 0.0 collective-permute-done.11
  22.6 0.0 collective-permute-done.10
  22.6 1.6 %collective-permute-start.14 = (bf16[4,2,32,256]{3,2,1,0:T(8,128)(2,1)S(1)}, bf16[4,2,32,256]{3,2,1,0:T(8,128)(2,1)S(1)}, u32[]{:S(2)}, u32[]{:S(2)}) collective-permute-start(bf16[4,2,32,256]{3,2,1,0:T(8,128)(2,1)S(1)} %get-tuple-element.30), channel_id=1, source_target_pairs={{0,2},{1,3},{2,0},{3,1},{4,6},{5,7},{6,4},{7,5},{8,10},{9,11},{10,... | collective-permute-start | bytes 393224 | tf_op jit(solution)/shard_map/ppermute | solution.py:346
  24.2 0.5 %collective-permute-start.13 = (bf16[4,2,32,256]{3,2,1,0:T(8,128)(2,1)S(1)}, bf16[4,2,32,256]{3,2,1,0:T(8,128)(2,1)S(1)}, u32[]{:S(2)}, u32[]{:S(2)}) collective-permute-start(bf16[4,2,32,256]{3,2,1,0:T(8,128)(2,1)S(1)} %get-tuple-element.30), channel_id=1, source_target_pairs={{0,1},{1,0},{2,3},{3,2},{4,5},{5,4},{6,7},{7,6},{8,9},{9,8},{10,11... | collective-permute-start | bytes 393224 | tf_op jit(solution)/shard_map/ppermute | solution.py:346
  24.8 0.0 collective-permute-done.5
  24.8 1.4 %collective-permute-start.15 = (bf16[4,2,32,256]{3,2,1,0:T(8,128)(2,1)S(1)}, bf16[4,2,32,256]{3,2,1,0:T(8,128)(2,1)S(1)}, u32[]{:S(2)}, u32[]{:S(2)}) collective-permute-start(bf16[4,2,32,256]{3,2,1,0:T(8,128)(2,1)S(1)} %get-tuple-element.30), channel_id=1, source_target_pairs={{0,3},{1,2},{2,1},{3,0},{4,7},{5,6},{6,5},{7,4},{8,11},{9,10},{10,... | collective-permute-start | bytes 393224 | tf_op jit(solution)/shard_map/ppermute | solution.py:346
  26.2 0.2 collective-permute-done.4
  26.5 0.0 collective-permute-done.3
  26.5 1.6 %collective-permute-start.8 = (f32[128,128]{1,0:T(8,128)S(1)}, f32[128,128]{1,0:T(8,128)S(1)}, u32[]{:S(2)}, u32[]{:S(2)}) collective-permute-start(f32[128,128]{1,0:T(8,128)S(1)} %pad_maximum_fusion.2), channel_id=1, source_target_pairs={{0,3},{1,2},{2,1},{3,0},{4,7},{5,6},{6,5},{7,4},{8,11},{9,10},{10,... | collective-permute-start | bytes 196616 | tf_op jit(solution)/shard_map/ppermute | solution.py:346
  28.0 1.2 %collective-permute-start.7 = (f32[128,128]{1,0:T(8,128)S(1)}, f32[128,128]{1,0:T(8,128)S(1)}, u32[]{:S(2)}, u32[]{:S(2)}) collective-permute-start(f32[128,128]{1,0:T(8,128)S(1)} %pad_maximum_fusion.2), channel_id=1, source_target_pairs={{0,2},{1,3},{2,0},{3,1},{4,6},{5,7},{6,4},{7,5},{8,10},{9,11},{10,... | collective-permute-start | bytes 196616 | tf_op jit(solution)/shard_map/ppermute | solution.py:346
  29.2 0.8 %collective-permute-done.14 = bf16[4,2,32,256]{3,2,1,0:T(8,128)(2,1)S(1)} collective-permute-done((bf16[4,2,32,256]{3,2,1,0:T(8,128)(2,1)S(1)}, bf16[4,2,32,256]{3,2,1,0:T(8,128)(2,1)S(1)}, u32[]{:S(2)}, u32[]{:S(2)}) %collective-permute-start.14) | collective-permute-done | bytes 131104 | tf_op jit(solution)/shard_map/ppermute | solution.py:346
  30.0 1.6 %collective-permute-start.6 = (f32[128,128]{1,0:T(8,128)S(1)}, f32[128,128]{1,0:T(8,128)S(1)}, u32[]{:S(2)}, u32[]{:S(2)}) collective-permute-start(f32[128,128]{1,0:T(8,128)S(1)} %pad_maximum_fusion.2), channel_id=1, source_target_pairs={{0,1},{1,0},{2,3},{3,2},{4,5},{5,4},{6,7},{7,6},{8,9},{9,8},{10,11... | collective-permute-start | bytes 196616 | tf_op jit(solution)/shard_map/ppermute | solution.py:346
  31.6 0.0 collective-permute-done.13
  31.6 0.0 collective-permute-done.15
  31.7 0.1 pad_maximum_fusion.qmine_ref
  31.7 0.1 collective-permute-start.16
  31.8 2.5 %collective-permute-done.6 = f32[128,128]{1,0:T(8,128)S(1)} collective-permute-done((f32[128,128]{1,0:T(8,128)S(1)}, f32[128,128]{1,0:T(8,128)S(1)}, u32[]{:S(2)}, u32[]{:S(2)}) %collective-permute-start.6) | collective-permute-done | bytes 65568 | tf_op jit(solution)/shard_map/ppermute | solution.py:346
  34.3 0.0 collective-permute-done.7
  34.3 0.0 collective-permute-done.8
  34.3 0.1 collective-permute-start.9
  34.4 0.0 collective-permute-done.16.qother_ref
  34.4 0.7 %own.1 = (bf16[2,64,1024]{2,1,0:T(8,128)(2,1)S(1)}, f32[2,32,32]{2,1,0:T(8,128)S(1)}, f32[2,32,256]{2,1,0:T(8,128)S(1)}, f32[2,8,256]{2,1,0:T(8,128)S(1)}) custom-call(f32[512,128]{1,0:T(8,128)S(1)} %constant_dynamic-update-slice_fusion.mine_ref, bf16[4,4,2,32,256]{4,3,2,1,0:T(8,128)(2,1)S(1)} %pad_maximum_fusion.qmine_ref, ...), custom_call_target="tpu_custom_call" | custom-call | tf_op jit(solution)/shard_map/own/pallas_call | solution.py:429
  35.1 0.8 %collective-permute-done.9.other_ref = f32[512,128]{1,0:T(8,128)S(1)} collective-permute-done((f32[512,128]{1,0:T(8,128)S(1)}, f32[512,128]{1,0:T(8,128)S(1)}, u32[]{:S(2)}, u32[]{:S(2)}) %collective-permute-start.9) | collective-permute-done | bytes 262176 | tf_op jit(solution)/shard_map/ppermute | solution.py:346
  35.9 2.1 %solve.1 = f32[8,256]{1,0:T(8,128)} custom-call(f32[512,128]{1,0:T(8,128)S(1)} %collective-permute-done.9.other_ref, bf16[2,64,1024]{2,1,0:T(8,128)(2,1)S(1)} %get-tuple-element.25.both_ref, f32[2,32,32]{2,1,0:T(8,128)S(1)} %get-tuple-element.26.gram_ref, f32[2,32,256]{2,1,0:T(8,128)S(1)} %get-tuple-element.27.u_ref, ...), custom_call_target="tpu_custom_call" | custom-call | tf_op jit(solution)/shard_map/solve/pallas_call | solution.py:442
  (9 shorter events, 0.1 us)
Async XLA Ops:
  0.0 11.0 %copy-start.1 = (bf16[2,256,32]{1,2,0:T(8,128)(2,1)S(1)}, bf16[2,256,32]{1,2,0:T(8,128)(2,1)}, u32[]{:S(2)}) copy-start(bf16[2,256,32]{1,2,0:T(8,128)(2,1)} %param.19) | copy-start | bytes 98308
  0.0 17.2 %copy-start = (s32[8]{0:T(128)S(1)}, s32[8]{0:T(128)}, u32[]{:S(2)}) copy-start(s32[8]{0:T(128)} %len_ref.1) | copy-start | bytes 100
  6.4 8.6 %collective-permute-start = (f32[256,128]{1,0:T(8,128)S(1)}, f32[256,128]{1,0:T(8,128)S(1)}, u32[]{:S(2)}, u32[]{:S(2)}) collective-permute-start(f32[256,128]{1,0:T(8,128)S(1)} %get-tuple-element.18), channel_id=1, source_target_pairs={{0,1},{1,0},{2,3},{3,2},{4,5},{5,4},{6,7},{7,6},{8,9},{9,8},{10,11... | collective-permute-start | bytes 393224 | tf_op jit(solution)/shard_map/ppermute | solution.py:407
  9.4 7.8 %collective-permute-start.1 = (f32[256,128]{1,0:T(8,128)S(1)}, f32[256,128]{1,0:T(8,128)S(1)}, u32[]{:S(2)}, u32[]{:S(2)}) collective-permute-start(f32[256,128]{1,0:T(8,128)S(1)} %get-tuple-element.19), channel_id=1, source_target_pairs={{0,2},{1,3},{2,0},{3,1},{4,6},{5,7},{6,4},{7,5},{8,10},{9,11},{10,... | collective-permute-start | bytes 393224 | tf_op jit(solution)/shard_map/ppermute | solution.py:407
  10.9 6.2 %collective-permute-start.2 = (f32[256,128]{1,0:T(8,128)S(1)}, f32[256,128]{1,0:T(8,128)S(1)}, u32[]{:S(2)}, u32[]{:S(2)}) collective-permute-start(f32[256,128]{1,0:T(8,128)S(1)} %get-tuple-element.20), channel_id=1, source_target_pairs={{0,3},{1,2},{2,1},{3,0},{4,7},{5,6},{6,5},{7,4},{8,11},{9,10},{10,... | collective-permute-start | bytes 393224 | tf_op jit(solution)/shard_map/ppermute | solution.py:407
  11.0 10.9 %collective-permute-start.12 = (bf16[2,32,256]{2,1,0:T(8,128)(2,1)S(1)}, bf16[2,32,256]{2,1,0:T(8,128)(2,1)S(1)}, u32[]{:S(2)}, u32[]{:S(2)}) collective-permute-start(bf16[2,32,256]{2,1,0:T(8,128)(2,1)S(1)} %bitcast.30), channel_id=1, source_target_pairs={{0,24},{4,28},{8,16},{12,20},{16,8},{20,12},{24,0},{28,4},{1,25},{... | collective-permute-start | bytes 98312 | tf_op jit(solution)/shard_map/ppermute | solution.py:346
  15.0 7.6 %collective-permute-start.11 = (bf16[2,32,256]{2,1,0:T(8,128)(2,1)S(1)}, bf16[2,32,256]{2,1,0:T(8,128)(2,1)S(1)}, u32[]{:S(2)}, u32[]{:S(2)}) collective-permute-start(bf16[2,32,256]{2,1,0:T(8,128)(2,1)S(1)} %bitcast.31), channel_id=1, source_target_pairs={{0,16},{4,20},{8,24},{12,28},{16,0},{20,4},{24,8},{28,12},{1,17},{... | collective-permute-start | bytes 98312 | tf_op jit(solution)/shard_map/ppermute | solution.py:346
  15.0 7.6 %collective-permute-start.10 = (bf16[2,32,256]{2,1,0:T(8,128)(2,1)S(1)}, bf16[2,32,256]{2,1,0:T(8,128)(2,1)S(1)}, u32[]{:S(2)}, u32[]{:S(2)}) collective-permute-start(bf16[2,32,256]{2,1,0:T(8,128)(2,1)S(1)} %bitcast.32), channel_id=1, source_target_pairs={{0,8},{4,12},{8,0},{12,4},{16,24},{20,28},{24,16},{28,20},{1,9},{5... | collective-permute-start | bytes 98312 | tf_op jit(solution)/shard_map/ppermute | solution.py:346
  18.1 6.6 %collective-permute-start.5 = (f32[32,128]{1,0:T(8,128)S(1)}, f32[32,128]{1,0:T(8,128)S(1)}, u32[]{:S(2)}, u32[]{:S(2)}) collective-permute-start(f32[32,128]{1,0:T(8,128)S(1)} %sketch.1), channel_id=1, source_target_pairs={{0,24},{4,28},{8,16},{12,20},{16,8},{20,12},{24,0},{28,4},{1,25},{... | collective-permute-start | bytes 49160 | tf_op jit(solution)/shard_map/ppermute | solution.py:346
  21.8 4.6 %collective-permute-start.4 = (f32[32,128]{1,0:T(8,128)S(1)}, f32[32,128]{1,0:T(8,128)S(1)}, u32[]{:S(2)}, u32[]{:S(2)}) collective-permute-start(f32[32,128]{1,0:T(8,128)S(1)} %sketch.1), channel_id=1, source_target_pairs={{0,16},{4,20},{8,24},{12,28},{16,0},{20,4},{24,8},{28,12},{1,17},{... | collective-permute-start | bytes 49160 | tf_op jit(solution)/shard_map/ppermute | solution.py:346
  21.8 4.6 %collective-permute-start.3 = (f32[32,128]{1,0:T(8,128)S(1)}, f32[32,128]{1,0:T(8,128)S(1)}, u32[]{:S(2)}, u32[]{:S(2)}) collective-permute-start(f32[32,128]{1,0:T(8,128)S(1)} %sketch.1), channel_id=1, source_target_pairs={{0,8},{4,12},{8,0},{12,4},{16,24},{20,28},{24,16},{28,20},{1,9},{5... | collective-permute-start | bytes 49160 | tf_op jit(solution)/shard_map/ppermute | solution.py:346
  22.6 7.4 %collective-permute-start.14 = (bf16[4,2,32,256]{3,2,1,0:T(8,128)(2,1)S(1)}, bf16[4,2,32,256]{3,2,1,0:T(8,128)(2,1)S(1)}, u32[]{:S(2)}, u32[]{:S(2)}) collective-permute-start(bf16[4,2,32,256]{3,2,1,0:T(8,128)(2,1)S(1)} %get-tuple-element.30), channel_id=1, source_target_pairs={{0,2},{1,3},{2,0},{3,1},{4,6},{5,7},{6,4},{7,5},{8,10},{9,11},{10,... | collective-permute-start | bytes 393224 | tf_op jit(solution)/shard_map/ppermute | solution.py:346
  24.2 7.4 %collective-permute-start.13 = (bf16[4,2,32,256]{3,2,1,0:T(8,128)(2,1)S(1)}, bf16[4,2,32,256]{3,2,1,0:T(8,128)(2,1)S(1)}, u32[]{:S(2)}, u32[]{:S(2)}) collective-permute-start(bf16[4,2,32,256]{3,2,1,0:T(8,128)(2,1)S(1)} %get-tuple-element.30), channel_id=1, source_target_pairs={{0,1},{1,0},{2,3},{3,2},{4,5},{5,4},{6,7},{7,6},{8,9},{9,8},{10,11... | collective-permute-start | bytes 393224 | tf_op jit(solution)/shard_map/ppermute | solution.py:346
  24.8 6.9 %collective-permute-start.15 = (bf16[4,2,32,256]{3,2,1,0:T(8,128)(2,1)S(1)}, bf16[4,2,32,256]{3,2,1,0:T(8,128)(2,1)S(1)}, u32[]{:S(2)}, u32[]{:S(2)}) collective-permute-start(bf16[4,2,32,256]{3,2,1,0:T(8,128)(2,1)S(1)} %get-tuple-element.30), channel_id=1, source_target_pairs={{0,3},{1,2},{2,1},{3,0},{4,7},{5,6},{6,5},{7,4},{8,11},{9,10},{10,... | collective-permute-start | bytes 393224 | tf_op jit(solution)/shard_map/ppermute | solution.py:346
  26.5 7.8 %collective-permute-start.8 = (f32[128,128]{1,0:T(8,128)S(1)}, f32[128,128]{1,0:T(8,128)S(1)}, u32[]{:S(2)}, u32[]{:S(2)}) collective-permute-start(f32[128,128]{1,0:T(8,128)S(1)} %pad_maximum_fusion.2), channel_id=1, source_target_pairs={{0,3},{1,2},{2,1},{3,0},{4,7},{5,6},{6,5},{7,4},{8,11},{9,10},{10,... | collective-permute-start | bytes 196616 | tf_op jit(solution)/shard_map/ppermute | solution.py:346
  28.0 6.3 %collective-permute-start.7 = (f32[128,128]{1,0:T(8,128)S(1)}, f32[128,128]{1,0:T(8,128)S(1)}, u32[]{:S(2)}, u32[]{:S(2)}) collective-permute-start(f32[128,128]{1,0:T(8,128)S(1)} %pad_maximum_fusion.2), channel_id=1, source_target_pairs={{0,2},{1,3},{2,0},{3,1},{4,6},{5,7},{6,4},{7,5},{8,10},{9,11},{10,... | collective-permute-start | bytes 196616 | tf_op jit(solution)/shard_map/ppermute | solution.py:346
  30.0 4.3 %collective-permute-start.6 = (f32[128,128]{1,0:T(8,128)S(1)}, f32[128,128]{1,0:T(8,128)S(1)}, u32[]{:S(2)}, u32[]{:S(2)}) collective-permute-start(f32[128,128]{1,0:T(8,128)S(1)} %pad_maximum_fusion.2), channel_id=1, source_target_pairs={{0,1},{1,0},{2,3},{3,2},{4,5},{5,4},{6,7},{7,6},{8,9},{9,8},{10,11... | collective-permute-start | bytes 196616 | tf_op jit(solution)/shard_map/ppermute | solution.py:346
  31.7 2.7 %collective-permute-start.16 = (bf16[4,4,2,32,256]{4,3,2,1,0:T(8,128)(2,1)S(1)}, bf16[4,4,2,32,256]{4,3,2,1,0:T(8,128)(2,1)S(1)}, u32[]{:S(2)}, u32[]{:S(2)}) collective-permute-start(bf16[4,4,2,32,256]{4,3,2,1,0:T(8,128)(2,1)S(1)} %pad_maximum_fusion.qmine_ref), channel_id=1, source_target_pairs={{0,4},{4,0},{8,12},{12,8},{16,20},{20,16},{24,28},{28,24},{1,5},{5... | collective-permute-start | bytes 1572872 | tf_op jit(solution)/shard_map/ppermute | solution.py:346
  34.3 1.6 %collective-permute-start.9 = (f32[512,128]{1,0:T(8,128)S(1)}, f32[512,128]{1,0:T(8,128)S(1)}, u32[]{:S(2)}, u32[]{:S(2)}) collective-permute-start(f32[512,128]{1,0:T(8,128)S(1)} %constant_dynamic-update-slice_fusion.mine_ref), channel_id=1, source_target_pairs={{0,4},{4,0},{8,12},{12,8},{16,20},{20,16},{24,28},{28,24},{1,5},{5... | collective-permute-start | bytes 786440 | tf_op jit(solution)/shard_map/ppermute | solution.py:346

commit v2 on v1

--- a/solution.py
+++ b/solution.py
@@ -10,6 +10,7 @@
 
 ITERS = 2
 LANES = 128
+AHEAD = 1
 
 damping = 0.01
 epsilon = 1e-06
@@ -103,6 +104,7 @@
     slot_len,
     per_member,
     ids_any,
+    len_any,
     table_any,
     grad0_any,
     grad1_any,
@@ -112,8 +114,9 @@
     basis2_any,
     *refs,
 ):
-    out_refs = refs[:-8]
-    ids_ref, table_ref, wide_ref, weight_ref, place_ref, scalar_ref, small_sem, wide_sem = refs[-8:]
+    out_refs = refs[:-9]
+    ids_ref, len_ref, table_ref, wide_ref, weight_ref, place_ref, scalar_ref = refs[-9:-2]
+    small_sem, wide_sem = refs[-2:]
     members = len(out_refs)
     me = lax.axis_index("mp").astype(jnp.int32)
     offset = me * vocab_rows
@@ -128,17 +131,20 @@
         return pltpu.make_async_copy(source.at[rows_of(r), :], wide_ref.at[k, rows_of(r), :], wide_sem.at[k, r])
 
     ids_copy = pltpu.make_async_copy(ids_any, ids_ref, small_sem.at[0])
+    len_copy = pltpu.make_async_copy(len_any, len_ref, small_sem.at[5])
     table_copy = pltpu.make_async_copy(table_any, table_ref, small_sem.at[1])
     basis_copies = [
         pltpu.make_async_copy(basis, weight_ref.at[k, pl.ds(k * rank, rank), :], small_sem.at[2 + k])
         for k, basis in enumerate((basis0_any, basis1_any, basis2_any))
     ]
     ids_copy.start()
+    table_copy.start()
+    len_copy.start()
     for copy in basis_copies:
         copy.start()
-    table_copy.start()
-    for k in range(3):
-        wide_copy(k, 0).start()
+    for r in range(AHEAD):
+        for k in range(3):
+            wide_copy(k, r).start()
     for k in range(3):
         if k:
             weight_ref[k, : k * rank, :] = jnp.zeros((k * rank, weight_ref.shape[2]), jnp.bfloat16)
@@ -146,33 +152,34 @@
     ids_copy.wait()
     local = ids_ref[...] - offset
     position = lax.broadcasted_iota(jnp.int32, local.shape, 1)
-    place_ref[0] = jnp.clip(local >> 7, 0, main - 1) * LANES
-    place_ref[1] = (position - local) & (LANES - 1)
+    place_ref[...] = jnp.clip(local >> 7, 0, main - 1) * LANES + ((position - local) & (LANES - 1))
     scalar_copy = pltpu.make_async_copy(place_ref, scalar_ref, small_sem.at[0])
     scalar_copy.start()
     scalar_copy.wait()
+    len_copy.wait()
     for copy in basis_copies:
         copy.wait()
     table_copy.wait()
-    for r in range(1, members):
+    for r in range(AHEAD, members):
         for k in range(3):
             wide_copy(k, r).start()
 
     lane = lax.broadcasted_iota(jnp.int32, (rank, LANES), 1)
+    row = lax.broadcasted_iota(jnp.int32, (slot_len, LANES), 0)
+    column = lax.broadcasted_iota(jnp.int32, (slot_len, LANES), 1)
     tail = vocab_rows - main * LANES
 
     def step(r, _):
-        member = me ^ r
-        values = []
         for k in range(3):
             wide_copy(k, r).wait()
+        values = []
         for s in range(per_member):
-            seq = member * per_member + s
+            seq = (me ^ r) * per_member + s
             found = jnp.zeros((rank, LANES), jnp.float32)
             for t in range(slot_len):
-                start = pl.multiple_of(scalar_ref[0, seq, t], LANES)
-                block = table_ref[:, pl.ds(start, LANES)].astype(jnp.float32)
-                found = jnp.where(lane == t, pltpu.roll(block, scalar_ref[1, seq, t], 1), found)
+                word = scalar_ref[seq, t]
+                block = table_ref[:, pl.ds(pl.multiple_of(word & -LANES, LANES), LANES)].astype(jnp.float32)
+                found = jnp.where(lane == t, pltpu.roll(block, word & (LANES - 1), 1), found)
             mine = ids_ref[pl.ds(seq, 1), :] - offset
             found = jnp.where((mine >= 0) & (mine < main * LANES), found, 0.0)
             if tail:
@@ -183,8 +190,10 @@
             total = contract_last(wide_ref[0, rows, :], weight_ref[0])
             total += contract_last(wide_ref[1, rows, :], weight_ref[1])
             total += contract_last(wide_ref[2, rows, :], weight_ref[2])
+            live = len_ref[seq]
+            share = jnp.where(row < live, 1.0 / jnp.full(row.shape, live, jnp.int32).astype(jnp.float32), 0.0)
             spread = jnp.concatenate([jnp.zeros((3 * rank, LANES), jnp.float32), found], axis=0)
-            values.append(total + spread.T)
+            values.append(total * jnp.where(column < 2 * rank, share, 1.0) + spread.T)
         for place, out_ref in enumerate(out_refs):
 
             @pl.when(r == place)
@@ -197,22 +206,33 @@
     lax.fori_loop(0, members, step, 0)
 
 
-def sketch_kernel(rank, slot_len, per_member, len_ref, *refs):
+def split(value):
+    high = value.astype(jnp.bfloat16)
+    return high, (value - high.astype(jnp.float32)).astype(jnp.bfloat16)
+
+
+def fold_rows(value):
+    half = value.shape[0] // 2
+    return value[:half] + value[half:]
+
+
+def sketch_kernel(rank, slot_len, per_member, *refs):
     parts, out_ref, full_ref = refs[:-2], refs[-2], refs[-1]
-    me = lax.axis_index("mp").astype(jnp.int32)
     lane = lax.broadcasted_iota(jnp.int32, (8, LANES), 1)
     for s in range(per_member):
         rows = slice(s * slot_len, (s + 1) * slot_len)
         total = parts[0][rows, :]
         for part in parts[1:]:
             total = total + part[rows, :]
-        live = len_ref[me * per_member + s]
-        position = lax.broadcasted_iota(jnp.int32, (slot_len, LANES), 0)
-        share = 1.0 / jnp.full((slot_len, LANES), live, jnp.int32).astype(jnp.float32)
-        weighted = total * jnp.where(position < live, share, 0.0)
-        full_ref[s] = lax.dot_general(
-            weighted, total, (((0,), (0,)), ((), ())), precision=highest, preferred_element_type=jnp.float32
+        grads_high, grads_low = split(total[:, : 2 * rank])
+        high, low = split(total)
+        product = lax.dot_general(
+            jnp.concatenate([grads_high, grads_low], axis=1),
+            jnp.concatenate([high, low], axis=1),
+            (((0,), (0,)), ((), ())),
+            preferred_element_type=jnp.float32,
         )
+        full_ref[s] = fold_rows(product[:, :LANES] + product[:, LANES:])
         for layer in range(2):
             source = 3 - layer
             unit = jnp.zeros((8, LANES), jnp.float32)
@@ -237,46 +257,29 @@
     return value
 
 
-def split_halves(ref, layer, first, count, chunk):
+def split_rows(ref, layer, first, count, chunk):
     wide = [ref[pl.ds(layer * 8 + first + j, count, stride=16), :] for j in range(chunk // LANES)]
-    value = jnp.concatenate(wide, axis=1)
-    high = value.astype(jnp.bfloat16)
-    low = (value - high.astype(jnp.float32)).astype(jnp.bfloat16)
-    return jnp.concatenate([high, low], axis=0)
-
-
-def fold_rows(value):
-    half = value.shape[0] // 2
-    return value[:half] + value[half:]
-
-
-def fold(value):
-    half = value.shape[1] // 2
-    value = fold_rows(value)
-    return value[:, :half] + value[:, half:]
-
-
-def own_kernel(mp, mine_ref, qmine_ref, qother_ref, both_ref, gram_ref, u_ref, norm_ref):
+    return jnp.concatenate(split(jnp.concatenate(wide, axis=1)), axis=0)
+
+
+def own_kernel(mp, mine_ref, qmine_ref, qother_ref, both_ref, u_ref, norm_ref):
     me = lax.axis_index("mp").astype(jnp.int32)
-    half = gram_ref.shape[1]
+    half = u_ref.shape[1]
     columns = qmine_ref.shape[1] * qmine_ref.shape[3]
     chunk = qmine_ref.shape[4]
     for layer in range(2):
-        square = jnp.zeros((2 * half, 2 * half), jnp.float32)
         mixed = [jnp.zeros((2 * half, columns), jnp.float32) for _ in range(2)]
         norms = [jnp.zeros((columns, LANES), jnp.float32) for _ in range(2)]
         for k in range(mp):
-            both = split_halves(mine_ref, layer, (me ^ k) * (chunk // LANES), half, chunk)
+            both = split_rows(mine_ref, layer, (me ^ k) * (chunk // LANES), half, chunk)
             both_ref[layer, :, k * chunk : (k + 1) * chunk] = both
-            square += contract_last(both, both)
-            for side, ref in enumerate((qmine_ref, qother_ref)):
-                query = ref[k, :, layer].reshape(columns, chunk)
+            for side in range(2):
+                query = (qmine_ref, qother_ref)[side][k, :, layer].reshape(columns, chunk)
                 mixed[side] += contract_last(both, query)
                 wide_query = query.astype(jnp.float32)
                 squared = wide_query * wide_query
                 for j in range(chunk // LANES):
                     norms[side] += squared[:, j * LANES : (j + 1) * LANES]
-        gram_ref[layer] = fold(square)
         for side in range(2):
             u_ref[layer, :, side * columns : (side + 1) * columns] = fold_rows(mixed[side])
         norm_ref[layer] = lax.dot_general(
@@ -289,33 +292,34 @@
 
 
 def solve_kernel(
-    mp, zs, per_member, examples, other_ref, both_ref, gram_ref, u_ref, norm_ref, qmine_ref, qother_ref, out_ref
+    mp, zs, per_member, examples, other_ref, both_ref, u_ref, norm_ref, qmine_ref, qother_ref, out_ref
 ):
     me = lax.axis_index("mp").astype(jnp.int32)
     mydp = lax.axis_index("dp").astype(jnp.int32)
-    half = gram_ref.shape[1]
+    half = u_ref.shape[1]
     columns = qmine_ref.shape[1] * qmine_ref.shape[3]
     chunk = qmine_ref.shape[4]
     scores = None
     for layer in range(2):
-        square = jnp.zeros((2 * half, 2 * half), jnp.float32)
-        cross = jnp.zeros((2 * half, 2 * half), jnp.float32)
+        square = jnp.zeros((4 * half, 4 * half), jnp.float32)
         mixed = [jnp.zeros((2 * half, columns), jnp.float32) for _ in range(2)]
         for k in range(mp):
-            both = split_halves(other_ref, layer, (me ^ k) * (chunk // LANES), half, chunk)
-            square += contract_last(both, both)
-            cross += contract_last(both_ref[layer, :, k * chunk : (k + 1) * chunk], both)
-            for side, ref in enumerate((qmine_ref, qother_ref)):
-                mixed[side] += contract_last(both, ref[k, :, layer].reshape(columns, chunk))
-        cross = fold(cross)
+            other = split_rows(other_ref, layer, (me ^ k) * (chunk // LANES), half, chunk)
+            every = jnp.concatenate([both_ref[layer, :, k * chunk : (k + 1) * chunk], other], axis=0)
+            square += contract_last(every, every)
+            for side in range(2):
+                query = (qmine_ref, qother_ref)[side][k, :, layer].reshape(columns, chunk)
+                mixed[side] += contract_last(other, query)
+        gram = jnp.concatenate([fold_rows(square[: 2 * half]), fold_rows(square[2 * half :])], axis=0)
         own_u = u_ref[layer]
         other_u = jnp.concatenate([fold_rows(m) for m in mixed], axis=1)
         u = jnp.concatenate([own_u, other_u], axis=0)
-        dot = functools.partial(jnp.dot, precision=highest, preferred_element_type=jnp.float32)
-        ku = jnp.concatenate(
-            [dot(gram_ref[layer], own_u) + dot(cross, other_u), dot(cross.T, own_u) + dot(fold(square), other_u)],
-            axis=0,
+        u_high, u_low = split(jnp.concatenate([own_u, own_u, other_u, other_u], axis=0))
+        gram_high, gram_low = split(gram)
+        terms = jnp.dot(
+            jnp.concatenate([gram_high, gram_low], axis=0), u_high, preferred_element_type=jnp.float32
         )
+        ku = fold_rows(terms) + jnp.dot(gram_high, u_low, preferred_element_type=jnp.float32)
         qq = norm_ref[layer][:1]
         uu = jnp.sum(u * u, axis=0, keepdims=True)
         uku = jnp.sum(u * ku, axis=0, keepdims=True)
@@ -327,24 +331,30 @@
         sd = a * u + beta * ku
         dd = jnp.maximum(a * a * qq + 2.0 * a * beta * uu + beta * beta * uku, 0.0)
         step1 = rr / (jnp.sum(sd * sd, axis=0, keepdims=True) / examples + damping * dd + epsilon)
-        value = step0 * u + step1 * sd
+
+        def own_rows(value):
+            starts = [k * zs * per_member for k in range(mp)]
+            return jnp.concatenate([value[start : start + per_member] for start in starts], axis=0)
+
+        value = step0 * own_rows(u) + step1 * own_rows(sd)
         scores = value if scores is None else scores + value
-    own = jnp.concatenate(
-        [scores[k * zs * per_member : k * zs * per_member + per_member] for k in range(mp)], axis=0
-    )
-    own = swap_blocks(own, 0, per_member, me, mp)
+    own = swap_blocks(scores, 0, per_member, me, mp)
     width = columns // zs
-    own = jnp.concatenate(
-        [own[:, (c * zs + z) * width : (c * zs + z + 1) * width] for z in range(zs) for c in range(2)], axis=1
-    )
+    places = [(c * zs + z) * width for z in range(zs) for c in range(2)]
+    own = jnp.concatenate([own[:, place : place + width] for place in places], axis=1)
     out_ref[...] = swap_blocks(own, 1, width, mydp, 2 * zs)
 
 
-def exchange(value, axis, count, unit=1):
-    size = lax.axis_size(axis)
-    return [value] + [
-        lax.ppermute(value, axis, [(i, i ^ (k * unit)) for i in range(size)]) for k in range(1, count)
-    ]
+def exchange_z(value, zs):
+    return [value] + [lax.ppermute(value, "dp", [(i, i ^ (2 * k)) for i in range(2 * zs)]) for k in range(1, zs)]
+
+
+def exchange_mp(value, mp):
+    return [value] + [lax.ppermute(value, "mp", [(i, i ^ k) for i in range(mp)]) for k in range(1, mp)]
+
+
+def exchange_core(value, dp):
+    return lax.ppermute(value, "dp", [(i, i ^ 1) for i in range(dp)])
 
 
 def fast_device(
@@ -375,16 +385,17 @@
     sent = pl.pallas_call(
         functools.partial(project_kernel, vocab_rows, rank, slot_len, per_member),
         out_shape=[pltpu.VMEM((block, LANES), jnp.float32)] * mp,
-        in_specs=[pl.BlockSpec(memory_space=pl.ANY)] * 8,
+        in_specs=[pl.BlockSpec(memory_space=pl.ANY)] * 9,
         out_specs=whole(mp),
         scratch_shapes=[
             pltpu.VMEM((seq_count, slot_len), jnp.int32),
+            pltpu.SMEM((seq_count,), jnp.int32),
             pltpu.VMEM((rank, vocab_rows), jnp.bfloat16),
             pltpu.VMEM((3, token_count, features), jnp.bfloat16),
             pltpu.VMEM((3, LANES, features), jnp.bfloat16),
-            pltpu.VMEM((2, seq_count, slot_len), jnp.int32),
-            pltpu.SMEM((2, seq_count, slot_len), jnp.int32),
-            pltpu.SemaphoreType.DMA((5,)),
+            pltpu.VMEM((seq_count, slot_len), jnp.int32),
+            pltpu.SMEM((seq_count, slot_len), jnp.int32),
+            pltpu.SemaphoreType.DMA((6,)),
             pltpu.SemaphoreType.DMA((3, mp)),
         ],
         compiler_params=limit,
@@ -393,6 +404,7 @@
         *placed(
             pltpu.HBM,
             token_ids.reshape(seq_count, slot_len),
+            lengths,
             vocab_basis.T,
             embed_grads,
             layer_grads[0],
@@ -406,23 +418,23 @@
     for k in range(1, mp):
         parts.append(lax.ppermute(sent[k], "mp", [(i, i ^ k) for i in range(mp)]))
 
-    pieces = exchange(queries.transpose(0, 2, 1), "dp", zs, 2)
+    pieces = exchange_z(queries.transpose(0, 2, 1), zs)
     rows = per_member * 2 * 8
     units = pl.pallas_call(
         functools.partial(sketch_kernel, rank, slot_len, per_member),
         out_shape=pltpu.VMEM((rows, LANES), jnp.float32),
-        in_specs=[pl.BlockSpec(memory_space=pltpu.SMEM)] + whole(mp),
+        in_specs=whole(mp),
         out_specs=whole(1)[0],
-        scratch_shapes=[pltpu.VMEM((per_member, LANES, LANES), jnp.float32)],
+        scratch_shapes=[pltpu.VMEM((per_member, 2 * rank, LANES), jnp.float32)],
         compiler_params=limit,
         name="sketch",
-    )(lengths, *placed(pltpu.VMEM, *parts))
-    along_z = jnp.concatenate(exchange(units, "dp", zs, 2))
+    )(*placed(pltpu.VMEM, *parts))
+    along_z = jnp.concatenate(exchange_z(units, zs))
     pieces = lax.optimization_barrier((*pieces, units))[:-1]
-    qall = jnp.stack(exchange(jnp.stack(pieces), "mp", mp))
-    qcore = exchange(qall, "dp", 2)[1]
-    mine = jnp.concatenate(exchange(along_z, "mp", mp))
-    other = exchange(mine, "dp", 2)[1]
+    qall = jnp.stack(exchange_mp(jnp.stack(pieces), mp))
+    qcore = exchange_core(qall, dp)
+    mine = jnp.concatenate(exchange_mp(along_z, mp))
+    other = exchange_core(mine, dp)
     half = mp * zs * per_member
     columns = queries.shape[2] * dp
     sketch_len = rank * rank
@@ -430,19 +442,18 @@
         functools.partial(own_kernel, mp),
         out_shape=[
             pltpu.VMEM((2, 2 * half, sketch_len), jnp.bfloat16),
-            pltpu.VMEM((2, half, half), jnp.float32),
             pltpu.VMEM((2, half, columns), jnp.float32),
             pltpu.VMEM((2, 8, columns), jnp.float32),
         ],
         in_specs=whole(3),
-        out_specs=whole(4),
+        out_specs=whole(3),
         compiler_params=limit,
         name="own",
     )(*placed(pltpu.VMEM, mine, qall, qcore))
     return pl.pallas_call(
         functools.partial(solve_kernel, mp, zs, per_member, examples),
         out_shape=jax.ShapeDtypeStruct((seq_count, columns), jnp.float32),
-        in_specs=whole(7),
+        in_specs=whole(6),
         out_specs=whole(1)[0],
         compiler_params=limit,
         name="solve",

time: 38.1 us -> 37.3 us (0.979)
  Pallas kernels: 10.1 us -> 9.22 us
    pallas_call x1, Pallas kernels: 0.95 us -> 0.37 us  [fast_device(): pl.pallas_call(functools.partial(sketch_kernel, rank, slot_len, per_membe...]
  transfers between devices with their start and end apart: 17 -> 17, of which waited for: 5 -> 5; matrix products, arithmetic and copies ran while one was open for 0% -> 0% of each run, Pallas kernels for 4% -> 3%
where the time goes in v2:
time: 37.3 us; the launch traced here: 37.2 us
  starting transfers between devices  21.7 us (58%)
  Pallas kernels  9.22 us (25%)
  waiting for transfers between devices  6.02 us (16%)
    ppermute x6, starting transfers between devices, exchange_z(): lax.ppermute(value, 'dp', [(i, i ^ 2 * k) for i in range(2 * zs)])  9.06 us
    ppermute x6, starting transfers between devices, exchange_mp(): lax.ppermute(value, 'mp', [(i, i ^ k) for i in range(mp)])  7.94 us
    pallas_call x1, Pallas kernels, fast_device(): pl.pallas_call(functools.partial(project_kernel, vocab_rows, rank, slot_l...  6.26 us
    ppermute x3, starting transfers between devices, fast_device(): parts.append(lax.ppermute(sent[k], 'mp', [(i, i ^ k) for i in range(mp)]))  4.58 us
    ppermute x6, waiting for transfers between devices, exchange_mp(): lax.ppermute(value, 'mp', [(i, i ^ k) for i in range(mp)])  3.25 us
    pallas_call x1, Pallas kernels, fast_device(): pl.pallas_call(functools.partial(solve_kernel, mp, zs, per_member, exampl...  1.95 us
    ppermute x3, waiting for transfers between devices, fast_device(): parts.append(lax.ppermute(sent[k], 'mp', [(i, i ^ k) for i in range(mp)]))  1.62 us
    ppermute x2, waiting for transfers between devices, exchange_core(): return lax.ppermute(value, 'dp', [(i, i ^ 1) for i in range(dp)])  0.88 us
  transfers between devices with their start and end apart: 17, of which 5 were waited for; matrix products, arithmetic and copies ran while one was open for 0% of the time, Pallas kernels for 3%

profile of v2, /device:TPU:0, one launch (start us, length us, event | category | flops | bytes accessed | tf_op | source)
XLA Modules:
  0.0 37.2 jit_solution(12291197848320264307)
XLA Ops:
  0.0 0.0 copy-start
  0.0 6.3 %project.1 = (f32[256,128]{1,0:T(8,128)S(1)}, f32[256,128]{1,0:T(8,128)S(1)}, f32[256,128]{1,0:T(8,128)S(1)}, f32[256,128]{1,0:T(8,128)S(1)}) custom-call(s32[8,128]{1,0:T(8,128)} %bitcast.37, s32[8]{0:T(128)} %len_any.1, bf16[32,32064]{1,0:T(8,128)(2,1)} %bitcast.23, bf16[1024,1024]{1,0:T(8,128)(2,1)} %grad0_any.1, bf16[1024,1024]{1,0:T(8,128)(2,1)} %bitcast.21, ...), custom_call_target="tpu_custom_call" | custom-call | tf_op jit(solution)/shard_map/project/pallas_call | solution.py:385
  6.3 3.0 %collective-permute-start = (f32[256,128]{1,0:T(8,128)S(1)}, f32[256,128]{1,0:T(8,128)S(1)}, u32[]{:S(2)}, u32[]{:S(2)}) collective-permute-start(f32[256,128]{1,0:T(8,128)S(1)} %get-tuple-element.17), channel_id=1, source_target_pairs={{0,1},{1,0},{2,3},{3,2},{4,5},{5,4},{6,7},{7,6},{8,9},{9,8},{10,11... | collective-permute-start | bytes 393224 | tf_op jit(solution)/shard_map/ppermute | solution.py:419
  9.3 1.5 %collective-permute-start.1 = (f32[256,128]{1,0:T(8,128)S(1)}, f32[256,128]{1,0:T(8,128)S(1)}, u32[]{:S(2)}, u32[]{:S(2)}) collective-permute-start(f32[256,128]{1,0:T(8,128)S(1)} %get-tuple-element.18), channel_id=1, source_target_pairs={{0,2},{1,3},{2,0},{3,1},{4,6},{5,7},{6,4},{7,5},{8,10},{9,11},{10,... | collective-permute-start | bytes 393224 | tf_op jit(solution)/shard_map/ppermute | solution.py:419
  10.9 0.0 collective-permute-start.2
  10.9 0.0 copy-done
  10.9 4.0 %collective-permute-start.12 = (bf16[2,32,256]{2,1,0:T(8,128)(2,1)S(1)}, bf16[2,32,256]{2,1,0:T(8,128)(2,1)S(1)}, u32[]{:S(2)}, u32[]{:S(2)}) collective-permute-start(bf16[2,32,256]{2,1,0:T(8,128)(2,1)S(1)} %bitcast.30), channel_id=1, source_target_pairs={{0,24},{4,28},{8,16},{12,20},{16,8},{20,12},{24,0},{28,4},{1,25},{... | collective-permute-start | bytes 98312 | tf_op jit(solution)/shard_map/ppermute | solution.py:349
  14.9 0.0 collective-permute-start.11
  14.9 0.0 collective-permute-done.refs_1_
  14.9 0.6 %collective-permute-start.10 = (bf16[2,32,256]{2,1,0:T(8,128)(2,1)S(1)}, bf16[2,32,256]{2,1,0:T(8,128)(2,1)S(1)}, u32[]{:S(2)}, u32[]{:S(2)}) collective-permute-start(bf16[2,32,256]{2,1,0:T(8,128)(2,1)S(1)} %bitcast.32), channel_id=1, source_target_pairs={{0,8},{4,12},{8,0},{12,4},{16,24},{20,28},{24,16},{28,20},{1,9},{5... | collective-permute-start | bytes 98312 | tf_op jit(solution)/shard_map/ppermute | solution.py:349
  15.5 1.6 %collective-permute-done.1.refs_2_ = f32[256,128]{1,0:T(8,128)S(1)} collective-permute-done((f32[256,128]{1,0:T(8,128)S(1)}, f32[256,128]{1,0:T(8,128)S(1)}, u32[]{:S(2)}, u32[]{:S(2)}) %collective-permute-start.1) | collective-permute-done | bytes 131104 | tf_op jit(solution)/shard_map/ppermute | solution.py:419
  17.1 0.0 collective-permute-done.2.refs_3_
  17.1 0.4 %sketch.1 = f32[32,128]{1,0:T(8,128)S(1)} custom-call(f32[256,128]{1,0:T(8,128)S(1)} %get-tuple-element.16.refs_0_, f32[256,128]{1,0:T(8,128)S(1)} %collective-permute-done.refs_1_, f32[256,128]{1,0:T(8,128)S(1)} %collective-permute-done.1.refs_2_, f32[256,128]{1,0:T(8,128)S(1)} %collective-permute-done.2.refs_3_), custom_call_target="tpu_custom_call" | custom-call | tf_op jit(solution)/shard_map/sketch/pallas_call | solution.py:423
  17.5 3.7 %collective-permute-start.5 = (f32[32,128]{1,0:T(8,128)S(1)}, f32[32,128]{1,0:T(8,128)S(1)}, u32[]{:S(2)}, u32[]{:S(2)}) collective-permute-start(f32[32,128]{1,0:T(8,128)S(1)} %sketch.1), channel_id=1, source_target_pairs={{0,24},{4,28},{8,16},{12,20},{16,8},{20,12},{24,0},{28,4},{1,25},{... | collective-permute-start | bytes 49160 | tf_op jit(solution)/shard_map/ppermute | solution.py:349
  21.1 0.0 collective-permute-start.4
  21.1 0.0 collective-permute-done.12
  21.2 0.8 %collective-permute-start.3 = (f32[32,128]{1,0:T(8,128)S(1)}, f32[32,128]{1,0:T(8,128)S(1)}, u32[]{:S(2)}, u32[]{:S(2)}) collective-permute-start(f32[32,128]{1,0:T(8,128)S(1)} %sketch.1), channel_id=1, source_target_pairs={{0,8},{4,12},{8,0},{12,4},{16,24},{20,28},{24,16},{28,20},{1,9},{5... | collective-permute-start | bytes 49160 | tf_op jit(solution)/shard_map/ppermute | solution.py:349
  21.9 0.0 collective-permute-done.11
  21.9 0.0 collective-permute-done.10
  22.0 1.6 %collective-permute-start.14 = (bf16[4,2,32,256]{3,2,1,0:T(8,128)(2,1)S(1)}, bf16[4,2,32,256]{3,2,1,0:T(8,128)(2,1)S(1)}, u32[]{:S(2)}, u32[]{:S(2)}) collective-permute-start(bf16[4,2,32,256]{3,2,1,0:T(8,128)(2,1)S(1)} %get-tuple-element.28), channel_id=1, source_target_pairs={{0,2},{1,3},{2,0},{3,1},{4,6},{5,7},{6,4},{7,5},{8,10},{9,11},{10,... | collective-permute-start | bytes 393224 | tf_op jit(solution)/shard_map/ppermute | solution.py:353
  23.6 0.5 %collective-permute-start.13 = (bf16[4,2,32,256]{3,2,1,0:T(8,128)(2,1)S(1)}, bf16[4,2,32,256]{3,2,1,0:T(8,128)(2,1)S(1)}, u32[]{:S(2)}, u32[]{:S(2)}) collective-permute-start(bf16[4,2,32,256]{3,2,1,0:T(8,128)(2,1)S(1)} %get-tuple-element.28), channel_id=1, source_target_pairs={{0,1},{1,0},{2,3},{3,2},{4,5},{5,4},{6,7},{7,6},{8,9},{9,8},{10,11... | collective-permute-start | bytes 393224 | tf_op jit(solution)/shard_map/ppermute | solution.py:353
  24.1 0.0 collective-permute-done.5
  24.1 1.4 %collective-permute-start.15 = (bf16[4,2,32,256]{3,2,1,0:T(8,128)(2,1)S(1)}, bf16[4,2,32,256]{3,2,1,0:T(8,128)(2,1)S(1)}, u32[]{:S(2)}, u32[]{:S(2)}) collective-permute-start(bf16[4,2,32,256]{3,2,1,0:T(8,128)(2,1)S(1)} %get-tuple-element.28), channel_id=1, source_target_pairs={{0,3},{1,2},{2,1},{3,0},{4,7},{5,6},{6,5},{7,4},{8,11},{9,10},{10,... | collective-permute-start | bytes 393224 | tf_op jit(solution)/shard_map/ppermute | solution.py:353
  25.5 0.2 collective-permute-done.4
  25.8 0.0 collective-permute-done.3
  25.8 1.5 %collective-permute-start.8 = (f32[128,128]{1,0:T(8,128)S(1)}, f32[128,128]{1,0:T(8,128)S(1)}, u32[]{:S(2)}, u32[]{:S(2)}) collective-permute-start(f32[128,128]{1,0:T(8,128)S(1)} %pad_maximum_fusion.2), channel_id=1, source_target_pairs={{0,3},{1,2},{2,1},{3,0},{4,7},{5,6},{6,5},{7,4},{8,11},{9,10},{10,... | collective-permute-start | bytes 196616 | tf_op jit(solution)/shard_map/ppermute | solution.py:353
  27.3 1.2 %collective-permute-start.7 = (f32[128,128]{1,0:T(8,128)S(1)}, f32[128,128]{1,0:T(8,128)S(1)}, u32[]{:S(2)}, u32[]{:S(2)}) collective-permute-start(f32[128,128]{1,0:T(8,128)S(1)} %pad_maximum_fusion.2), channel_id=1, source_target_pairs={{0,2},{1,3},{2,0},{3,1},{4,6},{5,7},{6,4},{7,5},{8,10},{9,11},{10,... | collective-permute-start | bytes 196616 | tf_op jit(solution)/shard_map/ppermute | solution.py:353
  28.6 0.8 %collective-permute-done.14 = bf16[4,2,32,256]{3,2,1,0:T(8,128)(2,1)S(1)} collective-permute-done((bf16[4,2,32,256]{3,2,1,0:T(8,128)(2,1)S(1)}, bf16[4,2,32,256]{3,2,1,0:T(8,128)(2,1)S(1)}, u32[]{:S(2)}, u32[]{:S(2)}) %collective-permute-start.14) | collective-permute-done | bytes 131104 | tf_op jit(solution)/shard_map/ppermute | solution.py:353
  29.3 1.6 %collective-permute-start.6 = (f32[128,128]{1,0:T(8,128)S(1)}, f32[128,128]{1,0:T(8,128)S(1)}, u32[]{:S(2)}, u32[]{:S(2)}) collective-permute-start(f32[128,128]{1,0:T(8,128)S(1)} %pad_maximum_fusion.2), channel_id=1, source_target_pairs={{0,1},{1,0},{2,3},{3,2},{4,5},{5,4},{6,7},{7,6},{8,9},{9,8},{10,11... | collective-permute-start | bytes 196616 | tf_op jit(solution)/shard_map/ppermute | solution.py:353
  30.9 0.0 collective-permute-done.13
  30.9 0.0 collective-permute-done.15
  31.0 0.1 pad_maximum_fusion.qmine_ref
  31.1 0.1 collective-permute-start.16
  31.1 2.5 %collective-permute-done.6 = f32[128,128]{1,0:T(8,128)S(1)} collective-permute-done((f32[128,128]{1,0:T(8,128)S(1)}, f32[128,128]{1,0:T(8,128)S(1)}, u32[]{:S(2)}, u32[]{:S(2)}) %collective-permute-start.6) | collective-permute-done | bytes 65568 | tf_op jit(solution)/shard_map/ppermute | solution.py:353
  33.6 0.0 collective-permute-done.7
  33.6 0.0 collective-permute-done.8
  33.6 0.1 collective-permute-start.9
  33.7 0.0 collective-permute-done.16.qother_ref
  33.7 0.6 %own.1 = (bf16[2,64,1024]{2,1,0:T(8,128)(2,1)S(1)}, f32[2,32,256]{2,1,0:T(8,128)S(1)}, f32[2,8,256]{2,1,0:T(8,128)S(1)}) custom-call(f32[512,128]{1,0:T(8,128)S(1)} %constant_dynamic-update-slice_fusion.mine_ref, bf16[4,4,2,32,256]{4,3,2,1,0:T(8,128)(2,1)S(1)} %pad_maximum_fusion.qmine_ref, bf16[4,4,2,32,256]{4,3,2,1,0:T(8,128)(2,1)S(1)} %collective-permute-done.16.qother_ref), custom_call_target="tpu_custom_call" | custom-call | tf_op jit(solution)/shard_map/own/pallas_call | solution.py:441
  34.4 0.9 %collective-permute-done.9.other_ref = f32[512,128]{1,0:T(8,128)S(1)} collective-permute-done((f32[512,128]{1,0:T(8,128)S(1)}, f32[512,128]{1,0:T(8,128)S(1)}, u32[]{:S(2)}, u32[]{:S(2)}) %collective-permute-start.9) | collective-permute-done | bytes 262176 | tf_op jit(solution)/shard_map/ppermute | solution.py:357
  35.2 2.0 %solve.1 = f32[8,256]{1,0:T(8,128)} custom-call(f32[512,128]{1,0:T(8,128)S(1)} %collective-permute-done.9.other_ref, bf16[2,64,1024]{2,1,0:T(8,128)(2,1)S(1)} %get-tuple-element.24.both_ref, f32[2,32,256]{2,1,0:T(8,128)S(1)} %get-tuple-element.25.u_ref, f32[2,8,256]{2,1,0:T(8,128)S(1)} %get-tuple-element.26.norm_ref, ...), custom_call_target="tpu_custom_call" | custom-call | tf_op jit(solution)/shard_map/solve/pallas_call | solution.py:453
  (9 shorter events, 0.1 us)
Async XLA Ops:
  0.0 10.9 %copy-start = (bf16[2,256,32]{1,2,0:T(8,128)(2,1)S(1)}, bf16[2,256,32]{1,2,0:T(8,128)(2,1)}, u32[]{:S(2)}) copy-start(bf16[2,256,32]{1,2,0:T(8,128)(2,1)} %param.19) | copy-start | bytes 98308
  6.3 8.6 %collective-permute-start = (f32[256,128]{1,0:T(8,128)S(1)}, f32[256,128]{1,0:T(8,128)S(1)}, u32[]{:S(2)}, u32[]{:S(2)}) collective-permute-start(f32[256,128]{1,0:T(8,128)S(1)} %get-tuple-element.17), channel_id=1, source_target_pairs={{0,1},{1,0},{2,3},{3,2},{4,5},{5,4},{6,7},{7,6},{8,9},{9,8},{10,11... | collective-permute-start | bytes 393224 | tf_op jit(solution)/shard_map/ppermute | solution.py:419
  9.3 7.8 %collective-permute-start.1 = (f32[256,128]{1,0:T(8,128)S(1)}, f32[256,128]{1,0:T(8,128)S(1)}, u32[]{:S(2)}, u32[]{:S(2)}) collective-permute-start(f32[256,128]{1,0:T(8,128)S(1)} %get-tuple-element.18), channel_id=1, source_target_pairs={{0,2},{1,3},{2,0},{3,1},{4,6},{5,7},{6,4},{7,5},{8,10},{9,11},{10,... | collective-permute-start | bytes 393224 | tf_op jit(solution)/shard_map/ppermute | solution.py:419
  10.9 6.2 %collective-permute-start.2 = (f32[256,128]{1,0:T(8,128)S(1)}, f32[256,128]{1,0:T(8,128)S(1)}, u32[]{:S(2)}, u32[]{:S(2)}) collective-permute-start(f32[256,128]{1,0:T(8,128)S(1)} %get-tuple-element.19), channel_id=1, source_target_pairs={{0,3},{1,2},{2,1},{3,0},{4,7},{5,6},{6,5},{7,4},{8,11},{9,10},{10,... | collective-permute-start | bytes 393224 | tf_op jit(solution)/shard_map/ppermute | solution.py:419
  10.9 10.3 %collective-permute-start.12 = (bf16[2,32,256]{2,1,0:T(8,128)(2,1)S(1)}, bf16[2,32,256]{2,1,0:T(8,128)(2,1)S(1)}, u32[]{:S(2)}, u32[]{:S(2)}) collective-permute-start(bf16[2,32,256]{2,1,0:T(8,128)(2,1)S(1)} %bitcast.30), channel_id=1, source_target_pairs={{0,24},{4,28},{8,16},{12,20},{16,8},{20,12},{24,0},{28,4},{1,25},{... | collective-permute-start | bytes 98312 | tf_op jit(solution)/shard_map/ppermute | solution.py:349
  14.9 7.0 %collective-permute-start.11 = (bf16[2,32,256]{2,1,0:T(8,128)(2,1)S(1)}, bf16[2,32,256]{2,1,0:T(8,128)(2,1)S(1)}, u32[]{:S(2)}, u32[]{:S(2)}) collective-permute-start(bf16[2,32,256]{2,1,0:T(8,128)(2,1)S(1)} %bitcast.31), channel_id=1, source_target_pairs={{0,16},{4,20},{8,24},{12,28},{16,0},{20,4},{24,8},{28,12},{1,17},{... | collective-permute-start | bytes 98312 | tf_op jit(solution)/shard_map/ppermute | solution.py:349
  14.9 7.0 %collective-permute-start.10 = (bf16[2,32,256]{2,1,0:T(8,128)(2,1)S(1)}, bf16[2,32,256]{2,1,0:T(8,128)(2,1)S(1)}, u32[]{:S(2)}, u32[]{:S(2)}) collective-permute-start(bf16[2,32,256]{2,1,0:T(8,128)(2,1)S(1)} %bitcast.32), channel_id=1, source_target_pairs={{0,8},{4,12},{8,0},{12,4},{16,24},{20,28},{24,16},{28,20},{1,9},{5... | collective-permute-start | bytes 98312 | tf_op jit(solution)/shard_map/ppermute | solution.py:349
  17.5 6.6 %collective-permute-start.5 = (f32[32,128]{1,0:T(8,128)S(1)}, f32[32,128]{1,0:T(8,128)S(1)}, u32[]{:S(2)}, u32[]{:S(2)}) collective-permute-start(f32[32,128]{1,0:T(8,128)S(1)} %sketch.1), channel_id=1, source_target_pairs={{0,24},{4,28},{8,16},{12,20},{16,8},{20,12},{24,0},{28,4},{1,25},{... | collective-permute-start | bytes 49160 | tf_op jit(solution)/shard_map/ppermute | solution.py:349
  21.1 4.6 %collective-permute-start.4 = (f32[32,128]{1,0:T(8,128)S(1)}, f32[32,128]{1,0:T(8,128)S(1)}, u32[]{:S(2)}, u32[]{:S(2)}) collective-permute-start(f32[32,128]{1,0:T(8,128)S(1)} %sketch.1), channel_id=1, source_target_pairs={{0,16},{4,20},{8,24},{12,28},{16,0},{20,4},{24,8},{28,12},{1,17},{... | collective-permute-start | bytes 49160 | tf_op jit(solution)/shard_map/ppermute | solution.py:349
  21.2 4.6 %collective-permute-start.3 = (f32[32,128]{1,0:T(8,128)S(1)}, f32[32,128]{1,0:T(8,128)S(1)}, u32[]{:S(2)}, u32[]{:S(2)}) collective-permute-start(f32[32,128]{1,0:T(8,128)S(1)} %sketch.1), channel_id=1, source_target_pairs={{0,8},{4,12},{8,0},{12,4},{16,24},{20,28},{24,16},{28,20},{1,9},{5... | collective-permute-start | bytes 49160 | tf_op jit(solution)/shard_map/ppermute | solution.py:349
  22.0 7.3 %collective-permute-start.14 = (bf16[4,2,32,256]{3,2,1,0:T(8,128)(2,1)S(1)}, bf16[4,2,32,256]{3,2,1,0:T(8,128)(2,1)S(1)}, u32[]{:S(2)}, u32[]{:S(2)}) collective-permute-start(bf16[4,2,32,256]{3,2,1,0:T(8,128)(2,1)S(1)} %get-tuple-element.28), channel_id=1, source_target_pairs={{0,2},{1,3},{2,0},{3,1},{4,6},{5,7},{6,4},{7,5},{8,10},{9,11},{10,... | collective-permute-start | bytes 393224 | tf_op jit(solution)/shard_map/ppermute | solution.py:353
  23.6 7.4 %collective-permute-start.13 = (bf16[4,2,32,256]{3,2,1,0:T(8,128)(2,1)S(1)}, bf16[4,2,32,256]{3,2,1,0:T(8,128)(2,1)S(1)}, u32[]{:S(2)}, u32[]{:S(2)}) collective-permute-start(bf16[4,2,32,256]{3,2,1,0:T(8,128)(2,1)S(1)} %get-tuple-element.28), channel_id=1, source_target_pairs={{0,1},{1,0},{2,3},{3,2},{4,5},{5,4},{6,7},{7,6},{8,9},{9,8},{10,11... | collective-permute-start | bytes 393224 | tf_op jit(solution)/shard_map/ppermute | solution.py:353
  24.1 6.9 %collective-permute-start.15 = (bf16[4,2,32,256]{3,2,1,0:T(8,128)(2,1)S(1)}, bf16[4,2,32,256]{3,2,1,0:T(8,128)(2,1)S(1)}, u32[]{:S(2)}, u32[]{:S(2)}) collective-permute-start(bf16[4,2,32,256]{3,2,1,0:T(8,128)(2,1)S(1)} %get-tuple-element.28), channel_id=1, source_target_pairs={{0,3},{1,2},{2,1},{3,0},{4,7},{5,6},{6,5},{7,4},{8,11},{9,10},{10,... | collective-permute-start | bytes 393224 | tf_op jit(solution)/shard_map/ppermute | solution.py:353
  25.8 7.8 %collective-permute-start.8 = (f32[128,128]{1,0:T(8,128)S(1)}, f32[128,128]{1,0:T(8,128)S(1)}, u32[]{:S(2)}, u32[]{:S(2)}) collective-permute-start(f32[128,128]{1,0:T(8,128)S(1)} %pad_maximum_fusion.2), channel_id=1, source_target_pairs={{0,3},{1,2},{2,1},{3,0},{4,7},{5,6},{6,5},{7,4},{8,11},{9,10},{10,... | collective-permute-start | bytes 196616 | tf_op jit(solution)/shard_map/ppermute | solution.py:353
  27.3 6.3 %collective-permute-start.7 = (f32[128,128]{1,0:T(8,128)S(1)}, f32[128,128]{1,0:T(8,128)S(1)}, u32[]{:S(2)}, u32[]{:S(2)}) collective-permute-start(f32[128,128]{1,0:T(8,128)S(1)} %pad_maximum_fusion.2), channel_id=1, source_target_pairs={{0,2},{1,3},{2,0},{3,1},{4,6},{5,7},{6,4},{7,5},{8,10},{9,11},{10,... | collective-permute-start | bytes 196616 | tf_op jit(solution)/shard_map/ppermute | solution.py:353
  29.3 4.3 %collective-permute-start.6 = (f32[128,128]{1,0:T(8,128)S(1)}, f32[128,128]{1,0:T(8,128)S(1)}, u32[]{:S(2)}, u32[]{:S(2)}) collective-permute-start(f32[128,128]{1,0:T(8,128)S(1)} %pad_maximum_fusion.2), channel_id=1, source_target_pairs={{0,1},{1,0},{2,3},{3,2},{4,5},{5,4},{6,7},{7,6},{8,9},{9,8},{10,11... | collective-permute-start | bytes 196616 | tf_op jit(solution)/shard_map/ppermute | solution.py:353
  31.1 2.7 %collective-permute-start.16 = (bf16[4,4,2,32,256]{4,3,2,1,0:T(8,128)(2,1)S(1)}, bf16[4,4,2,32,256]{4,3,2,1,0:T(8,128)(2,1)S(1)}, u32[]{:S(2)}, u32[]{:S(2)}) collective-permute-start(bf16[4,4,2,32,256]{4,3,2,1,0:T(8,128)(2,1)S(1)} %pad_maximum_fusion.qmine_ref), channel_id=1, source_target_pairs={{0,4},{4,0},{8,12},{12,8},{16,20},{20,16},{24,28},{28,24},{1,5},{5... | collective-permute-start | bytes 1572872 | tf_op jit(solution)/shard_map/ppermute | solution.py:357
  33.6 1.6 %collective-permute-start.9 = (f32[512,128]{1,0:T(8,128)S(1)}, f32[512,128]{1,0:T(8,128)S(1)}, u32[]{:S(2)}, u32[]{:S(2)}) collective-permute-start(f32[512,128]{1,0:T(8,128)S(1)} %constant_dynamic-update-slice_fusion.mine_ref), channel_id=1, source_target_pairs={{0,4},{4,0},{8,12},{12,8},{16,20},{20,16},{24,28},{28,24},{1,5},{5... | collective-permute-start | bytes 786440 | tf_op jit(solution)/shard_map/ppermute | solution.py:357

commit v3 on v2

--- a/solution.py
+++ b/solution.py
@@ -243,76 +243,59 @@
             out_ref[pl.ds((s * 2 + layer) * 8, 8), :] = unit
 
 
-def swap_blocks(value, axis, width, index, count):
-    size = value.shape[axis]
-    place = lax.broadcasted_iota(jnp.int32, value.shape, axis)
-    bit = 1
-    while bit < count:
-        shift = bit * width
-        up = pltpu.roll(value, shift, axis)
-        down = pltpu.roll(value, size - shift, axis)
-        other = jnp.where((place // shift) % 2 == 1, up, down)
-        value = jnp.where((index // bit) % 2 == 1, other, value)
-        bit *= 2
-    return value
-
-
 def split_rows(ref, layer, first, count, chunk):
     wide = [ref[pl.ds(layer * 8 + first + j, count, stride=16), :] for j in range(chunk // LANES)]
     return jnp.concatenate(split(jnp.concatenate(wide, axis=1)), axis=0)
 
 
-def own_kernel(mp, mine_ref, qmine_ref, qother_ref, both_ref, u_ref, norm_ref):
+def own_kernel(mp, zs, mine_ref, qmine_ref, qother_ref, both_ref, u_ref, norm_ref, query_ref):
     me = lax.axis_index("mp").astype(jnp.int32)
-    half = u_ref.shape[1]
-    columns = qmine_ref.shape[1] * qmine_ref.shape[3]
-    chunk = qmine_ref.shape[4]
+    mydp = lax.axis_index("dp").astype(jnp.int32)
+    half, columns = u_ref.shape[1:]
+    width, chunk = qmine_ref.shape[3:]
     for layer in range(2):
-        mixed = [jnp.zeros((2 * half, columns), jnp.float32) for _ in range(2)]
-        norms = [jnp.zeros((columns, LANES), jnp.float32) for _ in range(2)]
+        mixed = jnp.zeros((2 * half, columns), jnp.float32)
+        norms = jnp.zeros((columns, LANES), jnp.float32)
         for k in range(mp):
             both = split_rows(mine_ref, layer, (me ^ k) * (chunk // LANES), half, chunk)
             both_ref[layer, :, k * chunk : (k + 1) * chunk] = both
-            for side in range(2):
-                query = (qmine_ref, qother_ref)[side][k, :, layer].reshape(columns, chunk)
-                mixed[side] += contract_last(both, query)
-                wide_query = query.astype(jnp.float32)
-                squared = wide_query * wide_query
-                for j in range(chunk // LANES):
-                    norms[side] += squared[:, j * LANES : (j + 1) * LANES]
-        for side in range(2):
-            u_ref[layer, :, side * columns : (side + 1) * columns] = fold_rows(mixed[side])
+            for place in range(2 * zs):
+                away = (mydp // 2) ^ (place // 2)
+                query_ref[layer, k, place * width : (place + 1) * width, :] = jnp.where(
+                    mydp % 2 == place % 2, qmine_ref[k, away, layer], qother_ref[k, away, layer]
+                )
+            query = query_ref[layer, k]
+            mixed += contract_last(both, query)
+            wide_query = query.astype(jnp.float32)
+            squared = wide_query * wide_query
+            for j in range(chunk // LANES):
+                norms += squared[:, j * LANES : (j + 1) * LANES]
+        u_ref[layer] = fold_rows(mixed)
         norm_ref[layer] = lax.dot_general(
             jnp.ones((8, LANES), jnp.float32),
-            jnp.concatenate(norms, axis=0),
+            norms,
             (((1,), (1,)), ((), ())),
             precision=highest,
             preferred_element_type=jnp.float32,
         )
 
 
-def solve_kernel(
-    mp, zs, per_member, examples, other_ref, both_ref, u_ref, norm_ref, qmine_ref, qother_ref, out_ref
-):
+def solve_kernel(mp, zs, per_member, examples, other_ref, both_ref, u_ref, norm_ref, query_ref, out_ref):
     me = lax.axis_index("mp").astype(jnp.int32)
-    mydp = lax.axis_index("dp").astype(jnp.int32)
-    half = u_ref.shape[1]
-    columns = qmine_ref.shape[1] * qmine_ref.shape[3]
-    chunk = qmine_ref.shape[4]
+    half, columns = u_ref.shape[1:]
+    chunk = query_ref.shape[3]
     scores = None
     for layer in range(2):
         square = jnp.zeros((4 * half, 4 * half), jnp.float32)
-        mixed = [jnp.zeros((2 * half, columns), jnp.float32) for _ in range(2)]
+        mixed = jnp.zeros((2 * half, columns), jnp.float32)
         for k in range(mp):
             other = split_rows(other_ref, layer, (me ^ k) * (chunk // LANES), half, chunk)
             every = jnp.concatenate([both_ref[layer, :, k * chunk : (k + 1) * chunk], other], axis=0)
             square += contract_last(every, every)
-            for side in range(2):
-                query = (qmine_ref, qother_ref)[side][k, :, layer].reshape(columns, chunk)
-                mixed[side] += contract_last(other, query)
+            mixed += contract_last(other, query_ref[layer, k])
         gram = jnp.concatenate([fold_rows(square[: 2 * half]), fold_rows(square[2 * half :])], axis=0)
         own_u = u_ref[layer]
-        other_u = jnp.concatenate([fold_rows(m) for m in mixed], axis=1)
+        other_u = fold_rows(mixed)
         u = jnp.concatenate([own_u, other_u], axis=0)
         u_high, u_low = split(jnp.concatenate([own_u, own_u, other_u, other_u], axis=0))
         gram_high, gram_low = split(gram)
@@ -332,25 +315,24 @@
         dd = jnp.maximum(a * a * qq + 2.0 * a * beta * uu + beta * beta * uku, 0.0)
         step1 = rr / (jnp.sum(sd * sd, axis=0, keepdims=True) / examples + damping * dd + epsilon)
 
-        def own_rows(value):
-            starts = [k * zs * per_member for k in range(mp)]
-            return jnp.concatenate([value[start : start + per_member] for start in starts], axis=0)
-
-        value = step0 * own_rows(u) + step1 * own_rows(sd)
-        scores = value if scores is None else scores + value
-    own = swap_blocks(scores, 0, per_member, me, mp)
-    width = columns // zs
-    places = [(c * zs + z) * width for z in range(zs) for c in range(2)]
-    own = jnp.concatenate([own[:, place : place + width] for place in places], axis=1)
-    out_ref[...] = swap_blocks(own, 1, width, mydp, 2 * zs)
-
-
-def exchange_z(value, zs):
-    return [value] + [lax.ppermute(value, "dp", [(i, i ^ (2 * k)) for i in range(2 * zs)]) for k in range(1, zs)]
-
-
-def exchange_mp(value, mp):
-    return [value] + [lax.ppermute(value, "mp", [(i, i ^ k) for i in range(mp)]) for k in range(1, mp)]
+        value = [
+            step0 * u[start : start + per_member] + step1 * sd[start : start + per_member]
+            for start in range(0, half, zs * per_member)
+        ]
+        scores = value if scores is None else [total + part for total, part in zip(scores, value)]
+    for place in range(mp):
+        value = scores[0]
+        for k in range(1, mp):
+            value = jnp.where(me ^ k == place, scores[k], value)
+        out_ref[place * per_member : (place + 1) * per_member, :] = value
+
+
+def exchange(value, axis, count, unit=1):
+    size = lax.axis_size(axis)
+    found = [value]
+    for k in range(1, count):
+        found.append(lax.ppermute(value, axis, [(i, i ^ (k * unit)) for i in range(size)]))
+    return found
 
 
 def exchange_core(value, dp):
@@ -418,7 +400,7 @@
     for k in range(1, mp):
         parts.append(lax.ppermute(sent[k], "mp", [(i, i ^ k) for i in range(mp)]))
 
-    pieces = exchange_z(queries.transpose(0, 2, 1), zs)
+    pieces = exchange(queries.transpose(0, 2, 1), "dp", zs, 2)
     rows = per_member * 2 * 8
     units = pl.pallas_call(
         functools.partial(sketch_kernel, rank, slot_len, per_member),
@@ -429,35 +411,36 @@
         compiler_params=limit,
         name="sketch",
     )(*placed(pltpu.VMEM, *parts))
-    along_z = jnp.concatenate(exchange_z(units, zs))
+    along_z = jnp.concatenate(exchange(units, "dp", zs, 2))
     pieces = lax.optimization_barrier((*pieces, units))[:-1]
-    qall = jnp.stack(exchange_mp(jnp.stack(pieces), mp))
+    qall = jnp.stack(exchange(jnp.stack(pieces), "mp", mp))
     qcore = exchange_core(qall, dp)
-    mine = jnp.concatenate(exchange_mp(along_z, mp))
+    mine = jnp.concatenate(exchange(along_z, "mp", mp))
     other = exchange_core(mine, dp)
     half = mp * zs * per_member
     columns = queries.shape[2] * dp
     sketch_len = rank * rank
     own_terms = pl.pallas_call(
-        functools.partial(own_kernel, mp),
+        functools.partial(own_kernel, mp, zs),
         out_shape=[
             pltpu.VMEM((2, 2 * half, sketch_len), jnp.bfloat16),
             pltpu.VMEM((2, half, columns), jnp.float32),
             pltpu.VMEM((2, 8, columns), jnp.float32),
+            pltpu.VMEM((2, mp, columns, queries.shape[1]), jnp.bfloat16),
         ],
         in_specs=whole(3),
-        out_specs=whole(3),
+        out_specs=whole(4),
         compiler_params=limit,
         name="own",
     )(*placed(pltpu.VMEM, mine, qall, qcore))
     return pl.pallas_call(
         functools.partial(solve_kernel, mp, zs, per_member, examples),
         out_shape=jax.ShapeDtypeStruct((seq_count, columns), jnp.float32),
-        in_specs=whole(6),
+        in_specs=whole(5),
         out_specs=whole(1)[0],
         compiler_params=limit,
         name="solve",
-    )(*placed(pltpu.VMEM, other, *own_terms, qall, qcore))
+    )(*placed(pltpu.VMEM, other, *own_terms))
 
 
 def power_of_two(n):

time: 37.3 us -> 41.9 us (1.12)
  waiting for transfers between devices: 6.02 us -> 10.2 us
  starting transfers between devices: 21.7 us -> 22.3 us
    ppermute x12, waiting for transfers between devices: 3.51 us -> 9.35 us  [exchange(): lax.ppermute(value, axis, [(i, i ^ k * unit) for i in range(size)])]
    ppermute x3, waiting for transfers between devices: 1.62 us -> 0.03 us  [fast_device(): parts.append(lax.ppermute(sent[k], 'mp', [(i, i ^ k) for i in range(mp)]))]
    ppermute x12, starting transfers between devices: 17 us -> 17.7 us  [exchange(): lax.ppermute(value, axis, [(i, i ^ k * unit) for i in range(size)])]
  transfers between devices with their start and end apart: 17 -> 17, of which waited for: 5 -> 7; matrix products, arithmetic and copies ran while one was open for 0% -> 0% of each run, Pallas kernels for 3% -> 3%
where the time goes in v3:
time: 41.9 us; the launch traced here: 41.8 us
  starting transfers between devices  22.3 us (53%)
  waiting for transfers between devices  10.2 us (24%)
  Pallas kernels  9.04 us (22%)
    ppermute x12, starting transfers between devices, exchange(): lax.ppermute(value, axis, [(i, i ^ k * unit) for i in range(size)])  17.7 us
    ppermute x12, waiting for transfers between devices, exchange(): lax.ppermute(value, axis, [(i, i ^ k * unit) for i in range(size)])  9.35 us
    pallas_call x1, Pallas kernels, fast_device(): pl.pallas_call(functools.partial(project_kernel, vocab_rows, rank, slot_l...  6.26 us
    ppermute x3, starting transfers between devices, fast_device(): parts.append(lax.ppermute(sent[k], 'mp', [(i, i ^ k) for i in range(mp)]))  4.58 us
    pallas_call x1, Pallas kernels, fast_device(): pl.pallas_call(functools.partial(solve_kernel, mp, zs, per_member, exampl...  1.7 us
  transfers between devices with their start and end apart: 17, of which 7 were waited for; matrix products, arithmetic and copies ran while one was open for 0% of the time, Pallas kernels for 3%

profile of v3, /device:TPU:0, one launch (start us, length us, event | category | flops | bytes accessed | tf_op | source)
XLA Modules:
  0.0 41.8 jit_solution(15781264251033880698)
XLA Ops:
  0.0 0.0 copy-start
  0.0 6.3 %project.1 = (f32[256,128]{1,0:T(8,128)S(1)}, f32[256,128]{1,0:T(8,128)S(1)}, f32[256,128]{1,0:T(8,128)S(1)}, f32[256,128]{1,0:T(8,128)S(1)}) custom-call(s32[8,128]{1,0:T(8,128)} %bitcast.37, s32[8]{0:T(128)} %len_any.1, bf16[32,32064]{1,0:T(8,128)(2,1)} %bitcast.23, bf16[1024,1024]{1,0:T(8,128)(2,1)} %grad0_any.1, bf16[1024,1024]{1,0:T(8,128)(2,1)} %bitcast.21, ...), custom_call_target="tpu_custom_call" | custom-call | tf_op jit(solution)/shard_map/project/pallas_call | solution.py:367
  6.3 3.0 %collective-permute-start = (f32[256,128]{1,0:T(8,128)S(1)}, f32[256,128]{1,0:T(8,128)S(1)}, u32[]{:S(2)}, u32[]{:S(2)}) collective-permute-start(f32[256,128]{1,0:T(8,128)S(1)} %get-tuple-element.18), channel_id=1, source_target_pairs={{0,1},{1,0},{2,3},{3,2},{4,5},{5,4},{6,7},{7,6},{8,9},{9,8},{10,11... | collective-permute-start | bytes 393224 | tf_op jit(solution)/shard_map/ppermute | solution.py:401
  9.3 1.5 %collective-permute-start.1 = (f32[256,128]{1,0:T(8,128)S(1)}, f32[256,128]{1,0:T(8,128)S(1)}, u32[]{:S(2)}, u32[]{:S(2)}) collective-permute-start(f32[256,128]{1,0:T(8,128)S(1)} %get-tuple-element.19), channel_id=1, source_target_pairs={{0,2},{1,3},{2,0},{3,1},{4,6},{5,7},{6,4},{7,5},{8,10},{9,11},{10,... | collective-permute-start | bytes 393224 | tf_op jit(solution)/shard_map/ppermute | solution.py:401
  10.9 0.0 collective-permute-start.2
  10.9 0.0 copy-done
  10.9 2.0 %collective-permute-start.10 = (bf16[2,32,256]{2,1,0:T(8,128)(2,1)S(1)}, bf16[2,32,256]{2,1,0:T(8,128)(2,1)S(1)}, u32[]{:S(2)}, u32[]{:S(2)}) collective-permute-start(bf16[2,32,256]{2,1,0:T(8,128)(2,1)S(1)} %bitcast.30), channel_id=1, source_target_pairs={{0,8},{4,12},{8,0},{12,4},{16,24},{20,28},{24,16},{28,20},{1,9},{5... | collective-permute-start | bytes 98312 | tf_op jit(solution)/shard_map/ppermute | solution.py:334
  12.9 2.6 %collective-permute-start.11 = (bf16[2,32,256]{2,1,0:T(8,128)(2,1)S(1)}, bf16[2,32,256]{2,1,0:T(8,128)(2,1)S(1)}, u32[]{:S(2)}, u32[]{:S(2)}) collective-permute-start(bf16[2,32,256]{2,1,0:T(8,128)(2,1)S(1)} %bitcast.31), channel_id=1, source_target_pairs={{0,16},{4,20},{8,24},{12,28},{16,0},{20,4},{24,8},{28,12},{1,17},{... | collective-permute-start | bytes 98312 | tf_op jit(solution)/shard_map/ppermute | solution.py:334
  15.5 0.0 collective-permute-done.refs_1_
  15.5 1.6 %collective-permute-start.12 = (bf16[2,32,256]{2,1,0:T(8,128)(2,1)S(1)}, bf16[2,32,256]{2,1,0:T(8,128)(2,1)S(1)}, u32[]{:S(2)}, u32[]{:S(2)}) collective-permute-start(bf16[2,32,256]{2,1,0:T(8,128)(2,1)S(1)} %bitcast.32), channel_id=1, source_target_pairs={{0,24},{4,28},{8,16},{12,20},{16,8},{20,12},{24,0},{28,4},{1,25},{... | collective-permute-start | bytes 98312 | tf_op jit(solution)/shard_map/ppermute | solution.py:334
  17.1 0.0 collective-permute-done.1.refs_2_
  17.1 0.0 collective-permute-done.2.refs_3_
  17.1 0.4 sketch.1
  17.5 0.0 collective-permute-done.10
  17.5 0.5 %collective-permute-done.11 = bf16[2,32,256]{2,1,0:T(8,128)(2,1)S(1)} collective-permute-done((bf16[2,32,256]{2,1,0:T(8,128)(2,1)S(1)}, bf16[2,32,256]{2,1,0:T(8,128)(2,1)S(1)}, u32[]{:S(2)}, u32[]{:S(2)}) %collective-permute-start.11) | collective-permute-done | bytes 32800 | tf_op jit(solution)/shard_map/ppermute | solution.py:334
  17.9 3.2 %collective-permute-done.12 = bf16[2,32,256]{2,1,0:T(8,128)(2,1)S(1)} collective-permute-done((bf16[2,32,256]{2,1,0:T(8,128)(2,1)S(1)}, bf16[2,32,256]{2,1,0:T(8,128)(2,1)S(1)}, u32[]{:S(2)}, u32[]{:S(2)}) %collective-permute-start.12) | collective-permute-done | bytes 32800 | tf_op jit(solution)/shard_map/ppermute | solution.py:334
  21.2 1.6 %collective-permute-start.13 = (bf16[4,2,32,256]{3,2,1,0:T(8,128)(2,1)S(1)}, bf16[4,2,32,256]{3,2,1,0:T(8,128)(2,1)S(1)}, u32[]{:S(2)}, u32[]{:S(2)}) collective-permute-start(bf16[4,2,32,256]{3,2,1,0:T(8,128)(2,1)S(1)} %get-tuple-element.30), channel_id=1, source_target_pairs={{0,1},{1,0},{2,3},{3,2},{4,5},{5,4},{6,7},{7,6},{8,9},{9,8},{10,11... | collective-permute-start | bytes 393224 | tf_op jit(solution)/shard_map/ppermute | solution.py:334
  22.8 1.5 %collective-permute-start.14 = (bf16[4,2,32,256]{3,2,1,0:T(8,128)(2,1)S(1)}, bf16[4,2,32,256]{3,2,1,0:T(8,128)(2,1)S(1)}, u32[]{:S(2)}, u32[]{:S(2)}) collective-permute-start(bf16[4,2,32,256]{3,2,1,0:T(8,128)(2,1)S(1)} %get-tuple-element.30), channel_id=1, source_target_pairs={{0,2},{1,3},{2,0},{3,1},{4,6},{5,7},{6,4},{7,5},{8,10},{9,11},{10,... | collective-permute-start | bytes 393224 | tf_op jit(solution)/shard_map/ppermute | solution.py:334
  24.3 0.0 collective-permute-start.3
  24.3 2.9 %collective-permute-start.4 = (f32[32,128]{1,0:T(8,128)S(1)}, f32[32,128]{1,0:T(8,128)S(1)}, u32[]{:S(2)}, u32[]{:S(2)}) collective-permute-start(f32[32,128]{1,0:T(8,128)S(1)} %sketch.1), channel_id=1, source_target_pairs={{0,16},{4,20},{8,24},{12,28},{16,0},{20,4},{24,8},{28,12},{1,17},{... | collective-permute-start | bytes 49160 | tf_op jit(solution)/shard_map/ppermute | solution.py:334
  27.2 1.5 %collective-permute-start.5 = (f32[32,128]{1,0:T(8,128)S(1)}, f32[32,128]{1,0:T(8,128)S(1)}, u32[]{:S(2)}, u32[]{:S(2)}) collective-permute-start(f32[32,128]{1,0:T(8,128)S(1)} %sketch.1), channel_id=1, source_target_pairs={{0,24},{4,28},{8,16},{12,20},{16,8},{20,12},{24,0},{28,4},{1,25},{... | collective-permute-start | bytes 49160 | tf_op jit(solution)/shard_map/ppermute | solution.py:334
  28.7 0.0 collective-permute-done.3
  28.7 0.4 %collective-permute-start.15 = (bf16[4,2,32,256]{3,2,1,0:T(8,128)(2,1)S(1)}, bf16[4,2,32,256]{3,2,1,0:T(8,128)(2,1)S(1)}, u32[]{:S(2)}, u32[]{:S(2)}) collective-permute-start(bf16[4,2,32,256]{3,2,1,0:T(8,128)(2,1)S(1)} %get-tuple-element.30), channel_id=1, source_target_pairs={{0,3},{1,2},{2,1},{3,0},{4,7},{5,6},{6,5},{7,4},{8,11},{9,10},{10,... | collective-permute-start | bytes 393224 | tf_op jit(solution)/shard_map/ppermute | solution.py:334
  29.2 0.0 collective-permute-done.4
  29.2 3.6 %collective-permute-done.5 = f32[32,128]{1,0:T(8,128)S(1)} collective-permute-done((f32[32,128]{1,0:T(8,128)S(1)}, f32[32,128]{1,0:T(8,128)S(1)}, u32[]{:S(2)}, u32[]{:S(2)}) %collective-permute-start.5) | collective-permute-done | bytes 16416 | tf_op jit(solution)/shard_map/ppermute | solution.py:334
  32.7 0.1 collective-permute-start.6
  32.8 0.5 %collective-permute-start.7 = (f32[128,128]{1,0:T(8,128)S(1)}, f32[128,128]{1,0:T(8,128)S(1)}, u32[]{:S(2)}, u32[]{:S(2)}) collective-permute-start(f32[128,128]{1,0:T(8,128)S(1)} %pad_maximum_fusion.2), channel_id=1, source_target_pairs={{0,2},{1,3},{2,0},{3,1},{4,6},{5,7},{6,4},{7,5},{8,10},{9,11},{10,... | collective-permute-start | bytes 196616 | tf_op jit(solution)/shard_map/ppermute | solution.py:334
  33.3 0.0 collective-permute-done.13
  33.3 3.0 %collective-permute-start.8 = (f32[128,128]{1,0:T(8,128)S(1)}, f32[128,128]{1,0:T(8,128)S(1)}, u32[]{:S(2)}, u32[]{:S(2)}) collective-permute-start(f32[128,128]{1,0:T(8,128)S(1)} %pad_maximum_fusion.2), channel_id=1, source_target_pairs={{0,3},{1,2},{2,1},{3,0},{4,7},{5,6},{6,5},{7,4},{8,11},{9,10},{10,... | collective-permute-start | bytes 196616 | tf_op jit(solution)/shard_map/ppermute | solution.py:334
  36.3 0.0 collective-permute-done.14
  36.3 0.0 collective-permute-done.15
  36.3 0.1 pad_maximum_fusion.qmine_ref
  36.4 0.1 collective-permute-start.16
  36.5 0.5 %collective-permute-done.6 = f32[128,128]{1,0:T(8,128)S(1)} collective-permute-done((f32[128,128]{1,0:T(8,128)S(1)}, f32[128,128]{1,0:T(8,128)S(1)}, u32[]{:S(2)}, u32[]{:S(2)}) %collective-permute-start.6) | collective-permute-done | bytes 65568 | tf_op jit(solution)/shard_map/ppermute | solution.py:334
  37.0 0.1 collective-permute-done.7
  37.1 1.5 %collective-permute-done.8 = f32[128,128]{1,0:T(8,128)S(1)} collective-permute-done((f32[128,128]{1,0:T(8,128)S(1)}, f32[128,128]{1,0:T(8,128)S(1)}, u32[]{:S(2)}, u32[]{:S(2)}) %collective-permute-start.8) | collective-permute-done | bytes 65568 | tf_op jit(solution)/shard_map/ppermute | solution.py:334
  38.6 0.0 collective-permute-start.9
  38.6 0.0 collective-permute-done.16.qother_ref
  38.6 0.7 %own.1 = (bf16[2,64,1024]{2,1,0:T(8,128)(2,1)S(1)}, f32[2,32,256]{2,1,0:T(8,128)S(1)}, f32[2,8,256]{2,1,0:T(8,128)S(1)}, bf16[2,4,256,256]{3,2,1,0:T(8,128)(2,1)S(1)}) custom-call(f32[512,128]{1,0:T(8,128)S(1)} %constant_dynamic-update-slice_fusion.mine_ref, bf16[4,4,2,32,256]{4,3,2,1,0:T(8,128)(2,1)S(1)} %pad_maximum_fusion.qmine_ref, ...), custom_call_target="tpu_custom_call" | custom-call | tf_op jit(solution)/shard_map/own/pallas_call | solution.py:423
  39.3 0.8 %collective-permute-done.9.other_ref = f32[512,128]{1,0:T(8,128)S(1)} collective-permute-done((f32[512,128]{1,0:T(8,128)S(1)}, f32[512,128]{1,0:T(8,128)S(1)}, u32[]{:S(2)}, u32[]{:S(2)}) %collective-permute-start.9) | collective-permute-done | bytes 262176 | tf_op jit(solution)/shard_map/ppermute | solution.py:339
  40.1 1.7 %solve.1 = f32[8,256]{1,0:T(8,128)} custom-call(f32[512,128]{1,0:T(8,128)S(1)} %collective-permute-done.9.other_ref, bf16[2,64,1024]{2,1,0:T(8,128)(2,1)S(1)} %get-tuple-element.25.both_ref, f32[2,32,256]{2,1,0:T(8,128)S(1)} %get-tuple-element.26.u_ref, f32[2,8,256]{2,1,0:T(8,128)S(1)} %get-tuple-element.27.norm_ref, ...), custom_call_target="tpu_custom_call" | custom-call | tf_op jit(solution)/shard_map/solve/pallas_call | solution.py:436
  (9 shorter events, 0.1 us)
Async XLA Ops:
  0.0 10.9 %copy-start = (bf16[2,256,32]{1,2,0:T(8,128)(2,1)S(1)}, bf16[2,256,32]{1,2,0:T(8,128)(2,1)}, u32[]{:S(2)}) copy-start(bf16[2,256,32]{1,2,0:T(8,128)(2,1)} %param.19) | copy-start | bytes 98308
  6.3 9.2 %collective-permute-start = (f32[256,128]{1,0:T(8,128)S(1)}, f32[256,128]{1,0:T(8,128)S(1)}, u32[]{:S(2)}, u32[]{:S(2)}) collective-permute-start(f32[256,128]{1,0:T(8,128)S(1)} %get-tuple-element.18), channel_id=1, source_target_pairs={{0,1},{1,0},{2,3},{3,2},{4,5},{5,4},{6,7},{7,6},{8,9},{9,8},{10,11... | collective-permute-start | bytes 393224 | tf_op jit(solution)/shard_map/ppermute | solution.py:401
  9.3 7.8 %collective-permute-start.1 = (f32[256,128]{1,0:T(8,128)S(1)}, f32[256,128]{1,0:T(8,128)S(1)}, u32[]{:S(2)}, u32[]{:S(2)}) collective-permute-start(f32[256,128]{1,0:T(8,128)S(1)} %get-tuple-element.19), channel_id=1, source_target_pairs={{0,2},{1,3},{2,0},{3,1},{4,6},{5,7},{6,4},{7,5},{8,10},{9,11},{10,... | collective-permute-start | bytes 393224 | tf_op jit(solution)/shard_map/ppermute | solution.py:401
  10.9 6.2 %collective-permute-start.2 = (f32[256,128]{1,0:T(8,128)S(1)}, f32[256,128]{1,0:T(8,128)S(1)}, u32[]{:S(2)}, u32[]{:S(2)}) collective-permute-start(f32[256,128]{1,0:T(8,128)S(1)} %get-tuple-element.20), channel_id=1, source_target_pairs={{0,3},{1,2},{2,1},{3,0},{4,7},{5,6},{6,5},{7,4},{8,11},{9,10},{10,... | collective-permute-start | bytes 393224 | tf_op jit(solution)/shard_map/ppermute | solution.py:401
  10.9 6.6 %collective-permute-start.10 = (bf16[2,32,256]{2,1,0:T(8,128)(2,1)S(1)}, bf16[2,32,256]{2,1,0:T(8,128)(2,1)S(1)}, u32[]{:S(2)}, u32[]{:S(2)}) collective-permute-start(bf16[2,32,256]{2,1,0:T(8,128)(2,1)S(1)} %bitcast.30), channel_id=1, source_target_pairs={{0,8},{4,12},{8,0},{12,4},{16,24},{20,28},{24,16},{28,20},{1,9},{5... | collective-permute-start | bytes 98312 | tf_op jit(solution)/shard_map/ppermute | solution.py:334
  12.9 5.1 %collective-permute-start.11 = (bf16[2,32,256]{2,1,0:T(8,128)(2,1)S(1)}, bf16[2,32,256]{2,1,0:T(8,128)(2,1)S(1)}, u32[]{:S(2)}, u32[]{:S(2)}) collective-permute-start(bf16[2,32,256]{2,1,0:T(8,128)(2,1)S(1)} %bitcast.31), channel_id=1, source_target_pairs={{0,16},{4,20},{8,24},{12,28},{16,0},{20,4},{24,8},{28,12},{1,17},{... | collective-permute-start | bytes 98312 | tf_op jit(solution)/shard_map/ppermute | solution.py:334
  15.5 5.7 %collective-permute-start.12 = (bf16[2,32,256]{2,1,0:T(8,128)(2,1)S(1)}, bf16[2,32,256]{2,1,0:T(8,128)(2,1)S(1)}, u32[]{:S(2)}, u32[]{:S(2)}) collective-permute-start(bf16[2,32,256]{2,1,0:T(8,128)(2,1)S(1)} %bitcast.32), channel_id=1, source_target_pairs={{0,24},{4,28},{8,16},{12,20},{16,8},{20,12},{24,0},{28,4},{1,25},{... | collective-permute-start | bytes 98312 | tf_op jit(solution)/shard_map/ppermute | solution.py:334
  21.2 12.1 %collective-permute-start.13 = (bf16[4,2,32,256]{3,2,1,0:T(8,128)(2,1)S(1)}, bf16[4,2,32,256]{3,2,1,0:T(8,128)(2,1)S(1)}, u32[]{:S(2)}, u32[]{:S(2)}) collective-permute-start(bf16[4,2,32,256]{3,2,1,0:T(8,128)(2,1)S(1)} %get-tuple-element.30), channel_id=1, source_target_pairs={{0,1},{1,0},{2,3},{3,2},{4,5},{5,4},{6,7},{7,6},{8,9},{9,8},{10,11... | collective-permute-start | bytes 393224 | tf_op jit(solution)/shard_map/ppermute | solution.py:334
  22.8 13.5 %collective-permute-start.14 = (bf16[4,2,32,256]{3,2,1,0:T(8,128)(2,1)S(1)}, bf16[4,2,32,256]{3,2,1,0:T(8,128)(2,1)S(1)}, u32[]{:S(2)}, u32[]{:S(2)}) collective-permute-start(bf16[4,2,32,256]{3,2,1,0:T(8,128)(2,1)S(1)} %get-tuple-element.30), channel_id=1, source_target_pairs={{0,2},{1,3},{2,0},{3,1},{4,6},{5,7},{6,4},{7,5},{8,10},{9,11},{10,... | collective-permute-start | bytes 393224 | tf_op jit(solution)/shard_map/ppermute | solution.py:334
  24.3 4.4 %collective-permute-start.3 = (f32[32,128]{1,0:T(8,128)S(1)}, f32[32,128]{1,0:T(8,128)S(1)}, u32[]{:S(2)}, u32[]{:S(2)}) collective-permute-start(f32[32,128]{1,0:T(8,128)S(1)} %sketch.1), channel_id=1, source_target_pairs={{0,8},{4,12},{8,0},{12,4},{16,24},{20,28},{24,16},{28,20},{1,9},{5... | collective-permute-start | bytes 49160 | tf_op jit(solution)/shard_map/ppermute | solution.py:334
  24.3 4.8 %collective-permute-start.4 = (f32[32,128]{1,0:T(8,128)S(1)}, f32[32,128]{1,0:T(8,128)S(1)}, u32[]{:S(2)}, u32[]{:S(2)}) collective-permute-start(f32[32,128]{1,0:T(8,128)S(1)} %sketch.1), channel_id=1, source_target_pairs={{0,16},{4,20},{8,24},{12,28},{16,0},{20,4},{24,8},{28,12},{1,17},{... | collective-permute-start | bytes 49160 | tf_op jit(solution)/shard_map/ppermute | solution.py:334
  27.2 5.5 %collective-permute-start.5 = (f32[32,128]{1,0:T(8,128)S(1)}, f32[32,128]{1,0:T(8,128)S(1)}, u32[]{:S(2)}, u32[]{:S(2)}) collective-permute-start(f32[32,128]{1,0:T(8,128)S(1)} %sketch.1), channel_id=1, source_target_pairs={{0,24},{4,28},{8,16},{12,20},{16,8},{20,12},{24,0},{28,4},{1,25},{... | collective-permute-start | bytes 49160 | tf_op jit(solution)/shard_map/ppermute | solution.py:334
  28.7 7.6 %collective-permute-start.15 = (bf16[4,2,32,256]{3,2,1,0:T(8,128)(2,1)S(1)}, bf16[4,2,32,256]{3,2,1,0:T(8,128)(2,1)S(1)}, u32[]{:S(2)}, u32[]{:S(2)}) collective-permute-start(bf16[4,2,32,256]{3,2,1,0:T(8,128)(2,1)S(1)} %get-tuple-element.30), channel_id=1, source_target_pairs={{0,3},{1,2},{2,1},{3,0},{4,7},{5,6},{6,5},{7,4},{8,11},{9,10},{10,... | collective-permute-start | bytes 393224 | tf_op jit(solution)/shard_map/ppermute | solution.py:334
  32.7 4.3 %collective-permute-start.6 = (f32[128,128]{1,0:T(8,128)S(1)}, f32[128,128]{1,0:T(8,128)S(1)}, u32[]{:S(2)}, u32[]{:S(2)}) collective-permute-start(f32[128,128]{1,0:T(8,128)S(1)} %pad_maximum_fusion.2), channel_id=1, source_target_pairs={{0,1},{1,0},{2,3},{3,2},{4,5},{5,4},{6,7},{7,6},{8,9},{9,8},{10,11... | collective-permute-start | bytes 196616 | tf_op jit(solution)/shard_map/ppermute | solution.py:334
  32.8 4.3 %collective-permute-start.7 = (f32[128,128]{1,0:T(8,128)S(1)}, f32[128,128]{1,0:T(8,128)S(1)}, u32[]{:S(2)}, u32[]{:S(2)}) collective-permute-start(f32[128,128]{1,0:T(8,128)S(1)} %pad_maximum_fusion.2), channel_id=1, source_target_pairs={{0,2},{1,3},{2,0},{3,1},{4,6},{5,7},{6,4},{7,5},{8,10},{9,11},{10,... | collective-permute-start | bytes 196616 | tf_op jit(solution)/shard_map/ppermute | solution.py:334
  33.3 5.2 %collective-permute-start.8 = (f32[128,128]{1,0:T(8,128)S(1)}, f32[128,128]{1,0:T(8,128)S(1)}, u32[]{:S(2)}, u32[]{:S(2)}) collective-permute-start(f32[128,128]{1,0:T(8,128)S(1)} %pad_maximum_fusion.2), channel_id=1, source_target_pairs={{0,3},{1,2},{2,1},{3,0},{4,7},{5,6},{6,5},{7,4},{8,11},{9,10},{10,... | collective-permute-start | bytes 196616 | tf_op jit(solution)/shard_map/ppermute | solution.py:334
  36.4 2.2 %collective-permute-start.16 = (bf16[4,4,2,32,256]{4,3,2,1,0:T(8,128)(2,1)S(1)}, bf16[4,4,2,32,256]{4,3,2,1,0:T(8,128)(2,1)S(1)}, u32[]{:S(2)}, u32[]{:S(2)}) collective-permute-start(bf16[4,4,2,32,256]{4,3,2,1,0:T(8,128)(2,1)S(1)} %pad_maximum_fusion.qmine_ref), channel_id=1, source_target_pairs={{0,4},{4,0},{8,12},{12,8},{16,20},{20,16},{24,28},{28,24},{1,5},{5... | collective-permute-start | bytes 1572872 | tf_op jit(solution)/shard_map/ppermute | solution.py:339
  38.6 1.5 %collective-permute-start.9 = (f32[512,128]{1,0:T(8,128)S(1)}, f32[512,128]{1,0:T(8,128)S(1)}, u32[]{:S(2)}, u32[]{:S(2)}) collective-permute-start(f32[512,128]{1,0:T(8,128)S(1)} %constant_dynamic-update-slice_fusion.mine_ref), channel_id=1, source_target_pairs={{0,4},{4,0},{8,12},{12,8},{16,20},{20,16},{24,28},{28,24},{1,5},{5... | collective-permute-start | bytes 786440 | tf_op jit(solution)/shard_map/ppermute | solution.py:339

commit v4 on v3

--- a/solution.py
+++ b/solution.py
@@ -10,7 +10,7 @@
 
 ITERS = 2
 LANES = 128
-AHEAD = 1
+AHEAD = 2
 
 damping = 0.01
 epsilon = 1e-06
@@ -114,10 +114,11 @@
     basis2_any,
     *refs,
 ):
-    out_refs = refs[:-9]
-    ids_ref, len_ref, table_ref, wide_ref, weight_ref, place_ref, scalar_ref = refs[-9:-2]
-    small_sem, wide_sem = refs[-2:]
-    members = len(out_refs)
+    out_refs = refs[:-11]
+    table_ref, own_ref, weight_ref, place_ref, share_ref, own_ids_ref = refs[-11:-5]
+    ids_ref, len_ref, wide_ref, scalar_ref, sems = refs[-5:]
+    small_sem, wide_sem = sems.at[pl.ds(0, 6)], sems.at[pl.ds(6, 3 * (len(out_refs) + 1))]
+    members = len(out_refs) + 1
     me = lax.axis_index("mp").astype(jnp.int32)
     offset = me * vocab_rows
     main = vocab_rows // LANES
@@ -128,7 +129,8 @@
 
     def wide_copy(k, r):
         source = (grad0_any, grad1_any, input1_any)[k]
-        return pltpu.make_async_copy(source.at[rows_of(r), :], wide_ref.at[k, rows_of(r), :], wide_sem.at[k, r])
+        target = own_ref.at[k] if isinstance(r, int) and r == 0 else wide_ref.at[k, rows_of(r), :]
+        return pltpu.make_async_copy(source.at[rows_of(r), :], target, wide_sem.at[k * members + r])
 
     ids_copy = pltpu.make_async_copy(ids_any, ids_ref, small_sem.at[0])
     len_copy = pltpu.make_async_copy(len_any, len_ref, small_sem.at[5])
@@ -142,7 +144,7 @@
     len_copy.start()
     for copy in basis_copies:
         copy.start()
-    for r in range(AHEAD):
+    for r in range(1, 1 + AHEAD):
         for k in range(3):
             wide_copy(k, r).start()
     for k in range(3):
@@ -160,14 +162,9 @@
     for copy in basis_copies:
         copy.wait()
     table_copy.wait()
-    for r in range(AHEAD, members):
+    for r in [*range(1 + AHEAD, members), 0]:
         for k in range(3):
             wide_copy(k, r).start()
-
-    lane = lax.broadcasted_iota(jnp.int32, (rank, LANES), 1)
-    row = lax.broadcasted_iota(jnp.int32, (slot_len, LANES), 0)
-    column = lax.broadcasted_iota(jnp.int32, (slot_len, LANES), 1)
-    tail = vocab_rows - main * LANES
 
     def step(r, _):
         for k in range(3):
@@ -175,35 +172,88 @@
         values = []
         for s in range(per_member):
             seq = (me ^ r) * per_member + s
-            found = jnp.zeros((rank, LANES), jnp.float32)
-            for t in range(slot_len):
-                word = scalar_ref[seq, t]
-                block = table_ref[:, pl.ds(pl.multiple_of(word & -LANES, LANES), LANES)].astype(jnp.float32)
-                found = jnp.where(lane == t, pltpu.roll(block, word & (LANES - 1), 1), found)
-            mine = ids_ref[pl.ds(seq, 1), :] - offset
-            found = jnp.where((mine >= 0) & (mine < main * LANES), found, 0.0)
-            if tail:
-                sub = lax.broadcasted_iota(jnp.int32, (tail, LANES), 0)
-                pick = jnp.where(mine - main * LANES == sub, 1.0, 0.0).astype(jnp.bfloat16)
-                found += jnp.dot(table_ref[:, main * LANES :], pick, preferred_element_type=jnp.float32)
             rows = pl.ds(pl.multiple_of(seq * slot_len, slot_len), slot_len)
-            total = contract_last(wide_ref[0, rows, :], weight_ref[0])
-            total += contract_last(wide_ref[1, rows, :], weight_ref[1])
-            total += contract_last(wide_ref[2, rows, :], weight_ref[2])
-            live = len_ref[seq]
-            share = jnp.where(row < live, 1.0 / jnp.full(row.shape, live, jnp.int32).astype(jnp.float32), 0.0)
-            spread = jnp.concatenate([jnp.zeros((3 * rank, LANES), jnp.float32), found], axis=0)
-            values.append(total * jnp.where(column < 2 * rank, share, 1.0) + spread.T)
+            wide = [wide_ref[k, rows, :] for k in range(3)]
+            found = look_up(scalar_ref, seq, ids_ref[pl.ds(seq, 1), :] - offset, table_ref, vocab_rows)
+            position = lax.broadcasted_iota(jnp.int32, (slot_len, LANES), 0)
+            values.append(combine(products(wide, weight_ref), found, shares(position, len_ref[seq])))
         for place, out_ref in enumerate(out_refs):
 
-            @pl.when(r == place)
+            @pl.when(r == place + 1)
             def _():
                 for s in range(per_member):
                     out_ref[s * slot_len : (s + 1) * slot_len, :] = values[s]
 
         return 0
 
-    lax.fori_loop(0, members, step, 0)
+    lax.fori_loop(1, members, step, 0)
+    for s in range(per_member):
+        position = lax.broadcasted_iota(jnp.int32, (slot_len, LANES), 0)
+        share_ref[s * slot_len : (s + 1) * slot_len, :] = shares(position, len_ref[me * per_member + s])
+    own_ids_ref[...] = ids_ref[...] - offset
+    for k in range(3):
+        wide_copy(k, 0).wait()
+
+
+def look_up(scalar_ref, seq, local, table_ref, vocab_rows):
+    rank = table_ref.shape[0]
+    main = vocab_rows // LANES
+    tail = vocab_rows - main * LANES
+    lane = lax.broadcasted_iota(jnp.int32, (rank, LANES), 1)
+    found = jnp.zeros((rank, LANES), jnp.float32)
+    for t in range(LANES):
+        word = scalar_ref[seq, t]
+        block = table_ref[:, pl.ds(pl.multiple_of(word & -LANES, LANES), LANES)].astype(jnp.float32)
+        found = jnp.where(lane == t, pltpu.roll(block, word & (LANES - 1), 1), found)
+    found = jnp.where((local >= 0) & (local < main * LANES), found, 0.0)
+    if tail:
+        sub = lax.broadcasted_iota(jnp.int32, (tail, LANES), 0)
+        pick = jnp.where(local - main * LANES == sub, 1.0, 0.0).astype(jnp.bfloat16)
+        found += jnp.dot(table_ref[:, main * LANES :], pick, preferred_element_type=jnp.float32)
+    return found
+
+
+def shares(position, live):
+    return jnp.where(position < live, 1.0 / jnp.full(position.shape, live, jnp.int32).astype(jnp.float32), 0.0)
+
+
+def products(wide, weight_ref):
+    total = contract_last(wide[0], weight_ref[0])
+    total += contract_last(wide[1], weight_ref[1])
+    return total + contract_last(wide[2], weight_ref[2])
+
+
+def combine(total, found, share):
+    rank = found.shape[0]
+    column = lax.broadcasted_iota(jnp.int32, total.shape, 1)
+    spread = jnp.concatenate([jnp.zeros((3 * rank, LANES), jnp.float32), found], axis=0)
+    return total * jnp.where(column < 2 * rank, share, 1.0) + spread.T
+
+
+def own_block_kernel(
+    vocab_rows,
+    slot_len,
+    per_member,
+    table_ref,
+    wide_ref,
+    weight_ref,
+    place_ref,
+    share_ref,
+    local_ref,
+    out_ref,
+    scalar_ref,
+    copied,
+):
+    me = lax.axis_index("mp").astype(jnp.int32)
+    copy = pltpu.make_async_copy(place_ref, scalar_ref, copied)
+    copy.start()
+    total = products([wide_ref[k] for k in range(3)], weight_ref)
+    copy.wait()
+    for s in range(per_member):
+        seq = me * per_member + s
+        rows = slice(s * slot_len, (s + 1) * slot_len)
+        found = look_up(scalar_ref, seq, local_ref[pl.ds(seq, 1), :], table_ref, vocab_rows)
+        out_ref[rows, :] = combine(total[rows], found, share_ref[rows, :])
 
 
 def split(value):
@@ -366,19 +416,23 @@
     block = per_member * slot_len
     sent = pl.pallas_call(
         functools.partial(project_kernel, vocab_rows, rank, slot_len, per_member),
-        out_shape=[pltpu.VMEM((block, LANES), jnp.float32)] * mp,
+        out_shape=[pltpu.VMEM((block, LANES), jnp.float32)] * (mp - 1)
+        + [
+            pltpu.VMEM((rank, vocab_rows), jnp.bfloat16),
+            pltpu.VMEM((3, block, features), jnp.bfloat16),
+            pltpu.VMEM((3, LANES, features), jnp.bfloat16),
+            pltpu.VMEM((seq_count, slot_len), jnp.int32),
+            pltpu.VMEM((block, LANES), jnp.float32),
+            pltpu.VMEM((seq_count, slot_len), jnp.int32),
+        ],
         in_specs=[pl.BlockSpec(memory_space=pl.ANY)] * 9,
-        out_specs=whole(mp),
+        out_specs=whole(mp + 5),
         scratch_shapes=[
             pltpu.VMEM((seq_count, slot_len), jnp.int32),
             pltpu.SMEM((seq_count,), jnp.int32),
-            pltpu.VMEM((rank, vocab_rows), jnp.bfloat16),
             pltpu.VMEM((3, token_count, features), jnp.bfloat16),
-            pltpu.VMEM((3, LANES, features), jnp.bfloat16),
-            pltpu.VMEM((seq_count, slot_len), jnp.int32),
             pltpu.SMEM((seq_count, slot_len), jnp.int32),
-            pltpu.SemaphoreType.DMA((6,)),
-            pltpu.SemaphoreType.DMA((3, mp)),
+            pltpu.SemaphoreType.DMA((6 + 3 * mp,)),
         ],
         compiler_params=limit,
         name="project",
@@ -396,9 +450,18 @@
             input_basis[0].T,
         )
     )
-    parts = [sent[0]]
+    mine = pl.pallas_call(
+        functools.partial(own_block_kernel, vocab_rows, slot_len, per_member),
+        out_shape=pltpu.VMEM((block, LANES), jnp.float32),
+        in_specs=whole(6),
+        out_specs=whole(1)[0],
+        scratch_shapes=[pltpu.SMEM((seq_count, slot_len), jnp.int32), pltpu.SemaphoreType.DMA],
+        compiler_params=limit,
+        name="own_block",
+    )(*placed(pltpu.VMEM, *sent[mp - 1 :]))
+    parts = [mine]
     for k in range(1, mp):
-        parts.append(lax.ppermute(sent[k], "mp", [(i, i ^ k) for i in range(mp)]))
+        parts.append(lax.ppermute(sent[k - 1], "mp", [(i, i ^ k) for i in range(mp)]))
 
     pieces = exchange(queries.transpose(0, 2, 1), "dp", zs, 2)
     rows = per_member * 2 * 8

time: 41.9 us -> 40.9 us (0.976)
  waiting for transfers between devices: 10.2 us -> 8.63 us
  Pallas kernels: 9.04 us -> 9.49 us
    ppermute x12, waiting for transfers between devices: 9.35 us -> 7.82 us  [exchange(): lax.ppermute(value, axis, [(i, i ^ k * unit) for i in range(size)])]
    pallas_call x0 -> x1, Pallas kernels: none -> 1.48 us  [fast_device(): pl.pallas_call(functools.partial(own_block_kernel, vocab_rows, slot_len,...]
    pallas_call x1, Pallas kernels: 6.26 us -> 5.22 us  [fast_device(): pl.pallas_call(functools.partial(project_kernel, vocab_rows, rank, slot_l...]
  transfers between devices with their start and end apart: 17 -> 17, of which waited for: 7 -> 6; matrix products, arithmetic and copies ran while one was open for 0% -> 0% of each run, Pallas kernels for 3% -> 6%
where the time goes in v4:
time: 40.9 us; the launch traced here: 40.7 us
  starting transfers between devices  22.4 us (55%)
  Pallas kernels  9.49 us (23%)
  waiting for transfers between devices  8.63 us (21%)
    ppermute x12, starting transfers between devices, exchange(): lax.ppermute(value, axis, [(i, i ^ k * unit) for i in range(size)])  17.7 us
    ppermute x12, waiting for transfers between devices, exchange(): lax.ppermute(value, axis, [(i, i ^ k * unit) for i in range(size)])  7.82 us
    pallas_call x1, Pallas kernels, fast_device(): pl.pallas_call(functools.partial(project_kernel, vocab_rows, rank, slot_l...  5.22 us
    ppermute x3, starting transfers between devices, fast_device(): lax.ppermute(sent[k - 1], 'mp', [(i, i ^ k) for i in range(mp)])  4.58 us
    pallas_call x1, Pallas kernels, fast_device(): pl.pallas_call(functools.partial(solve_kernel, mp, zs, per_member, exampl...  1.7 us
    pallas_call x1, Pallas kernels, fast_device(): pl.pallas_call(functools.partial(own_block_kernel, vocab_rows, slot_len,...  1.48 us
  transfers between devices with their start and end apart: 17, of which 6 were waited for; matrix products, arithmetic and copies ran while one was open for 0% of the time, Pallas kernels for 6%

profile of v4, /device:TPU:0, one launch (start us, length us, event | category | flops | bytes accessed | tf_op | source)
XLA Modules:
  0.0 40.7 jit_solution(17322791605756743782)
XLA Ops:
  0.0 0.0 copy-start
  0.0 5.2 %project.1 = (f32[256,128]{1,0:T(8,128)S(1)}, f32[256,128]{1,0:T(8,128)S(1)}, f32[256,128]{1,0:T(8,128)S(1)}, bf16[32,32064]{1,0:T(8,128)(2,1)S(1)}, bf16[3,256,...) custom-call(s32[8,128]{1,0:T(8,128)} %bitcast.37, ...), custom_call_target="tpu_custom_call" | custom-call | tf_op jit(solution)/shard_map/project/pallas_call | solution.py:417
  5.2 3.0 %collective-permute-start = (f32[256,128]{1,0:T(8,128)S(1)}, f32[256,128]{1,0:T(8,128)S(1)}, u32[]{:S(2)}, u32[]{:S(2)}) collective-permute-start(f32[256,128]{1,0:T(8,128)S(1)} %get-tuple-element.28), channel_id=1, source_target_pairs={{0,1},{1,0},{2,3},{3,2},{4,5},{5,4},{6,7},{7,6},{8,9},{9,8},{10,11... | collective-permute-start | bytes 393224 | tf_op jit(solution)/shard_map/ppermute | solution.py:464
  8.3 1.5 %collective-permute-start.1 = (f32[256,128]{1,0:T(8,128)S(1)}, f32[256,128]{1,0:T(8,128)S(1)}, u32[]{:S(2)}, u32[]{:S(2)}) collective-permute-start(f32[256,128]{1,0:T(8,128)S(1)} %get-tuple-element.29), channel_id=1, source_target_pairs={{0,2},{1,3},{2,0},{3,1},{4,6},{5,7},{6,4},{7,5},{8,10},{9,11},{10,... | collective-permute-start | bytes 393224 | tf_op jit(solution)/shard_map/ppermute | solution.py:464
  9.8 0.0 collective-permute-start.2
  9.8 0.0 copy-done
  9.8 2.0 %collective-permute-start.10 = (bf16[2,32,256]{2,1,0:T(8,128)(2,1)S(1)}, bf16[2,32,256]{2,1,0:T(8,128)(2,1)S(1)}, u32[]{:S(2)}, u32[]{:S(2)}) collective-permute-start(bf16[2,32,256]{2,1,0:T(8,128)(2,1)S(1)} %bitcast.30), channel_id=1, source_target_pairs={{0,8},{4,12},{8,0},{12,4},{16,24},{20,28},{24,16},{28,20},{1,9},{5... | collective-permute-start | bytes 98312 | tf_op jit(solution)/shard_map/ppermute | solution.py:384
  11.8 2.6 %collective-permute-start.11 = (bf16[2,32,256]{2,1,0:T(8,128)(2,1)S(1)}, bf16[2,32,256]{2,1,0:T(8,128)(2,1)S(1)}, u32[]{:S(2)}, u32[]{:S(2)}) collective-permute-start(bf16[2,32,256]{2,1,0:T(8,128)(2,1)S(1)} %bitcast.31), channel_id=1, source_target_pairs={{0,16},{4,20},{8,24},{12,28},{16,0},{20,4},{24,8},{28,12},{1,17},{... | collective-permute-start | bytes 98312 | tf_op jit(solution)/shard_map/ppermute | solution.py:384
  14.5 0.0 collective-permute-done.refs_1_
  14.5 1.6 %collective-permute-start.12 = (bf16[2,32,256]{2,1,0:T(8,128)(2,1)S(1)}, bf16[2,32,256]{2,1,0:T(8,128)(2,1)S(1)}, u32[]{:S(2)}, u32[]{:S(2)}) collective-permute-start(bf16[2,32,256]{2,1,0:T(8,128)(2,1)S(1)} %bitcast.32), channel_id=1, source_target_pairs={{0,24},{4,28},{8,16},{12,20},{16,8},{20,12},{24,0},{28,4},{1,25},{... | collective-permute-start | bytes 98312 | tf_op jit(solution)/shard_map/ppermute | solution.py:384
  16.1 1.5 %own_block.1.refs_0_ = f32[256,128]{1,0:T(8,128)S(1)} custom-call(bf16[32,32064]{1,0:T(8,128)(2,1)S(1)} %get-tuple-element.22.table_ref, bf16[3,256,1024]{2,1,0:T(8,128)(2,1)S(1)} %get-tuple-element.23.wide_ref, bf16[3,128,1024]{2,1,0:T(8,128)(2,1)S(1)} %get-tuple-element.24.weight_ref, s32[8,128]{1,0:T(8,128)S(1)} %get-tuple-element.25.place_ref, ...), custom_call_target="tpu_custom_call" | custom-call | tf_op jit(solution)/shard_map/own_block/pallas_call | solution.py:453
  17.5 0.0 collective-permute-done.1.refs_2_
  17.6 0.0 collective-permute-done.2.refs_3_
  17.6 0.4 sketch.1
  18.0 0.0 collective-permute-done.10
  18.0 0.0 collective-permute-done.11
  18.0 2.2 %collective-permute-done.12 = bf16[2,32,256]{2,1,0:T(8,128)(2,1)S(1)} collective-permute-done((bf16[2,32,256]{2,1,0:T(8,128)(2,1)S(1)}, bf16[2,32,256]{2,1,0:T(8,128)(2,1)S(1)}, u32[]{:S(2)}, u32[]{:S(2)}) %collective-permute-start.12) | collective-permute-done | bytes 32800 | tf_op jit(solution)/shard_map/ppermute | solution.py:384
  20.2 1.5 %collective-permute-start.13 = (bf16[4,2,32,256]{3,2,1,0:T(8,128)(2,1)S(1)}, bf16[4,2,32,256]{3,2,1,0:T(8,128)(2,1)S(1)}, u32[]{:S(2)}, u32[]{:S(2)}) collective-permute-start(bf16[4,2,32,256]{3,2,1,0:T(8,128)(2,1)S(1)} %get-tuple-element.40), channel_id=1, source_target_pairs={{0,1},{1,0},{2,3},{3,2},{4,5},{5,4},{6,7},{7,6},{8,9},{9,8},{10,11... | collective-permute-start | bytes 393224 | tf_op jit(solution)/shard_map/ppermute | solution.py:384
  21.7 1.5 %collective-permute-start.14 = (bf16[4,2,32,256]{3,2,1,0:T(8,128)(2,1)S(1)}, bf16[4,2,32,256]{3,2,1,0:T(8,128)(2,1)S(1)}, u32[]{:S(2)}, u32[]{:S(2)}) collective-permute-start(bf16[4,2,32,256]{3,2,1,0:T(8,128)(2,1)S(1)} %get-tuple-element.40), channel_id=1, source_target_pairs={{0,2},{1,3},{2,0},{3,1},{4,6},{5,7},{6,4},{7,5},{8,10},{9,11},{10,... | collective-permute-start | bytes 393224 | tf_op jit(solution)/shard_map/ppermute | solution.py:384
  23.2 0.0 collective-permute-start.3
  23.2 2.9 %collective-permute-start.4 = (f32[32,128]{1,0:T(8,128)S(1)}, f32[32,128]{1,0:T(8,128)S(1)}, u32[]{:S(2)}, u32[]{:S(2)}) collective-permute-start(f32[32,128]{1,0:T(8,128)S(1)} %sketch.1), channel_id=1, source_target_pairs={{0,16},{4,20},{8,24},{12,28},{16,0},{20,4},{24,8},{28,12},{1,17},{... | collective-permute-start | bytes 49160 | tf_op jit(solution)/shard_map/ppermute | solution.py:384
  26.1 1.5 %collective-permute-start.5 = (f32[32,128]{1,0:T(8,128)S(1)}, f32[32,128]{1,0:T(8,128)S(1)}, u32[]{:S(2)}, u32[]{:S(2)}) collective-permute-start(f32[32,128]{1,0:T(8,128)S(1)} %sketch.1), channel_id=1, source_target_pairs={{0,24},{4,28},{8,16},{12,20},{16,8},{20,12},{24,0},{28,4},{1,25},{... | collective-permute-start | bytes 49160 | tf_op jit(solution)/shard_map/ppermute | solution.py:384
  27.6 0.0 collective-permute-done.3
  27.6 0.5 %collective-permute-start.15 = (bf16[4,2,32,256]{3,2,1,0:T(8,128)(2,1)S(1)}, bf16[4,2,32,256]{3,2,1,0:T(8,128)(2,1)S(1)}, u32[]{:S(2)}, u32[]{:S(2)}) collective-permute-start(bf16[4,2,32,256]{3,2,1,0:T(8,128)(2,1)S(1)} %get-tuple-element.40), channel_id=1, source_target_pairs={{0,3},{1,2},{2,1},{3,0},{4,7},{5,6},{6,5},{7,4},{8,11},{9,10},{10,... | collective-permute-start | bytes 393224 | tf_op jit(solution)/shard_map/ppermute | solution.py:384
  28.1 0.0 collective-permute-done.4
  28.2 3.5 %collective-permute-done.5 = f32[32,128]{1,0:T(8,128)S(1)} collective-permute-done((f32[32,128]{1,0:T(8,128)S(1)}, f32[32,128]{1,0:T(8,128)S(1)}, u32[]{:S(2)}, u32[]{:S(2)}) %collective-permute-start.5) | collective-permute-done | bytes 16416 | tf_op jit(solution)/shard_map/ppermute | solution.py:384
  31.6 0.1 collective-permute-start.6
  31.7 0.5 %collective-permute-start.7 = (f32[128,128]{1,0:T(8,128)S(1)}, f32[128,128]{1,0:T(8,128)S(1)}, u32[]{:S(2)}, u32[]{:S(2)}) collective-permute-start(f32[128,128]{1,0:T(8,128)S(1)} %pad_maximum_fusion.2), channel_id=1, source_target_pairs={{0,2},{1,3},{2,0},{3,1},{4,6},{5,7},{6,4},{7,5},{8,10},{9,11},{10,... | collective-permute-start | bytes 196616 | tf_op jit(solution)/shard_map/ppermute | solution.py:384
  32.3 0.0 collective-permute-done.13
  32.3 2.9 %collective-permute-start.8 = (f32[128,128]{1,0:T(8,128)S(1)}, f32[128,128]{1,0:T(8,128)S(1)}, u32[]{:S(2)}, u32[]{:S(2)}) collective-permute-start(f32[128,128]{1,0:T(8,128)S(1)} %pad_maximum_fusion.2), channel_id=1, source_target_pairs={{0,3},{1,2},{2,1},{3,0},{4,7},{5,6},{6,5},{7,4},{8,11},{9,10},{10,... | collective-permute-start | bytes 196616 | tf_op jit(solution)/shard_map/ppermute | solution.py:384
  35.2 0.0 collective-permute-done.14
  35.2 0.0 collective-permute-done.15
  35.2 0.1 pad_maximum_fusion.qmine_ref
  35.3 0.1 collective-permute-start.16
  35.4 0.5 %collective-permute-done.6 = f32[128,128]{1,0:T(8,128)S(1)} collective-permute-done((f32[128,128]{1,0:T(8,128)S(1)}, f32[128,128]{1,0:T(8,128)S(1)}, u32[]{:S(2)}, u32[]{:S(2)}) %collective-permute-start.6) | collective-permute-done | bytes 65568 | tf_op jit(solution)/shard_map/ppermute | solution.py:384
  35.9 0.1 collective-permute-done.7
  36.0 1.5 %collective-permute-done.8 = f32[128,128]{1,0:T(8,128)S(1)} collective-permute-done((f32[128,128]{1,0:T(8,128)S(1)}, f32[128,128]{1,0:T(8,128)S(1)}, u32[]{:S(2)}, u32[]{:S(2)}) %collective-permute-start.8) | collective-permute-done | bytes 65568 | tf_op jit(solution)/shard_map/ppermute | solution.py:384
  37.5 0.0 collective-permute-start.9
  37.5 0.0 collective-permute-done.16.qother_ref
  37.5 0.7 %own.1 = (bf16[2,64,1024]{2,1,0:T(8,128)(2,1)S(1)}, f32[2,32,256]{2,1,0:T(8,128)S(1)}, f32[2,8,256]{2,1,0:T(8,128)S(1)}, bf16[2,4,256,256]{3,2,1,0:T(8,128)(2,1)S(1)}) custom-call(f32[512,128]{1,0:T(8,128)S(1)} %constant_dynamic-update-slice_fusion.mine_ref, bf16[4,4,2,32,256]{4,3,2,1,0:T(8,128)(2,1)S(1)} %pad_maximum_fusion.qmine_ref, ...), custom_call_target="tpu_custom_call" | custom-call | tf_op jit(solution)/shard_map/own/pallas_call | solution.py:486
  38.2 0.8 %collective-permute-done.9.other_ref = f32[512,128]{1,0:T(8,128)S(1)} collective-permute-done((f32[512,128]{1,0:T(8,128)S(1)}, f32[512,128]{1,0:T(8,128)S(1)}, u32[]{:S(2)}, u32[]{:S(2)}) %collective-permute-start.9) | collective-permute-done | bytes 262176 | tf_op jit(solution)/shard_map/ppermute | solution.py:389
  39.0 1.7 %solve.1 = f32[8,256]{1,0:T(8,128)} custom-call(f32[512,128]{1,0:T(8,128)S(1)} %collective-permute-done.9.other_ref, bf16[2,64,1024]{2,1,0:T(8,128)(2,1)S(1)} %get-tuple-element.35.both_ref, f32[2,32,256]{2,1,0:T(8,128)S(1)} %get-tuple-element.36.u_ref, f32[2,8,256]{2,1,0:T(8,128)S(1)} %get-tuple-element.37.norm_ref, ...), custom_call_target="tpu_custom_call" | custom-call | tf_op jit(solution)/shard_map/solve/pallas_call | solution.py:499
  (9 shorter events, 0.1 us)
Async XLA Ops:
  0.0 9.8 %copy-start = (bf16[2,256,32]{1,2,0:T(8,128)(2,1)S(1)}, bf16[2,256,32]{1,2,0:T(8,128)(2,1)}, u32[]{:S(2)}) copy-start(bf16[2,256,32]{1,2,0:T(8,128)(2,1)} %param.19) | copy-start | bytes 98308
  5.2 9.2 %collective-permute-start = (f32[256,128]{1,0:T(8,128)S(1)}, f32[256,128]{1,0:T(8,128)S(1)}, u32[]{:S(2)}, u32[]{:S(2)}) collective-permute-start(f32[256,128]{1,0:T(8,128)S(1)} %get-tuple-element.28), channel_id=1, source_target_pairs={{0,1},{1,0},{2,3},{3,2},{4,5},{5,4},{6,7},{7,6},{8,9},{9,8},{10,11... | collective-permute-start | bytes 393224 | tf_op jit(solution)/shard_map/ppermute | solution.py:464
  8.3 9.3 %collective-permute-start.1 = (f32[256,128]{1,0:T(8,128)S(1)}, f32[256,128]{1,0:T(8,128)S(1)}, u32[]{:S(2)}, u32[]{:S(2)}) collective-permute-start(f32[256,128]{1,0:T(8,128)S(1)} %get-tuple-element.29), channel_id=1, source_target_pairs={{0,2},{1,3},{2,0},{3,1},{4,6},{5,7},{6,4},{7,5},{8,10},{9,11},{10,... | collective-permute-start | bytes 393224 | tf_op jit(solution)/shard_map/ppermute | solution.py:464
  9.8 7.8 %collective-permute-start.2 = (f32[256,128]{1,0:T(8,128)S(1)}, f32[256,128]{1,0:T(8,128)S(1)}, u32[]{:S(2)}, u32[]{:S(2)}) collective-permute-start(f32[256,128]{1,0:T(8,128)S(1)} %get-tuple-element.30), channel_id=1, source_target_pairs={{0,3},{1,2},{2,1},{3,0},{4,7},{5,6},{6,5},{7,4},{8,11},{9,10},{10,... | collective-permute-start | bytes 393224 | tf_op jit(solution)/shard_map/ppermute | solution.py:464
  9.8 8.1 %collective-permute-start.10 = (bf16[2,32,256]{2,1,0:T(8,128)(2,1)S(1)}, bf16[2,32,256]{2,1,0:T(8,128)(2,1)S(1)}, u32[]{:S(2)}, u32[]{:S(2)}) collective-permute-start(bf16[2,32,256]{2,1,0:T(8,128)(2,1)S(1)} %bitcast.30), channel_id=1, source_target_pairs={{0,8},{4,12},{8,0},{12,4},{16,24},{20,28},{24,16},{28,20},{1,9},{5... | collective-permute-start | bytes 98312 | tf_op jit(solution)/shard_map/ppermute | solution.py:384
  11.8 6.1 %collective-permute-start.11 = (bf16[2,32,256]{2,1,0:T(8,128)(2,1)S(1)}, bf16[2,32,256]{2,1,0:T(8,128)(2,1)S(1)}, u32[]{:S(2)}, u32[]{:S(2)}) collective-permute-start(bf16[2,32,256]{2,1,0:T(8,128)(2,1)S(1)} %bitcast.31), channel_id=1, source_target_pairs={{0,16},{4,20},{8,24},{12,28},{16,0},{20,4},{24,8},{28,12},{1,17},{... | collective-permute-start | bytes 98312 | tf_op jit(solution)/shard_map/ppermute | solution.py:384
  14.5 5.7 %collective-permute-start.12 = (bf16[2,32,256]{2,1,0:T(8,128)(2,1)S(1)}, bf16[2,32,256]{2,1,0:T(8,128)(2,1)S(1)}, u32[]{:S(2)}, u32[]{:S(2)}) collective-permute-start(bf16[2,32,256]{2,1,0:T(8,128)(2,1)S(1)} %bitcast.32), channel_id=1, source_target_pairs={{0,24},{4,28},{8,16},{12,20},{16,8},{20,12},{24,0},{28,4},{1,25},{... | collective-permute-start | bytes 98312 | tf_op jit(solution)/shard_map/ppermute | solution.py:384
  20.2 12.1 %collective-permute-start.13 = (bf16[4,2,32,256]{3,2,1,0:T(8,128)(2,1)S(1)}, bf16[4,2,32,256]{3,2,1,0:T(8,128)(2,1)S(1)}, u32[]{:S(2)}, u32[]{:S(2)}) collective-permute-start(bf16[4,2,32,256]{3,2,1,0:T(8,128)(2,1)S(1)} %get-tuple-element.40), channel_id=1, source_target_pairs={{0,1},{1,0},{2,3},{3,2},{4,5},{5,4},{6,7},{7,6},{8,9},{9,8},{10,11... | collective-permute-start | bytes 393224 | tf_op jit(solution)/shard_map/ppermute | solution.py:384
  21.7 13.5 %collective-permute-start.14 = (bf16[4,2,32,256]{3,2,1,0:T(8,128)(2,1)S(1)}, bf16[4,2,32,256]{3,2,1,0:T(8,128)(2,1)S(1)}, u32[]{:S(2)}, u32[]{:S(2)}) collective-permute-start(bf16[4,2,32,256]{3,2,1,0:T(8,128)(2,1)S(1)} %get-tuple-element.40), channel_id=1, source_target_pairs={{0,2},{1,3},{2,0},{3,1},{4,6},{5,7},{6,4},{7,5},{8,10},{9,11},{10,... | collective-permute-start | bytes 393224 | tf_op jit(solution)/shard_map/ppermute | solution.py:384
  23.2 4.4 %collective-permute-start.3 = (f32[32,128]{1,0:T(8,128)S(1)}, f32[32,128]{1,0:T(8,128)S(1)}, u32[]{:S(2)}, u32[]{:S(2)}) collective-permute-start(f32[32,128]{1,0:T(8,128)S(1)} %sketch.1), channel_id=1, source_target_pairs={{0,8},{4,12},{8,0},{12,4},{16,24},{20,28},{24,16},{28,20},{1,9},{5... | collective-permute-start | bytes 49160 | tf_op jit(solution)/shard_map/ppermute | solution.py:384
  23.2 4.9 %collective-permute-start.4 = (f32[32,128]{1,0:T(8,128)S(1)}, f32[32,128]{1,0:T(8,128)S(1)}, u32[]{:S(2)}, u32[]{:S(2)}) collective-permute-start(f32[32,128]{1,0:T(8,128)S(1)} %sketch.1), channel_id=1, source_target_pairs={{0,16},{4,20},{8,24},{12,28},{16,0},{20,4},{24,8},{28,12},{1,17},{... | collective-permute-start | bytes 49160 | tf_op jit(solution)/shard_map/ppermute | solution.py:384
  26.1 5.5 %collective-permute-start.5 = (f32[32,128]{1,0:T(8,128)S(1)}, f32[32,128]{1,0:T(8,128)S(1)}, u32[]{:S(2)}, u32[]{:S(2)}) collective-permute-start(f32[32,128]{1,0:T(8,128)S(1)} %sketch.1), channel_id=1, source_target_pairs={{0,24},{4,28},{8,16},{12,20},{16,8},{20,12},{24,0},{28,4},{1,25},{... | collective-permute-start | bytes 49160 | tf_op jit(solution)/shard_map/ppermute | solution.py:384
  27.6 7.6 %collective-permute-start.15 = (bf16[4,2,32,256]{3,2,1,0:T(8,128)(2,1)S(1)}, bf16[4,2,32,256]{3,2,1,0:T(8,128)(2,1)S(1)}, u32[]{:S(2)}, u32[]{:S(2)}) collective-permute-start(bf16[4,2,32,256]{3,2,1,0:T(8,128)(2,1)S(1)} %get-tuple-element.40), channel_id=1, source_target_pairs={{0,3},{1,2},{2,1},{3,0},{4,7},{5,6},{6,5},{7,4},{8,11},{9,10},{10,... | collective-permute-start | bytes 393224 | tf_op jit(solution)/shard_map/ppermute | solution.py:384
  31.6 4.3 %collective-permute-start.6 = (f32[128,128]{1,0:T(8,128)S(1)}, f32[128,128]{1,0:T(8,128)S(1)}, u32[]{:S(2)}, u32[]{:S(2)}) collective-permute-start(f32[128,128]{1,0:T(8,128)S(1)} %pad_maximum_fusion.2), channel_id=1, source_target_pairs={{0,1},{1,0},{2,3},{3,2},{4,5},{5,4},{6,7},{7,6},{8,9},{9,8},{10,11... | collective-permute-start | bytes 196616 | tf_op jit(solution)/shard_map/ppermute | solution.py:384
  31.7 4.3 %collective-permute-start.7 = (f32[128,128]{1,0:T(8,128)S(1)}, f32[128,128]{1,0:T(8,128)S(1)}, u32[]{:S(2)}, u32[]{:S(2)}) collective-permute-start(f32[128,128]{1,0:T(8,128)S(1)} %pad_maximum_fusion.2), channel_id=1, source_target_pairs={{0,2},{1,3},{2,0},{3,1},{4,6},{5,7},{6,4},{7,5},{8,10},{9,11},{10,... | collective-permute-start | bytes 196616 | tf_op jit(solution)/shard_map/ppermute | solution.py:384
  32.3 5.2 %collective-permute-start.8 = (f32[128,128]{1,0:T(8,128)S(1)}, f32[128,128]{1,0:T(8,128)S(1)}, u32[]{:S(2)}, u32[]{:S(2)}) collective-permute-start(f32[128,128]{1,0:T(8,128)S(1)} %pad_maximum_fusion.2), channel_id=1, source_target_pairs={{0,3},{1,2},{2,1},{3,0},{4,7},{5,6},{6,5},{7,4},{8,11},{9,10},{10,... | collective-permute-start | bytes 196616 | tf_op jit(solution)/shard_map/ppermute | solution.py:384
  35.3 2.2 %collective-permute-start.16 = (bf16[4,4,2,32,256]{4,3,2,1,0:T(8,128)(2,1)S(1)}, bf16[4,4,2,32,256]{4,3,2,1,0:T(8,128)(2,1)S(1)}, u32[]{:S(2)}, u32[]{:S(2)}) collective-permute-start(bf16[4,4,2,32,256]{4,3,2,1,0:T(8,128)(2,1)S(1)} %pad_maximum_fusion.qmine_ref), channel_id=1, source_target_pairs={{0,4},{4,0},{8,12},{12,8},{16,20},{20,16},{24,28},{28,24},{1,5},{5... | collective-permute-start | bytes 1572872 | tf_op jit(solution)/shard_map/ppermute | solution.py:389
  37.5 1.5 %collective-permute-start.9 = (f32[512,128]{1,0:T(8,128)S(1)}, f32[512,128]{1,0:T(8,128)S(1)}, u32[]{:S(2)}, u32[]{:S(2)}) collective-permute-start(f32[512,128]{1,0:T(8,128)S(1)} %constant_dynamic-update-slice_fusion.mine_ref), channel_id=1, source_target_pairs={{0,4},{4,0},{8,12},{12,8},{16,20},{20,16},{24,28},{28,24},{1,5},{5... | collective-permute-start | bytes 786440 | tf_op jit(solution)/shard_map/ppermute | solution.py:389

commit v5 on v4

--- a/solution.py
+++ b/solution.py
@@ -115,8 +115,8 @@
     *refs,
 ):
     out_refs = refs[:-11]
-    table_ref, own_ref, weight_ref, place_ref, share_ref, own_ids_ref = refs[-11:-5]
-    ids_ref, len_ref, wide_ref, scalar_ref, sems = refs[-5:]
+    table_ref, own_ref, weight_ref, scalar_ref, share_ref, own_ids_ref = refs[-11:-5]
+    ids_ref, len_ref, wide_ref, place_ref, sems = refs[-5:]
     small_sem, wide_sem = sems.at[pl.ds(0, 6)], sems.at[pl.ds(6, 3 * (len(out_refs) + 1))]
     members = len(out_refs) + 1
     me = lax.axis_index("mp").astype(jnp.int32)
@@ -237,18 +237,13 @@
     table_ref,
     wide_ref,
     weight_ref,
-    place_ref,
+    scalar_ref,
     share_ref,
     local_ref,
     out_ref,
-    scalar_ref,
-    copied,
 ):
     me = lax.axis_index("mp").astype(jnp.int32)
-    copy = pltpu.make_async_copy(place_ref, scalar_ref, copied)
-    copy.start()
     total = products([wide_ref[k] for k in range(3)], weight_ref)
-    copy.wait()
     for s in range(per_member):
         seq = me * per_member + s
         rows = slice(s * slot_len, (s + 1) * slot_len)
@@ -421,17 +416,17 @@
             pltpu.VMEM((rank, vocab_rows), jnp.bfloat16),
             pltpu.VMEM((3, block, features), jnp.bfloat16),
             pltpu.VMEM((3, LANES, features), jnp.bfloat16),
-            pltpu.VMEM((seq_count, slot_len), jnp.int32),
+            pltpu.SMEM((seq_count, slot_len), jnp.int32),
             pltpu.VMEM((block, LANES), jnp.float32),
             pltpu.VMEM((seq_count, slot_len), jnp.int32),
         ],
         in_specs=[pl.BlockSpec(memory_space=pl.ANY)] * 9,
-        out_specs=whole(mp + 5),
+        out_specs=whole(mp + 2) + [pl.BlockSpec(memory_space=pltpu.SMEM)] + whole(2),
         scratch_shapes=[
             pltpu.VMEM((seq_count, slot_len), jnp.int32),
             pltpu.SMEM((seq_count,), jnp.int32),
             pltpu.VMEM((3, token_count, features), jnp.bfloat16),
-            pltpu.SMEM((seq_count, slot_len), jnp.int32),
+            pltpu.VMEM((seq_count, slot_len), jnp.int32),
             pltpu.SemaphoreType.DMA((6 + 3 * mp,)),
         ],
         compiler_params=limit,
@@ -453,12 +448,15 @@
     mine = pl.pallas_call(
         functools.partial(own_block_kernel, vocab_rows, slot_len, per_member),
         out_shape=pltpu.VMEM((block, LANES), jnp.float32),
-        in_specs=whole(6),
+        in_specs=whole(3) + [pl.BlockSpec(memory_space=pltpu.SMEM)] + whole(2),
         out_specs=whole(1)[0],
-        scratch_shapes=[pltpu.SMEM((seq_count, slot_len), jnp.int32), pltpu.SemaphoreType.DMA],
         compiler_params=limit,
         name="own_block",
-    )(*placed(pltpu.VMEM, *sent[mp - 1 :]))
+    )(
+        *placed(pltpu.VMEM, *sent[mp - 1 : mp + 2]),
+        *placed(pltpu.SMEM, sent[mp + 2]),
+        *placed(pltpu.VMEM, *sent[mp + 3 :]),
+    )
     parts = [mine]
     for k in range(1, mp):
         parts.append(lax.ppermute(sent[k - 1], "mp", [(i, i ^ k) for i in range(mp)]))

time: 40.9 us -> 41.1 us (level)
  waiting for transfers between devices: 8.63 us -> 9.27 us
  Pallas kernels: 9.49 us -> 9.06 us
    ppermute x12, waiting for transfers between devices: 7.82 us -> 8.46 us  [exchange(): lax.ppermute(value, axis, [(i, i ^ k * unit) for i in range(size)])]
    pallas_call x1, Pallas kernels: 1.48 us -> 0.93 us  [fast_device(): pl.pallas_call(functools.partial(own_block_kernel, vocab_rows, slot_len,...]
  transfers between devices with their start and end apart: 17 -> 17, of which waited for: 6 -> 6; matrix products, arithmetic and copies ran while one was open for 0% -> 0% of each run, Pallas kernels for 6% -> 5%
where the time goes in v5:
time: 41.1 us; the launch traced here: 40.9 us
  starting transfers between devices  22.4 us (55%)
  waiting for transfers between devices  9.27 us (23%)
  Pallas kernels  9.06 us (22%)
    ppermute x12, starting transfers between devices, exchange(): lax.ppermute(value, axis, [(i, i ^ k * unit) for i in range(size)])  17.7 us
    ppermute x12, waiting for transfers between devices, exchange(): lax.ppermute(value, axis, [(i, i ^ k * unit) for i in range(size)])  8.46 us
    pallas_call x1, Pallas kernels, fast_device(): pl.pallas_call(functools.partial(project_kernel, vocab_rows, rank, slot_l...  5.34 us
    ppermute x3, starting transfers between devices, fast_device(): lax.ppermute(sent[k - 1], 'mp', [(i, i ^ k) for i in range(mp)])  4.62 us
    pallas_call x1, Pallas kernels, fast_device(): pl.pallas_call(functools.partial(solve_kernel, mp, zs, per_member, exampl...  1.7 us
    pallas_call x1, Pallas kernels, fast_device(): pl.pallas_call(functools.partial(own_block_kernel, vocab_rows, slot_len,...  0.93 us
  transfers between devices with their start and end apart: 17, of which 6 were waited for; matrix products, arithmetic and copies ran while one was open for 0% of the time, Pallas kernels for 5%

profile of v5, /device:TPU:0, one launch (start us, length us, event | category | flops | bytes accessed | tf_op | source)
XLA Modules:
  0.0 40.9 jit_solution(2535019252871253920)
XLA Ops:
  0.0 0.0 copy-start
  0.0 5.3 %project.1 = (f32[256,128]{1,0:T(8,128)S(1)}, f32[256,128]{1,0:T(8,128)S(1)}, f32[256,128]{1,0:T(8,128)S(1)}, bf16[32,32064]{1,0:T(8,128)(2,1)S(1)}, bf16[3,256,...) custom-call(s32[8,128]{1,0:T(8,128)} %bitcast.37, ...), custom_call_target="tpu_custom_call" | custom-call | tf_op jit(solution)/shard_map/project/pallas_call | solution.py:412
  5.4 3.1 %collective-permute-start = (f32[256,128]{1,0:T(8,128)S(1)}, f32[256,128]{1,0:T(8,128)S(1)}, u32[]{:S(2)}, u32[]{:S(2)}) collective-permute-start(f32[256,128]{1,0:T(8,128)S(1)} %get-tuple-element.28), channel_id=1, source_target_pairs={{0,1},{1,0},{2,3},{3,2},{4,5},{5,4},{6,7},{7,6},{8,9},{9,8},{10,11... | collective-permute-start | bytes 393224 | tf_op jit(solution)/shard_map/ppermute | solution.py:462
  8.4 1.5 %collective-permute-start.1 = (f32[256,128]{1,0:T(8,128)S(1)}, f32[256,128]{1,0:T(8,128)S(1)}, u32[]{:S(2)}, u32[]{:S(2)}) collective-permute-start(f32[256,128]{1,0:T(8,128)S(1)} %get-tuple-element.29), channel_id=1, source_target_pairs={{0,2},{1,3},{2,0},{3,1},{4,6},{5,7},{6,4},{7,5},{8,10},{9,11},{10,... | collective-permute-start | bytes 393224 | tf_op jit(solution)/shard_map/ppermute | solution.py:462
  9.9 0.0 collective-permute-start.2
  10.0 0.0 copy-done
  10.0 2.0 %collective-permute-start.10 = (bf16[2,32,256]{2,1,0:T(8,128)(2,1)S(1)}, bf16[2,32,256]{2,1,0:T(8,128)(2,1)S(1)}, u32[]{:S(2)}, u32[]{:S(2)}) collective-permute-start(bf16[2,32,256]{2,1,0:T(8,128)(2,1)S(1)} %bitcast.30), channel_id=1, source_target_pairs={{0,8},{4,12},{8,0},{12,4},{16,24},{20,28},{24,16},{28,20},{1,9},{5... | collective-permute-start | bytes 98312 | tf_op jit(solution)/shard_map/ppermute | solution.py:379
  12.0 2.6 %collective-permute-start.11 = (bf16[2,32,256]{2,1,0:T(8,128)(2,1)S(1)}, bf16[2,32,256]{2,1,0:T(8,128)(2,1)S(1)}, u32[]{:S(2)}, u32[]{:S(2)}) collective-permute-start(bf16[2,32,256]{2,1,0:T(8,128)(2,1)S(1)} %bitcast.31), channel_id=1, source_target_pairs={{0,16},{4,20},{8,24},{12,28},{16,0},{20,4},{24,8},{28,12},{1,17},{... | collective-permute-start | bytes 98312 | tf_op jit(solution)/shard_map/ppermute | solution.py:379
  14.5 0.0 collective-permute-done.refs_1_
  14.5 1.6 %collective-permute-start.12 = (bf16[2,32,256]{2,1,0:T(8,128)(2,1)S(1)}, bf16[2,32,256]{2,1,0:T(8,128)(2,1)S(1)}, u32[]{:S(2)}, u32[]{:S(2)}) collective-permute-start(bf16[2,32,256]{2,1,0:T(8,128)(2,1)S(1)} %bitcast.32), channel_id=1, source_target_pairs={{0,24},{4,28},{8,16},{12,20},{16,8},{20,12},{24,0},{28,4},{1,25},{... | collective-permute-start | bytes 98312 | tf_op jit(solution)/shard_map/ppermute | solution.py:379
  16.1 0.9 %own_block.1.refs_0_ = f32[256,128]{1,0:T(8,128)S(1)} custom-call(bf16[32,32064]{1,0:T(8,128)(2,1)S(1)} %get-tuple-element.22.table_ref, bf16[3,256,1024]{2,1,0:T(8,128)(2,1)S(1)} %get-tuple-element.23.wide_ref, bf16[3,128,1024]{2,1,0:T(8,128)(2,1)S(1)} %get-tuple-element.24.weight_ref, s32[8,128]{1,0:T(8,128)S(4)} %get-tuple-element.25.scalar_ref, ...), custom_call_target="tpu_custom_call" | custom-call | tf_op jit(solution)/shard_map/own_block/pallas_call | solution.py:448
  17.1 0.0 collective-permute-done.1.refs_2_
  17.1 0.0 collective-permute-done.2.refs_3_
  17.1 0.4 sketch.1
  17.5 0.0 collective-permute-done.10
  17.5 0.0 collective-permute-done.11
  17.5 2.7 %collective-permute-done.12 = bf16[2,32,256]{2,1,0:T(8,128)(2,1)S(1)} collective-permute-done((bf16[2,32,256]{2,1,0:T(8,128)(2,1)S(1)}, bf16[2,32,256]{2,1,0:T(8,128)(2,1)S(1)}, u32[]{:S(2)}, u32[]{:S(2)}) %collective-permute-start.12) | collective-permute-done | bytes 32800 | tf_op jit(solution)/shard_map/ppermute | solution.py:379
  20.3 1.6 %collective-permute-start.13 = (bf16[4,2,32,256]{3,2,1,0:T(8,128)(2,1)S(1)}, bf16[4,2,32,256]{3,2,1,0:T(8,128)(2,1)S(1)}, u32[]{:S(2)}, u32[]{:S(2)}) collective-permute-start(bf16[4,2,32,256]{3,2,1,0:T(8,128)(2,1)S(1)} %get-tuple-element.40), channel_id=1, source_target_pairs={{0,1},{1,0},{2,3},{3,2},{4,5},{5,4},{6,7},{7,6},{8,9},{9,8},{10,11... | collective-permute-start | bytes 393224 | tf_op jit(solution)/shard_map/ppermute | solution.py:379
  21.9 1.5 %collective-permute-start.14 = (bf16[4,2,32,256]{3,2,1,0:T(8,128)(2,1)S(1)}, bf16[4,2,32,256]{3,2,1,0:T(8,128)(2,1)S(1)}, u32[]{:S(2)}, u32[]{:S(2)}) collective-permute-start(bf16[4,2,32,256]{3,2,1,0:T(8,128)(2,1)S(1)} %get-tuple-element.40), channel_id=1, source_target_pairs={{0,2},{1,3},{2,0},{3,1},{4,6},{5,7},{6,4},{7,5},{8,10},{9,11},{10,... | collective-permute-start | bytes 393224 | tf_op jit(solution)/shard_map/ppermute | solution.py:379
  23.4 0.0 collective-permute-start.3
  23.5 2.9 %collective-permute-start.4 = (f32[32,128]{1,0:T(8,128)S(1)}, f32[32,128]{1,0:T(8,128)S(1)}, u32[]{:S(2)}, u32[]{:S(2)}) collective-permute-start(f32[32,128]{1,0:T(8,128)S(1)} %sketch.1), channel_id=1, source_target_pairs={{0,16},{4,20},{8,24},{12,28},{16,0},{20,4},{24,8},{28,12},{1,17},{... | collective-permute-start | bytes 49160 | tf_op jit(solution)/shard_map/ppermute | solution.py:379
  26.3 1.5 %collective-permute-start.5 = (f32[32,128]{1,0:T(8,128)S(1)}, f32[32,128]{1,0:T(8,128)S(1)}, u32[]{:S(2)}, u32[]{:S(2)}) collective-permute-start(f32[32,128]{1,0:T(8,128)S(1)} %sketch.1), channel_id=1, source_target_pairs={{0,24},{4,28},{8,16},{12,20},{16,8},{20,12},{24,0},{28,4},{1,25},{... | collective-permute-start | bytes 49160 | tf_op jit(solution)/shard_map/ppermute | solution.py:379
  27.8 0.0 collective-permute-done.3
  27.8 0.4 collective-permute-start.15
  28.2 0.0 collective-permute-done.4
  28.2 3.6 %collective-permute-done.5 = f32[32,128]{1,0:T(8,128)S(1)} collective-permute-done((f32[32,128]{1,0:T(8,128)S(1)}, f32[32,128]{1,0:T(8,128)S(1)}, u32[]{:S(2)}, u32[]{:S(2)}) %collective-permute-start.5) | collective-permute-done | bytes 16416 | tf_op jit(solution)/shard_map/ppermute | solution.py:379
  31.9 0.1 collective-permute-start.6
  31.9 0.5 %collective-permute-start.7 = (f32[128,128]{1,0:T(8,128)S(1)}, f32[128,128]{1,0:T(8,128)S(1)}, u32[]{:S(2)}, u32[]{:S(2)}) collective-permute-start(f32[128,128]{1,0:T(8,128)S(1)} %pad_maximum_fusion.2), channel_id=1, source_target_pairs={{0,2},{1,3},{2,0},{3,1},{4,6},{5,7},{6,4},{7,5},{8,10},{9,11},{10,... | collective-permute-start | bytes 196616 | tf_op jit(solution)/shard_map/ppermute | solution.py:379
  32.4 0.0 collective-permute-done.13
  32.4 3.0 %collective-permute-start.8 = (f32[128,128]{1,0:T(8,128)S(1)}, f32[128,128]{1,0:T(8,128)S(1)}, u32[]{:S(2)}, u32[]{:S(2)}) collective-permute-start(f32[128,128]{1,0:T(8,128)S(1)} %pad_maximum_fusion.2), channel_id=1, source_target_pairs={{0,3},{1,2},{2,1},{3,0},{4,7},{5,6},{6,5},{7,4},{8,11},{9,10},{10,... | collective-permute-start | bytes 196616 | tf_op jit(solution)/shard_map/ppermute | solution.py:379
  35.4 0.0 collective-permute-done.14
  35.4 0.0 collective-permute-done.15
  35.4 0.1 pad_maximum_fusion.qmine_ref
  35.5 0.1 collective-permute-start.16
  35.6 0.5 %collective-permute-done.6 = f32[128,128]{1,0:T(8,128)S(1)} collective-permute-done((f32[128,128]{1,0:T(8,128)S(1)}, f32[128,128]{1,0:T(8,128)S(1)}, u32[]{:S(2)}, u32[]{:S(2)}) %collective-permute-start.6) | collective-permute-done | bytes 65568 | tf_op jit(solution)/shard_map/ppermute | solution.py:379
  36.1 0.1 collective-permute-done.7
  36.2 1.5 %collective-permute-done.8 = f32[128,128]{1,0:T(8,128)S(1)} collective-permute-done((f32[128,128]{1,0:T(8,128)S(1)}, f32[128,128]{1,0:T(8,128)S(1)}, u32[]{:S(2)}, u32[]{:S(2)}) %collective-permute-start.8) | collective-permute-done | bytes 65568 | tf_op jit(solution)/shard_map/ppermute | solution.py:379
  37.7 0.0 collective-permute-start.9
  37.7 0.0 collective-permute-done.16.qother_ref
  37.7 0.7 %own.1 = (bf16[2,64,1024]{2,1,0:T(8,128)(2,1)S(1)}, f32[2,32,256]{2,1,0:T(8,128)S(1)}, f32[2,8,256]{2,1,0:T(8,128)S(1)}, bf16[2,4,256,256]{3,2,1,0:T(8,128)(2,1)S(1)}) custom-call(f32[512,128]{1,0:T(8,128)S(1)} %constant_dynamic-update-slice_fusion.mine_ref, bf16[4,4,2,32,256]{4,3,2,1,0:T(8,128)(2,1)S(1)} %pad_maximum_fusion.qmine_ref, ...), custom_call_target="tpu_custom_call" | custom-call | tf_op jit(solution)/shard_map/own/pallas_call | solution.py:484
  38.4 0.8 %collective-permute-done.9.other_ref = f32[512,128]{1,0:T(8,128)S(1)} collective-permute-done((f32[512,128]{1,0:T(8,128)S(1)}, f32[512,128]{1,0:T(8,128)S(1)}, u32[]{:S(2)}, u32[]{:S(2)}) %collective-permute-start.9) | collective-permute-done | bytes 262176 | tf_op jit(solution)/shard_map/ppermute | solution.py:384
  39.2 1.7 %solve.1 = f32[8,256]{1,0:T(8,128)} custom-call(f32[512,128]{1,0:T(8,128)S(1)} %collective-permute-done.9.other_ref, bf16[2,64,1024]{2,1,0:T(8,128)(2,1)S(1)} %get-tuple-element.35.both_ref, f32[2,32,256]{2,1,0:T(8,128)S(1)} %get-tuple-element.36.u_ref, f32[2,8,256]{2,1,0:T(8,128)S(1)} %get-tuple-element.37.norm_ref, ...), custom_call_target="tpu_custom_call" | custom-call | tf_op jit(solution)/shard_map/solve/pallas_call | solution.py:497
  (9 shorter events, 0.1 us)
Async XLA Ops:
  0.0 10.0 %copy-start = (bf16[2,256,32]{1,2,0:T(8,128)(2,1)S(1)}, bf16[2,256,32]{1,2,0:T(8,128)(2,1)}, u32[]{:S(2)}) copy-start(bf16[2,256,32]{1,2,0:T(8,128)(2,1)} %param.19) | copy-start | bytes 98308
  5.4 9.2 %collective-permute-start = (f32[256,128]{1,0:T(8,128)S(1)}, f32[256,128]{1,0:T(8,128)S(1)}, u32[]{:S(2)}, u32[]{:S(2)}) collective-permute-start(f32[256,128]{1,0:T(8,128)S(1)} %get-tuple-element.28), channel_id=1, source_target_pairs={{0,1},{1,0},{2,3},{3,2},{4,5},{5,4},{6,7},{7,6},{8,9},{9,8},{10,11... | collective-permute-start | bytes 393224 | tf_op jit(solution)/shard_map/ppermute | solution.py:462
  8.4 8.7 %collective-permute-start.1 = (f32[256,128]{1,0:T(8,128)S(1)}, f32[256,128]{1,0:T(8,128)S(1)}, u32[]{:S(2)}, u32[]{:S(2)}) collective-permute-start(f32[256,128]{1,0:T(8,128)S(1)} %get-tuple-element.29), channel_id=1, source_target_pairs={{0,2},{1,3},{2,0},{3,1},{4,6},{5,7},{6,4},{7,5},{8,10},{9,11},{10,... | collective-permute-start | bytes 393224 | tf_op jit(solution)/shard_map/ppermute | solution.py:462
  9.9 7.1 %collective-permute-start.2 = (f32[256,128]{1,0:T(8,128)S(1)}, f32[256,128]{1,0:T(8,128)S(1)}, u32[]{:S(2)}, u32[]{:S(2)}) collective-permute-start(f32[256,128]{1,0:T(8,128)S(1)} %get-tuple-element.30), channel_id=1, source_target_pairs={{0,3},{1,2},{2,1},{3,0},{4,7},{5,6},{6,5},{7,4},{8,11},{9,10},{10,... | collective-permute-start | bytes 393224 | tf_op jit(solution)/shard_map/ppermute | solution.py:462
  10.0 7.5 %collective-permute-start.10 = (bf16[2,32,256]{2,1,0:T(8,128)(2,1)S(1)}, bf16[2,32,256]{2,1,0:T(8,128)(2,1)S(1)}, u32[]{:S(2)}, u32[]{:S(2)}) collective-permute-start(bf16[2,32,256]{2,1,0:T(8,128)(2,1)S(1)} %bitcast.30), channel_id=1, source_target_pairs={{0,8},{4,12},{8,0},{12,4},{16,24},{20,28},{24,16},{28,20},{1,9},{5... | collective-permute-start | bytes 98312 | tf_op jit(solution)/shard_map/ppermute | solution.py:379
  12.0 5.5 %collective-permute-start.11 = (bf16[2,32,256]{2,1,0:T(8,128)(2,1)S(1)}, bf16[2,32,256]{2,1,0:T(8,128)(2,1)S(1)}, u32[]{:S(2)}, u32[]{:S(2)}) collective-permute-start(bf16[2,32,256]{2,1,0:T(8,128)(2,1)S(1)} %bitcast.31), channel_id=1, source_target_pairs={{0,16},{4,20},{8,24},{12,28},{16,0},{20,4},{24,8},{28,12},{1,17},{... | collective-permute-start | bytes 98312 | tf_op jit(solution)/shard_map/ppermute | solution.py:379
  14.5 5.7 %collective-permute-start.12 = (bf16[2,32,256]{2,1,0:T(8,128)(2,1)S(1)}, bf16[2,32,256]{2,1,0:T(8,128)(2,1)S(1)}, u32[]{:S(2)}, u32[]{:S(2)}) collective-permute-start(bf16[2,32,256]{2,1,0:T(8,128)(2,1)S(1)} %bitcast.32), channel_id=1, source_target_pairs={{0,24},{4,28},{8,16},{12,20},{16,8},{20,12},{24,0},{28,4},{1,25},{... | collective-permute-start | bytes 98312 | tf_op jit(solution)/shard_map/ppermute | solution.py:379
  20.3 12.1 %collective-permute-start.13 = (bf16[4,2,32,256]{3,2,1,0:T(8,128)(2,1)S(1)}, bf16[4,2,32,256]{3,2,1,0:T(8,128)(2,1)S(1)}, u32[]{:S(2)}, u32[]{:S(2)}) collective-permute-start(bf16[4,2,32,256]{3,2,1,0:T(8,128)(2,1)S(1)} %get-tuple-element.40), channel_id=1, source_target_pairs={{0,1},{1,0},{2,3},{3,2},{4,5},{5,4},{6,7},{7,6},{8,9},{9,8},{10,11... | collective-permute-start | bytes 393224 | tf_op jit(solution)/shard_map/ppermute | solution.py:379
  21.9 13.5 %collective-permute-start.14 = (bf16[4,2,32,256]{3,2,1,0:T(8,128)(2,1)S(1)}, bf16[4,2,32,256]{3,2,1,0:T(8,128)(2,1)S(1)}, u32[]{:S(2)}, u32[]{:S(2)}) collective-permute-start(bf16[4,2,32,256]{3,2,1,0:T(8,128)(2,1)S(1)} %get-tuple-element.40), channel_id=1, source_target_pairs={{0,2},{1,3},{2,0},{3,1},{4,6},{5,7},{6,4},{7,5},{8,10},{9,11},{10,... | collective-permute-start | bytes 393224 | tf_op jit(solution)/shard_map/ppermute | solution.py:379
  23.4 4.4 %collective-permute-start.3 = (f32[32,128]{1,0:T(8,128)S(1)}, f32[32,128]{1,0:T(8,128)S(1)}, u32[]{:S(2)}, u32[]{:S(2)}) collective-permute-start(f32[32,128]{1,0:T(8,128)S(1)} %sketch.1), channel_id=1, source_target_pairs={{0,8},{4,12},{8,0},{12,4},{16,24},{20,28},{24,16},{28,20},{1,9},{5... | collective-permute-start | bytes 49160 | tf_op jit(solution)/shard_map/ppermute | solution.py:379
  23.5 4.8 %collective-permute-start.4 = (f32[32,128]{1,0:T(8,128)S(1)}, f32[32,128]{1,0:T(8,128)S(1)}, u32[]{:S(2)}, u32[]{:S(2)}) collective-permute-start(f32[32,128]{1,0:T(8,128)S(1)} %sketch.1), channel_id=1, source_target_pairs={{0,16},{4,20},{8,24},{12,28},{16,0},{20,4},{24,8},{28,12},{1,17},{... | collective-permute-start | bytes 49160 | tf_op jit(solution)/shard_map/ppermute | solution.py:379
  26.3 5.5 %collective-permute-start.5 = (f32[32,128]{1,0:T(8,128)S(1)}, f32[32,128]{1,0:T(8,128)S(1)}, u32[]{:S(2)}, u32[]{:S(2)}) collective-permute-start(f32[32,128]{1,0:T(8,128)S(1)} %sketch.1), channel_id=1, source_target_pairs={{0,24},{4,28},{8,16},{12,20},{16,8},{20,12},{24,0},{28,4},{1,25},{... | collective-permute-start | bytes 49160 | tf_op jit(solution)/shard_map/ppermute | solution.py:379
  27.8 7.6 %collective-permute-start.15 = (bf16[4,2,32,256]{3,2,1,0:T(8,128)(2,1)S(1)}, bf16[4,2,32,256]{3,2,1,0:T(8,128)(2,1)S(1)}, u32[]{:S(2)}, u32[]{:S(2)}) collective-permute-start(bf16[4,2,32,256]{3,2,1,0:T(8,128)(2,1)S(1)} %get-tuple-element.40), channel_id=1, source_target_pairs={{0,3},{1,2},{2,1},{3,0},{4,7},{5,6},{6,5},{7,4},{8,11},{9,10},{10,... | collective-permute-start | bytes 393224 | tf_op jit(solution)/shard_map/ppermute | solution.py:379
  31.9 4.3 %collective-permute-start.6 = (f32[128,128]{1,0:T(8,128)S(1)}, f32[128,128]{1,0:T(8,128)S(1)}, u32[]{:S(2)}, u32[]{:S(2)}) collective-permute-start(f32[128,128]{1,0:T(8,128)S(1)} %pad_maximum_fusion.2), channel_id=1, source_target_pairs={{0,1},{1,0},{2,3},{3,2},{4,5},{5,4},{6,7},{7,6},{8,9},{9,8},{10,11... | collective-permute-start | bytes 196616 | tf_op jit(solution)/shard_map/ppermute | solution.py:379
  31.9 4.3 %collective-permute-start.7 = (f32[128,128]{1,0:T(8,128)S(1)}, f32[128,128]{1,0:T(8,128)S(1)}, u32[]{:S(2)}, u32[]{:S(2)}) collective-permute-start(f32[128,128]{1,0:T(8,128)S(1)} %pad_maximum_fusion.2), channel_id=1, source_target_pairs={{0,2},{1,3},{2,0},{3,1},{4,6},{5,7},{6,4},{7,5},{8,10},{9,11},{10,... | collective-permute-start | bytes 196616 | tf_op jit(solution)/shard_map/ppermute | solution.py:379
  32.4 5.2 %collective-permute-start.8 = (f32[128,128]{1,0:T(8,128)S(1)}, f32[128,128]{1,0:T(8,128)S(1)}, u32[]{:S(2)}, u32[]{:S(2)}) collective-permute-start(f32[128,128]{1,0:T(8,128)S(1)} %pad_maximum_fusion.2), channel_id=1, source_target_pairs={{0,3},{1,2},{2,1},{3,0},{4,7},{5,6},{6,5},{7,4},{8,11},{9,10},{10,... | collective-permute-start | bytes 196616 | tf_op jit(solution)/shard_map/ppermute | solution.py:379
  35.5 2.2 %collective-permute-start.16 = (bf16[4,4,2,32,256]{4,3,2,1,0:T(8,128)(2,1)S(1)}, bf16[4,4,2,32,256]{4,3,2,1,0:T(8,128)(2,1)S(1)}, u32[]{:S(2)}, u32[]{:S(2)}) collective-permute-start(bf16[4,4,2,32,256]{4,3,2,1,0:T(8,128)(2,1)S(1)} %pad_maximum_fusion.qmine_ref), channel_id=1, source_target_pairs={{0,4},{4,0},{8,12},{12,8},{16,20},{20,16},{24,28},{28,24},{1,5},{5... | collective-permute-start | bytes 1572872 | tf_op jit(solution)/shard_map/ppermute | solution.py:384
  37.7 1.5 %collective-permute-start.9 = (f32[512,128]{1,0:T(8,128)S(1)}, f32[512,128]{1,0:T(8,128)S(1)}, u32[]{:S(2)}, u32[]{:S(2)}) collective-permute-start(f32[512,128]{1,0:T(8,128)S(1)} %constant_dynamic-update-slice_fusion.mine_ref), channel_id=1, source_target_pairs={{0,4},{4,0},{8,12},{12,8},{16,20},{20,16},{24,28},{28,24},{1,5},{5... | collective-permute-start | bytes 786440 | tf_op jit(solution)/shard_map/ppermute | solution.py:384
